TPU v7x, 32 devices: a whole 2x2x4 slice. The times are simulated.
32 devices in a mesh: section: 2 (over core), dp: 4 (over z), tensor: 4 (over y, x).
Axes of the slice: x: 2, y: 2, z: 4, core: 2. Of those that a mesh axis runs over, the one named last changes fastest.
Arguments:
- block_input: bfloat16 [4, 512, 2048], P(None, 'dp'), may hold values from -6 to 6
- cotangent: bfloat16 [4, 512, 2048], P(None, 'dp'), may hold values from -6 to 6
- segments: int32 [4, 512], P(None, 'dp'), may hold values from -1 to 127, as said below
- ln_gain: float32 [2, 2048], P('section'), may hold values from 0.5 to 1.5
- ln_bias: float32 [2, 2048], P('section'), may hold values from -3 to 3
- qkv_weight: bfloat16 [2, 3, 2048, 2048], P('section', None, None, 'tensor')
- qv_bias: float32 [2, 2, 2048], P('section', None, 'tensor'), may hold values from -3 to 3
- dense_weight: bfloat16 [2, 2048, 2048], P('section', 'tensor'), may hold values from -0.75 to 0.75
- out_bias: float32 [2, 2048], P('section'), may hold values from -3 to 3
- fc1_weight: bfloat16 [2, 2048, 8192], P('section', None, 'tensor'), may hold values from -0.125 to 0.125
- fc1_bias: float32 [2, 8192], P('section', 'tensor'), may hold values from -3 to 3
- fc2_weight: bfloat16 [2, 8192, 2048], P('section', 'tensor'), may hold values from -0.0625 to 0.0625
Outputs:
- layer_out: bfloat16 [2, 4, 512, 2048], P('section', None, ('dp', 'tensor'))
- in_grad: bfloat16 [2, 4, 512, 2048], P('section', None, ('dp', 'tensor'))
- grad_ln_gain: float32 [2, 2048], P('section')
- grad_ln_bias: float32 [2, 2048], P('section')
- grad_qkv: float32 [2, 3, 2048, 2048], P('section', None, 'dp', 'tensor')
- grad_qv_bias: float32 [2, 2, 2048], P('section', None, 'tensor')
- grad_dense: float32 [2, 2048, 2048], P('section', 'tensor', 'dp')
- grad_out_bias: float32 [2, 2048], P('section')
- grad_fc1: float32 [2, 2048, 8192], P('section', 'dp', 'tensor')
- grad_fc1_bias: float32 [2, 8192], P('section', 'tensor')
- grad_fc2: float32 [2, 8192, 2048], P('section', 'tensor', 'dp')
Inputs may be any that keep to these rules, and one draw needn't show every extreme that they name: `segments`: within each data group's 128 positions of a micro-batch the ids start at 0 and never fall over a first stretch of 64 or more positions, after which the rest are -1 for padding. In every draw the first micro-batch of the first data group has no padding and gives each position a sequence of its own, and the last one of the last data group has exactly 64 live positions.
All inputs are finite; a program needn't handle non-finite values.
Results may differ from a plain program's by a relative error of at most 0.014.
Values may be sent and summed in bfloat16 or wider, within the bound.
A program may use at most 320 MiB of HBM per device.

v0:
```python
import jax
import jax.numpy as jnp
from jax import lax
from jax.sharding import PartitionSpec as P

HEAD_DIM = 64
ROT = 32


NORM_EPS = 1e-05
MASKED = -1e30


def from_behind(x, axis, by):
    count = lax.axis_size(axis)
    pairs = [(i, i + by) for i in range(count) if 0 <= i + by < count]
    return lax.ppermute(x, axis, pairs)


def positions_of(segment):
    length = segment.shape[0]
    row_index = jnp.arange(length, dtype=jnp.int32)
    previous = jnp.concatenate([segment[:1], segment[:-1]])
    starts = jnp.where((row_index == 0) | (segment != previous), row_index, 0)
    return (row_index - lax.cummax(starts, axis=0)).astype(jnp.float32)


def rotary_tables(segment):
    half_rot = ROT // 2
    frequency = 10000.0 ** (-2.0 * jnp.arange(half_rot, dtype=jnp.float32) / ROT)
    phase_angle = positions_of(segment)[:, None] * frequency[None, :]
    return (jnp.cos(phase_angle)[:, None, :], jnp.sin(phase_angle)[:, None, :])


def rotate_pairs(heads_in, cos_part, sin_part):
    half_rot = ROT // 2
    lower_half = heads_in[..., :half_rot]
    upper_half = heads_in[..., half_rot:ROT]
    return jnp.concatenate(
        [
            lower_half * cos_part - upper_half * sin_part,
            upper_half * cos_part + lower_half * sin_part,
            heads_in[..., ROT:],
        ],
        axis=-1,
    )


def inner_product(left, right):
    return lax.dot_general(
        left, right, (((0,), (0,)), ((), ())), preferred_element_type=jnp.float32
    )


def transposed_product(left, right):
    return lax.dot_general(
        left, right, (((1,), (1,)), ((), ())), preferred_element_type=jnp.float32
    )


def score_block(queries, key_rows, segment):
    length = segment.shape[0]
    row_index = jnp.arange(length, dtype=jnp.int32)
    allowed = (segment[:, None] == segment[None, :]) & (row_index[None, :] <= row_index[:, None])
    scores = jnp.einsum(
        "qhd,khd->hqk", queries, key_rows, preferred_element_type=jnp.float32
    ) * HEAD_DIM ** (-0.5)
    return jnp.where(allowed[None, :, :], scores, MASKED)


def gelu_grad(pre_act, grad_act):
    _, pull_back = jax.vjp(lambda value_in: jax.nn.gelu(value_in, approximate=True), pre_act)
    return pull_back(grad_act)[0]


def normalize(hidden, norm_gain, norm_shift):
    residual = hidden.astype(jnp.float32)
    centred = residual - jnp.mean(residual, axis=-1, keepdims=True)
    inv_std = lax.rsqrt(jnp.mean(centred * centred, axis=-1, keepdims=True) + NORM_EPS)
    standard = centred * inv_std
    normed = (standard * norm_gain + norm_shift).astype(jnp.bfloat16)
    return (residual, standard, inv_std, normed)


def branch_forward(normed, segment, matrices, biases):
    proj_qkv, proj_dense, fc_one, fc_two = matrices
    bias_qv, bias_fc = biases
    row_count = normed.shape[0]
    feature_width = proj_qkv.shape[-1]
    head_count = feature_width // HEAD_DIM
    cos_part, sin_part = rotary_tables(segment)
    query_f = jnp.dot(normed, proj_qkv[0], preferred_element_type=jnp.float32) + bias_qv[0]
    key_f = jnp.dot(normed, proj_qkv[1], preferred_element_type=jnp.float32)
    values = (
        (jnp.dot(normed, proj_qkv[2], preferred_element_type=jnp.float32) + bias_qv[1])
        .astype(jnp.bfloat16)
        .reshape(row_count, head_count, HEAD_DIM)
    )
    queries = rotate_pairs(
        query_f.reshape(row_count, head_count, HEAD_DIM), cos_part, sin_part
    ).astype(jnp.bfloat16)
    key_rows = rotate_pairs(
        key_f.reshape(row_count, head_count, HEAD_DIM), cos_part, sin_part
    ).astype(jnp.bfloat16)
    scores = score_block(queries, key_rows, segment)
    row_max = jnp.max(scores, axis=-1, keepdims=True)
    log_total = row_max + jnp.log(jnp.sum(jnp.exp(scores - row_max), axis=-1, keepdims=True))
    attn_prob = jnp.exp(scores - log_total).astype(jnp.bfloat16)
    attended = (
        jnp.einsum("hqk,khd->qhd", attn_prob, values, preferred_element_type=jnp.float32)
        .astype(jnp.bfloat16)
        .reshape(row_count, feature_width)
    )
    pre_act = jnp.dot(normed, fc_one, preferred_element_type=jnp.float32) + bias_fc
    activation = jax.nn.gelu(pre_act, approximate=True).astype(jnp.bfloat16)
    partial_sum = jnp.dot(attended, proj_dense, preferred_element_type=jnp.float32) + jnp.dot(
        activation, fc_two, preferred_element_type=jnp.float32
    )
    return (partial_sum, (queries, key_rows, values, log_total, attended, pre_act, activation))


def branch_backward(upstream, normed, kept, segment, matrices):
    proj_qkv, proj_dense, fc_one, fc_two = matrices
    queries, key_rows, values, log_total, attended, pre_act, activation = kept
    row_count = upstream.shape[0]
    feature_width = proj_qkv.shape[-1]
    head_count = feature_width // HEAD_DIM
    grad_dense = inner_product(attended, upstream)
    grad_fc_two = inner_product(activation, upstream)
    grad_out = jnp.sum(upstream.astype(jnp.float32), axis=0)
    grad_pre = gelu_grad(pre_act, transposed_product(upstream, fc_two))
    grad_fc_bias = jnp.sum(grad_pre, axis=0)
    grad_pre_b = grad_pre.astype(jnp.bfloat16)
    grad_fc_one = inner_product(normed, grad_pre_b)
    grad_att = (
        transposed_product(upstream, proj_dense)
        .astype(jnp.bfloat16)
        .reshape(row_count, head_count, HEAD_DIM)
    )
    cos_part, sin_part = rotary_tables(segment)
    scores = score_block(queries, key_rows, segment)
    prob_f = jnp.exp(scores - log_total)
    prob_b = prob_f.astype(jnp.bfloat16)
    grad_prob = jnp.einsum("qhd,khd->hqk", grad_att, values, preferred_element_type=jnp.float32)
    row_dot = jnp.sum(prob_f * grad_prob, axis=-1, keepdims=True)
    grad_score = (prob_f * (grad_prob - row_dot)).astype(jnp.bfloat16)
    score_scale = HEAD_DIM ** (-0.5)
    grad_query = rotate_pairs(
        jnp.einsum("hqk,khd->qhd", grad_score, key_rows, preferred_element_type=jnp.float32)
        * score_scale,
        cos_part,
        -sin_part,
    ).reshape(row_count, feature_width)
    grad_key = rotate_pairs(
        jnp.einsum("hqk,qhd->khd", grad_score, queries, preferred_element_type=jnp.float32)
        * score_scale,
        cos_part,
        -sin_part,
    ).reshape(row_count, feature_width)
    grad_value = jnp.einsum(
        "hqk,qhd->khd", prob_b, grad_att, preferred_element_type=jnp.float32
    ).reshape(row_count, feature_width)
    grad_qv = jnp.stack([jnp.sum(grad_query, axis=0), jnp.sum(grad_value, axis=0)])
    rounded = [piece_grad.astype(jnp.bfloat16) for piece_grad in (grad_query, grad_key, grad_value)]
    grad_qkv = jnp.stack([inner_product(normed, piece_grad) for piece_grad in rounded])
    grad_normed = transposed_product(grad_pre_b, fc_one)
    for which in range(3):
        grad_normed = grad_normed + transposed_product(rounded[which], proj_qkv[which])
    return (
        grad_normed,
        (grad_qkv, grad_dense, grad_fc_one, grad_fc_two),
        (grad_qv, grad_out, grad_fc_bias),
    )


def norm_backward(grad_normed, standard, inv_std, norm_gain):
    scaled = grad_normed * norm_gain
    grad_gain = jnp.sum(grad_normed * standard, axis=0)
    grad_shift = jnp.sum(grad_normed, axis=0)
    grad_in = inv_std * (
        scaled
        - jnp.mean(scaled, axis=-1, keepdims=True)
        - standard * jnp.mean(scaled * standard, axis=-1, keepdims=True)
    )
    return (grad_in, grad_gain, grad_shift)


def per_device(
    block_input,
    cotangent,
    segments,
    ln_gain,
    ln_bias,
    qkv_weight,
    qv_bias,
    dense_weight,
    out_bias,
    fc1_weight,
    fc1_bias,
    fc2_weight,
):
    micro_count = block_input.shape[0]
    row_count = block_input.shape[1]
    row_share = row_count // lax.axis_size("tensor")
    section_index = lax.axis_index("section")
    is_first = section_index == 0
    row_start = lax.axis_index("tensor") * row_share
    norm_gain = ln_gain[0]
    norm_shift = ln_bias[0]
    bias_out = out_bias[0]
    matrices = (qkv_weight[0], dense_weight[0], fc1_weight[0], fc2_weight[0])
    biases = (qv_bias[0], fc1_bias[0])
    stored = []
    outputs = []
    outgoing = None
    for moment in range(micro_count + 1):
        segment = jnp.where(
            is_first, segments[min(moment, micro_count - 1)], segments[max(moment - 1, 0)]
        )
        incoming = block_input[min(moment, micro_count - 1)]
        if moment > 0:
            arrived = from_behind(outgoing, "section", 1)
        else:
            arrived = jnp.zeros_like(incoming)
        entering = jnp.where(is_first, incoming, arrived)
        residual, standard, inv_std, normed = normalize(entering, norm_gain, norm_shift)
        partial_sum, kept = branch_forward(normed, segment, matrices, biases)
        mixture = lax.psum(partial_sum, "tensor")
        outgoing = (residual + mixture + bias_out).astype(jnp.bfloat16)
        outputs.append(outgoing)
        stored.append((segment, normed, standard, inv_std, kept))
    big_total = None
    small_total = None
    in_grads = []
    passed = None
    for moment in range(micro_count + 1):
        segment, normed, standard, inv_std, kept = stored[micro_count - moment]
        usable = jnp.where(
            is_first, 1.0 if moment > 0 else 0.0, 1.0 if moment < micro_count else 0.0
        ).astype(jnp.bfloat16)
        top_grad = cotangent[max(micro_count - 1 - moment, 0)] * (segment >= 0)[:, None].astype(
            jnp.bfloat16
        )
        if moment > 0:
            returned = from_behind(passed, "section", -1)
        else:
            returned = jnp.zeros_like(top_grad)
        upstream = jnp.where(is_first, returned, top_grad) * usable
        grad_normed, big_terms, small_terms = branch_backward(
            upstream, normed, kept, segment, matrices
        )
        grad_normed = lax.psum(grad_normed, "tensor")
        grad_in, grad_gain, grad_shift = norm_backward(grad_normed, standard, inv_std, norm_gain)
        passed = (upstream.astype(jnp.float32) + grad_in).astype(jnp.bfloat16)
        in_grads.append(passed)
        small_terms = (grad_gain, grad_shift) + tuple(small_terms)
        if big_total is None:
            big_total = tuple(big_terms)
            small_total = small_terms
        else:
            big_total = tuple((jnp.add(total, term) for total, term in zip(big_total, big_terms)))
            small_total = tuple(
                (jnp.add(total, term) for total, term in zip(small_total, small_terms))
            )
    big_total = (
        lax.psum_scatter(
            big_total[0].astype(jnp.bfloat16), "dp", scatter_dimension=1, tiled=True
        ).astype(jnp.float32),
        lax.psum_scatter(
            big_total[1].astype(jnp.bfloat16), "dp", scatter_dimension=1, tiled=True
        ).astype(jnp.float32),
        lax.psum_scatter(
            big_total[2].astype(jnp.bfloat16), "dp", scatter_dimension=0, tiled=True
        ).astype(jnp.float32),
        lax.psum_scatter(
            big_total[3].astype(jnp.bfloat16), "dp", scatter_dimension=1, tiled=True
        ).astype(jnp.float32),
    )
    grad_qkv, grad_dense, grad_fc_one, grad_fc_two = big_total
    grad_gain, grad_shift, grad_qv, grad_out, grad_fc_bias = small_total
    grad_gain, grad_shift, grad_qv, grad_out, grad_fc_bias = (
        lax.psum(grad_gain.astype(jnp.bfloat16), "dp").astype(jnp.float32),
        lax.psum(grad_shift.astype(jnp.bfloat16), "dp").astype(jnp.float32),
        lax.psum(grad_qv.astype(jnp.bfloat16), "dp").astype(jnp.float32),
        lax.psum(grad_out.astype(jnp.bfloat16), "dp").astype(jnp.float32),
        lax.psum(grad_fc_bias.astype(jnp.bfloat16), "dp").astype(jnp.float32),
    )
    layer_out = lax.dynamic_slice_in_dim(jnp.stack(outputs), section_index, micro_count, 0)
    in_grad = lax.dynamic_slice_in_dim(jnp.stack(in_grads[::-1]), section_index, micro_count, 0)
    layer_out = lax.dynamic_slice_in_dim(layer_out, row_start, row_share, 1)
    in_grad = lax.dynamic_slice_in_dim(in_grad, row_start, row_share, 1)
    return (
        layer_out[None],
        in_grad[None],
        grad_gain[None],
        grad_shift[None],
        grad_qkv[None],
        grad_qv[None],
        grad_dense[None],
        grad_out[None],
        grad_fc_one[None],
        grad_fc_bias[None],
        grad_fc_two[None],
    )


def solution(mesh):
    return jax.shard_map(
        per_device,
        mesh=mesh,
        in_specs=(
            P(None, "dp", None),
            P(None, "dp", None),
            P(None, "dp"),
            P("section", None),
            P("section", None),
            P("section", None, None, "tensor"),
            P("section", None, "tensor"),
            P("section", "tensor", None),
            P("section", None),
            P("section", None, "tensor"),
            P("section", "tensor"),
            P("section", "tensor", None),
        ),
        out_specs=(
            P("section", None, ("dp", "tensor"), None),
            P("section", None, ("dp", "tensor"), None),
            P("section", None),
            P("section", None),
            P("section", None, "dp", "tensor"),
            P("section", None, "tensor"),
            P("section", "tensor", "dp"),
            P("section", None),
            P("section", "dp", "tensor"),
            P("section", "tensor"),
            P("section", "tensor", "dp"),
        ),
        check_vma=False,
    )
```

profile of v0, /device:TPU:0, one launch (start us, length us, event | category | flops | bytes accessed | tf_op | source)
XLA Modules:
  0.0 1297.7 jit_solution(3893750009898846996)
XLA Ops:
  44.5 55.3 %all-reduce.12.cloned.1.call-done = f32[128,2048]{1,0:T(8,128)} async-done(((f32[128,2048]{1,0:T(8,128)}), f32[128,2048]{1,0:T(8,128)}) %all-reduce.12.cloned.1.call-update) | async-done | bytes 1048592 | tf_op jit(solution)/shard_map/psum | solution.py:228
  123.7 52.6 %all-reduce.14.cloned.1.call-done = f32[128,2048]{1,0:T(8,128)} async-done(((f32[128,2048]{1,0:T(8,128)}), f32[128,2048]{1,0:T(8,128)}) %all-reduce.14.cloned.1.call-update) | async-done | bytes 1048592 | tf_op jit(solution)/shard_map/psum | solution.py:228
  204.4 52.6 %all-reduce.16.cloned.1.call-done = f32[128,2048]{1,0:T(8,128)} async-done(((f32[128,2048]{1,0:T(8,128)}), f32[128,2048]{1,0:T(8,128)}) %all-reduce.16.cloned.1.call-update) | async-done | bytes 1048592 | tf_op jit(solution)/shard_map/psum | solution.py:228
  259.3 13.9 %collective-permute-start.2 = (bf16[128,2048]{1,0:T(8,128)(2,1)S(1)}, bf16[128,2048]{1,0:T(8,128)(2,1)S(1)}, u32[]{:S(2)}, u32[]{:S(2)}) collective-permute-start(bf16[128,2048]{1,0:T(8,128)(2,1)S(1)} %get-tuple-element.59), channel_id=1, source_target_pairs={{0,16},{1,17},{2,18},{3,19},{4,20},{5,21},{6,22},{7,23},{8,24},{9,... | collective-permute-start | bytes 1572872 | tf_op jit(solution)/shard_map/ppermute | solution.py:17
  295.9 52.5 %all-reduce.18.cloned.1.call-done = f32[128,2048]{1,0:T(8,128)} async-done(((f32[128,2048]{1,0:T(8,128)}), f32[128,2048]{1,0:T(8,128)}) %all-reduce.18.cloned.1.call-update) | async-done | bytes 1048592 | tf_op jit(solution)/shard_map/psum | solution.py:228
  377.6 8.3 fusion.511
  392.8 52.2 %all-reduce.20.cloned.1.call-done = f32[128,2048]{1,0:T(8,128)} async-done(((f32[128,2048]{1,0:T(8,128)}), f32[128,2048]{1,0:T(8,128)}) %all-reduce.20.cloned.1.call-update) | async-done | bytes 1048592 | tf_op jit(solution)/shard_map/psum | solution.py:252
  456.0 8.3 fusion.512
  483.2 52.6 %all-reduce.22.cloned.1.call-done = f32[128,2048]{1,0:T(8,128)} async-done(((f32[128,2048]{1,0:T(8,128)}), f32[128,2048]{1,0:T(8,128)}) %all-reduce.22.cloned.1.call-update) | async-done | bytes 1048592 | tf_op jit(solution)/shard_map/psum | solution.py:252
  546.1 8.3 fusion.510
  574.1 52.6 %all-reduce.24.cloned.1.call-done = f32[128,2048]{1,0:T(8,128)} async-done(((f32[128,2048]{1,0:T(8,128)}), f32[128,2048]{1,0:T(8,128)}) %all-reduce.24.cloned.1.call-update) | async-done | bytes 1048592 | tf_op jit(solution)/shard_map/psum | solution.py:252
  636.7 8.3 fusion.509
  675.6 41.7 %all-reduce.26.cloned.1.call-done = f32[128,2048]{1,0:T(8,128)} async-done(((f32[128,2048]{1,0:T(8,128)}), f32[128,2048]{1,0:T(8,128)}) %all-reduce.26.cloned.1.call-update) | async-done | bytes 1048592 | tf_op jit(solution)/shard_map/psum | solution.py:252
  732.6 8.3 fusion.508
  803.0 21.3 %fusion.3 = bf16[3,2048,512]{2,1,0:T(8,128)(2,1)} fusion(f32[1,2048,512]{2,1,0:T(8,128)S(1)} %copy-done.9, f32[1,2048,512]{2,1,0:T(8,128)S(1)} %copy-done.10, f32[1,2048,512]{2,1,0:T(8,128)S(1)} %copy-done.11, f32[1,2048,512]{2,1,0:T(8,128)} %convolution_bitcast_fusion.9, f32[1,2048,512]{2,1,0:T(8,128)} %convolution_bitcast_fusion.10, ...), kind=kLoop, calls=%fused_computation.6 | loop fusion | flops 47185920 | bytes 69206016 | tf_op jit(solution)/shard_map/convert_element_type | solution.py:267
  825.4 9.4 fusion.367
  834.8 8.4 fusion.364
  843.3 8.3 fusion.361
  859.9 25.7 %add_convert_fusion.1 = bf16[2048,2048]{1,0:T(8,128)(2,1)} fusion(f32[2048,2048]{1,0:T(8,128)} %fusion.358, f32[2048,2048]{1,0:T(8,128)} %fusion.361, f32[2048,2048]{1,0:T(8,128)} %fusion.367, f32[2048,2048]{1,0:T(8,128)} %fusion.364, f32[128]{0:T(128)S(1)} %copy-done.235, f32[2048]{0:T(1024)S(1)} %bitcast.733, f32[2048]{0:T(1024)S(1)} %bitcast.691, ...), kind=kOutput, calls=%fused_computation.1 | convolution fusion | flops 1096548352 | bytes 76563456 | tf_op jit(solution)/shard_map/dot_general | solution.py:50
  887.1 9.4 fusion.447
  921.0 25.2 %add_convert_fusion = bf16[2048,2048]{1,0:T(8,128)(2,1)} fusion(f32[2048,2048]{1,0:T(8,128)} %fusion.444, f32[2048,2048]{1,0:T(8,128)} %fusion.445, f32[2048,2048]{1,0:T(8,128)} %fusion.447, f32[2048,2048]{1,0:T(8,128)} %fusion.446, bf16[128,2048]{1,0:T(8,128)(2,1)S(1)} %copy-done.13, f32[128,2048]{1,0:T(8,128)S(1)} %copy-done.118), kind=kOutput, calls=%fused_computation | convolution fusion | flops 1097072640 | bytes 77070336 | tf_op jit(solution)/shard_map/dot_general | solution.py:50
  950.9 23.0 %all-reduce.1 = (bf16[1,2048]{1,0:T(2,128)(2,1)S(1)}, bf16[1,2048]{1,0:T(2,128)(2,1)S(1)}, bf16[1,2,512]{2,1,0:T(2,128)(2,1)S(1)}, bf16[1,2048]{1,0:T(2,128)(2,1)S(1)}, bf16[1,2048]{1,0:T(2,128)(2,1)S(1)}) all-reduce(bf16[1,2048]{1,0:T(2,128)(2,1)S(1)} %broadcast_in_dim.124, ...), channel_id=1, replica_groups=mesh['section'=2,'dp'=4,'tensor'=4] {'dp'}, use_global_device_ids=true, to_apply=%region_55.56 | all-reduce | flops 9216 | bytes 36864 | tf_op jit(solution)/shard_map/psum | solution.py:282
  995.3 143.8 %reduce-scatter.9.cloned.1.call-done = bf16[512,2048]{1,0:T(8,128)(2,1)} async-done(((bf16[2048,2048]{1,0:T(8,128)(2,1)}), bf16[512,2048]{1,0:T(8,128)(2,1)}) %reduce-scatter.9.cloned.1.call-update) | async-done | bytes 2097168 | tf_op jit(solution)/shard_map/reduce_scatter | solution.py:272
  1143.4 143.3 %reduce-scatter.11.cloned.1.call-done = bf16[2048,512]{1,0:T(8,128)(2,1)} async-done(((bf16[2048,2048]{1,0:T(8,128)(2,1)}), bf16[2048,512]{1,0:T(8,128)(2,1)}) %reduce-scatter.11.cloned.1.call-update) | async-done | bytes 2097168 | tf_op jit(solution)/shard_map/reduce_scatter | solution.py:275
  (940 shorter events, 394.2 us)
Async XLA Ops:
  7.2 92.6 %all-reduce.12.cloned.1.call-start = ((), (), s32[]{:S(2)}) async-start(), calls=%async_computation.4 | async-start | bytes 2097152 | tf_op jit(solution)/shard_map/psum | solution.py:228
  15.0 97.0 %copy-start.258 = (f32[1,1,512]{2,1,0:T(1,128)}, f32[1,1,512]{2,1,0:T(1,128)S(1)}, u32[]{:S(2)}) copy-start(f32[1,1,512]{2,1,0:T(1,128)S(1)} %get-tuple-element.133) | copy-start | bytes 6148
  15.0 99.8 %copy-start.254 = (f32[1,1,512]{2,1,0:T(1,128)}, f32[1,1,512]{2,1,0:T(1,128)S(1)}, u32[]{:S(2)}) copy-start(f32[1,1,512]{2,1,0:T(1,128)S(1)} %get-tuple-element.132) | copy-start | bytes 6148
  44.5 131.8 %all-reduce.14.cloned.1.call-start = ((), (), s32[]{:S(2)}) async-start(), calls=%async_computation.5 | async-start | bytes 2097152 | tf_op jit(solution)/shard_map/psum | solution.py:228
  102.3 3.1 collective-permute-start
  123.6 133.3 %all-reduce.16.cloned.1.call-start = ((), (), s32[]{:S(2)}) async-start(), calls=%async_computation.6 | async-start | bytes 2097152 | tf_op jit(solution)/shard_map/psum | solution.py:228
  178.6 3.1 collective-permute-start.1
  204.4 144.0 %all-reduce.18.cloned.1.call-start = ((), (), s32[]{:S(2)}) async-start(), calls=%async_computation.7 | async-start | bytes 2097152 | tf_op jit(solution)/shard_map/psum | solution.py:228
  259.3 13.9 %collective-permute-start.2 = (bf16[128,2048]{1,0:T(8,128)(2,1)S(1)}, bf16[128,2048]{1,0:T(8,128)(2,1)S(1)}, u32[]{:S(2)}, u32[]{:S(2)}) collective-permute-start(bf16[128,2048]{1,0:T(8,128)(2,1)S(1)} %get-tuple-element.59), channel_id=1, source_target_pairs={{0,16},{1,17},{2,18},{3,19},{4,20},{5,21},{6,22},{7,23},{8,24},{9,... | collective-permute-start | bytes 1572872 | tf_op jit(solution)/shard_map/ppermute | solution.py:17
  295.8 149.2 %all-reduce.20.cloned.1.call-start = ((), (), s32[]{:S(2)}) async-start(), calls=%async_computation.8 | async-start | bytes 2097152 | tf_op jit(solution)/shard_map/psum | solution.py:252
  350.9 4.4 collective-permute-start.3
  392.4 143.4 %all-reduce.22.cloned.1.call-start = ((), (), s32[]{:S(2)}) async-start(), calls=%async_computation.9 | async-start | bytes 2097152 | tf_op jit(solution)/shard_map/psum | solution.py:252
  450.3 3.8 collective-permute-start.4
  483.2 143.5 %all-reduce.24.cloned.1.call-start = ((), (), s32[]{:S(2)}) async-start(), calls=%async_computation.10 | async-start | bytes 2097152 | tf_op jit(solution)/shard_map/psum | solution.py:252
  540.4 3.8 collective-permute-start.5
  574.1 143.2 %all-reduce.26.cloned.1.call-start = ((), (), s32[]{:S(2)}) async-start(), calls=%async_computation.11 | async-start | bytes 2097152 | tf_op jit(solution)/shard_map/psum | solution.py:252
  631.0 3.8 collective-permute-start.6
  664.7 284.2 %all-reduce.28.cloned.1.call-start = ((), (), s32[]{:S(2)}) async-start(), calls=%async_computation.16 | async-start | bytes 4194304 | tf_op jit(solution)/shard_map/psum | solution.py:228
  721.6 9.1 collective-permute-start.7
  761.7 224.3 %reduce-scatter.7.cloned.1.call-start = ((), (), s32[]{:S(2)}) async-start(), calls=%async_computation.13 | async-start | bytes 2621440 | tf_op jit(solution)/shard_map/reduce_scatter | solution.py:269
  768.4 223.4 %reduce-scatter.5.cloned.1.call-start = ((), (), s32[]{:S(2)}) async-start(), calls=%async_computation.12 | async-start | bytes 7864320 | tf_op jit(solution)/shard_map/reduce_scatter | solution.py:266
  824.4 314.8 %reduce-scatter.9.cloned.1.call-start = ((), (), s32[]{:S(2)}) async-start(), calls=%async_computation.14 | async-start | bytes 10485760 | tf_op jit(solution)/shard_map/reduce_scatter | solution.py:272
  885.6 401.2 %reduce-scatter.11.cloned.1.call-start = ((), (), s32[]{:S(2)}) async-start(), calls=%async_computation.15 | async-start | bytes 10485760 | tf_op jit(solution)/shard_map/reduce_scatter | solution.py:275
  1139.1 151.8 %copy-start.1 = (bf16[1,512,2048]{2,1,0:T(8,128)(2,1)S(1)}, bf16[1,512,2048]{2,1,0:T(8,128)(2,1)}, u32[]{:S(2)}) copy-start(bf16[1,512,2048]{2,1,0:T(8,128)(2,1)} %param.19) | copy-start | bytes 6291460
  (285 other events, 2061.7 us)
Sparse Core Ops, SparseCore 0:
  44.6 55.1 all-reduce.11
  123.7 52.4 all-reduce.13
  204.5 52.4 all-reduce.15
  295.9 52.4 all-reduce.17
  392.5 52.4 all-reduce.19
  483.3 52.4 all-reduce.21
  574.2 52.4 all-reduce.23
  664.8 52.4 all-reduce.25
  761.8 70.2 all-reduce.27
  834.2 43.6 reduce-scatter.6
  880.2 111.5 reduce-scatter.4
  994.0 145.0 reduce-scatter.8
  1141.5 145.2 reduce-scatter.10
where the time goes:
time: 1310 us; the launch traced here: 1300 us
  waiting for transfers between devices  711 us (54%)
  matrix products  366 us (28%)
  other arithmetic  107 us (8%)
  local copies, waits for them, and re-layouts  44.1 us (3%)
  starting transfers between devices  27.7 us (2%)
  blocking collectives  23 us (2%)
  between operations  18.4 us (1%)
    psum x5, waiting for transfers between devices, per_device(): mixture = lax.psum(partial_sum, 'tensor')  213 us
    psum x4, waiting for transfers between devices, per_device(): grad_normed = lax.psum(grad_normed, 'tensor')  199 us
    dot_general x30, matrix products, inner_product(): lax.dot_general(left, right, (((0,), (0,)), ((), ())), preferred_element_...  170 us
    reduce_scatter x1, waiting for transfers between devices, per_device(): lax.psum_scatter(big_total[2].astype(jnp.bfloat16), 'dp', scatter_dimensi...  144 us
    reduce_scatter x1, waiting for transfers between devices, per_device(): lax.psum_scatter(big_total[3].astype(jnp.bfloat16), 'dp', scatter_dimensi...  143 us
    dot_general x30, matrix products, transposed_product(): lax.dot_general(left, right, (((1,), (1,)), ((), ())), preferred_element_...  96.9 us
  transfers between devices with their start and end apart: 21, of which 16 were waited for; matrix products, arithmetic and copies ran while one was open for 18% of the time, Pallas kernels for 0%

commit v1 on v0

v1 whole, which is shorter than its diff:
```python
import functools

import jax
import jax.numpy as jnp
from jax import lax
from jax.experimental import pallas as pl
from jax.experimental.pallas import tpu as pltpu
from jax.sharding import PartitionSpec as P

HEAD_DIM = 64
ROT = 32

NORM_EPS = 1e-05
MASKED = -1e30
MESH = pl.DeviceIdType.MESH


def rotary_tables(segment):
    length = segment.shape[-1]
    row_index = jnp.arange(length, dtype=jnp.int32)[None, :]
    previous = jnp.concatenate([segment[:, :1], segment[:, :-1]], axis=1)
    starts = jnp.where((row_index == 0) | (segment != previous), row_index, 0)
    position = (row_index - lax.cummax(starts, axis=1)).astype(jnp.float32)
    half_rot = ROT // 2
    frequency = 10000.0 ** (-2.0 * jnp.arange(half_rot, dtype=jnp.float32) / ROT)
    phase_angle = position[..., None] * frequency
    return (jnp.cos(phase_angle)[:, :, None, :], jnp.sin(phase_angle)[:, :, None, :])


def rotate_pairs(heads_in, cos_part, sin_part):
    half_rot = ROT // 2
    lower_half = heads_in[..., :half_rot]
    upper_half = heads_in[..., half_rot:ROT]
    return jnp.concatenate(
        [
            lower_half * cos_part - upper_half * sin_part,
            upper_half * cos_part + lower_half * sin_part,
            heads_in[..., ROT:],
        ],
        axis=-1,
    )


def mm(left, right, dims=((1,), (0,))):
    return lax.dot_general(left, right, (dims, ((), ())), preferred_element_type=jnp.float32)


def score_blocks(queries, key_rows, segment):
    length = segment.shape[-1]
    row_index = jnp.arange(length, dtype=jnp.int32)
    allowed = (segment[:, :, None] == segment[:, None, :]) & (
        row_index[None, :] <= row_index[:, None]
    )
    scores = jnp.einsum(
        "bqhd,bkhd->bhqk", queries, key_rows, preferred_element_type=jnp.float32
    ) * HEAD_DIM ** (-0.5)
    return jnp.where(allowed[:, None, :, :], scores, MASKED)


def gelu_grad(pre_act, grad_act):
    _, pull_back = jax.vjp(lambda value_in: jax.nn.gelu(value_in, approximate=True), pre_act)
    return pull_back(grad_act)[0]


def normalize(hidden, norm_gain, norm_shift):
    residual = hidden.astype(jnp.float32)
    centred = residual - jnp.mean(residual, axis=-1, keepdims=True)
    inv_std = lax.rsqrt(jnp.mean(centred * centred, axis=-1, keepdims=True) + NORM_EPS)
    return (centred * inv_std * norm_gain + norm_shift).astype(jnp.bfloat16)


def attention_forward(normed, segment, tables, proj_qkv, bias_qv):
    blocks, rows = segment.shape
    heads = proj_qkv.shape[-1] // HEAD_DIM
    shape = (blocks, rows, heads, HEAD_DIM)
    cos_part, sin_part = tables
    query_f = (mm(normed, proj_qkv[0]) + bias_qv[0]).reshape(shape)
    key_f = mm(normed, proj_qkv[1]).reshape(shape)
    values = (mm(normed, proj_qkv[2]) + bias_qv[1]).astype(jnp.bfloat16).reshape(shape)
    queries = rotate_pairs(query_f, cos_part, sin_part).astype(jnp.bfloat16)
    key_rows = rotate_pairs(key_f, cos_part, sin_part).astype(jnp.bfloat16)
    scores = score_blocks(queries, key_rows, segment)
    row_max = jnp.max(scores, axis=-1, keepdims=True)
    log_total = row_max + jnp.log(jnp.sum(jnp.exp(scores - row_max), axis=-1, keepdims=True))
    prob_f = jnp.exp(scores - log_total)
    attended = (
        jnp.einsum(
            "bhqk,bkhd->bqhd", prob_f.astype(jnp.bfloat16), values,
            preferred_element_type=jnp.float32,
        )
        .astype(jnp.bfloat16)
        .reshape(blocks * rows, heads * HEAD_DIM)
    )
    return attended, (queries, key_rows, values, log_total)


def attention_backward(upstream, segment, tables, proj_dense, kept):
    queries, key_rows, values, log_total = kept
    shape = queries.shape
    flat = (shape[0] * shape[1], shape[2] * shape[3])
    cos_part, sin_part = tables
    grad_att = mm(upstream, proj_dense, ((1,), (1,))).astype(jnp.bfloat16).reshape(shape)
    prob_f = jnp.exp(score_blocks(queries, key_rows, segment) - log_total)
    prob_b = prob_f.astype(jnp.bfloat16)
    grad_prob = jnp.einsum("bqhd,bkhd->bhqk", grad_att, values, preferred_element_type=jnp.float32)
    row_dot = jnp.sum(prob_f * grad_prob, axis=-1, keepdims=True)
    grad_score = (prob_f * (grad_prob - row_dot)).astype(jnp.bfloat16)
    scale = HEAD_DIM ** (-0.5)
    grad_query = rotate_pairs(
        jnp.einsum("bhqk,bkhd->bqhd", grad_score, key_rows, preferred_element_type=jnp.float32)
        * scale,
        cos_part,
        -sin_part,
    ).reshape(flat)
    grad_key = rotate_pairs(
        jnp.einsum("bhqk,bqhd->bkhd", grad_score, queries, preferred_element_type=jnp.float32)
        * scale,
        cos_part,
        -sin_part,
    ).reshape(flat)
    grad_value = jnp.einsum(
        "bhqk,bqhd->bkhd", prob_b, grad_att, preferred_element_type=jnp.float32
    ).reshape(flat)
    return grad_query, grad_key, grad_value


def partner(t, k):
    out, bit = t, 1
    while bit <= k:
        if k & bit:
            out = out + (1 - 2 * (lax.rem(lax.div(t, bit), 2))) * bit
        bit *= 2
    return out


def enter(n, section_target, is_waiter):
    t = lax.axis_index("tensor")
    sec = lax.axis_index("section")
    barrier = pltpu.get_barrier_semaphore()
    for k in range(1, n):
        pl.semaphore_signal(
            barrier, inc=1, device_id={"tensor": partner(t, k)}, device_id_type=MESH
        )
    if section_target is None:
        pl.semaphore_wait(barrier, n - 1)
        return

    @pl.when(sec == section_target)
    def _():
        pl.semaphore_signal(barrier, inc=1, device_id={"section": 1 - sec}, device_id_type=MESH)
        pl.semaphore_wait(barrier, n - 1)

    @pl.when(sec != section_target)
    def _():
        pl.semaphore_wait(barrier, n)


def scatter_sum(n, partial_ref, recv, send_sem, recv_sem, own_rows):
    t = lax.axis_index("tensor")
    copies = []
    for k in range(n - 1, 0, -1):
        peer = partner(t, k)
        copy = pltpu.make_async_remote_copy(
            src_ref=partial_ref.at[:, peer],
            dst_ref=recv.at[k - 1],
            send_sem=send_sem.at[k - 1],
            recv_sem=recv_sem.at[k - 1],
            device_id={"tensor": peer},
            device_id_type=MESH,
        )
        copy.start()
        copies.append((k, copy))
    total = partial_ref[:, t].astype(jnp.float32) + own_rows
    for k, copy in copies:
        copy.wait_recv()
        total = total + recv[k - 1].astype(jnp.float32)
    return total, copies


def spread(n, full_ref, send_sem, recv_sem):
    t = lax.axis_index("tensor")
    copies = []
    for k in range(n - 1, 0, -1):
        copy = pltpu.make_async_remote_copy(
            src_ref=full_ref.at[:, t],
            dst_ref=full_ref.at[:, t],
            send_sem=send_sem.at[k - 1],
            recv_sem=recv_sem.at[k - 1],
            device_id={"tensor": partner(t, k)},
            device_id_type=MESH,
        )
        copy.start()
        copies.append(copy)
    for copy in copies:
        copy.wait()


def forward_kernel(
    n, last, partial_ref, resid_ref, bias_ref, gain_ref, shift_ref, *rest
):
    if last:
        out_ref, recv, send_sem, recv_sem = rest
        enter(n, None, None)
        total, copies = scatter_sum(
            n, partial_ref, recv, send_sem, recv_sem,
            resid_ref[...].astype(jnp.float32) + bias_ref[...][None],
        )
        out_ref[...] = total.astype(jnp.bfloat16)
        for _, copy in copies:
            copy.wait_send()
        return
    (n0_ref, x_ref, out_ref, hidden_ref, full_ref, recv, send_sem, recv_sem,
     hop_send, hop_recv, ag_send, ag_recv) = rest
    sec = lax.axis_index("section")
    t = lax.axis_index("tensor")
    enter(n, 1, None)
    total, copies = scatter_sum(
        n, partial_ref, recv, send_sem, recv_sem,
        resid_ref[...].astype(jnp.float32) + bias_ref[...][None],
    )
    out_ref[...] = total.astype(jnp.bfloat16)
    hop = pltpu.make_async_remote_copy(
        src_ref=out_ref,
        dst_ref=hidden_ref,
        send_sem=hop_send,
        recv_sem=hop_recv,
        device_id={"section": 1 - sec},
        device_id_type=MESH,
    )

    @pl.when(sec == 0)
    def _():
        hop.start()
        full_ref[...] = n0_ref[...]
        hidden_ref[...] = x_ref[...]
        hop.wait_send()

    @pl.when(sec == 1)
    def _():
        hop.wait_recv()
        residual = hidden_ref[...].astype(jnp.float32)
        centred = residual - jnp.mean(residual, axis=-1, keepdims=True)
        inv_std = lax.rsqrt(jnp.mean(centred * centred, axis=-1, keepdims=True) + NORM_EPS)
        normed = centred * inv_std * gain_ref[...][None] + shift_ref[...][None]
        full_ref[:, t] = normed.astype(jnp.bfloat16)
        spread(n, full_ref, ag_send, ag_recv)

    for _, copy in copies:
        copy.wait_send()


def backward_kernel(n, last, partial_ref, up_ref, hidden_ref, gain_ref, *rest):
    t = lax.axis_index("tensor")
    sec = lax.axis_index("section")
    if last:
        out_ref, ggain_ref, gshift_ref, recv, send_sem, recv_sem = rest
        enter(n, None, None)
    else:
        (cot_ref, out_ref, ggain_ref, gshift_ref, full_ref, recv, send_sem, recv_sem,
         hop_send, hop_recv, ag_send, ag_recv) = rest
        enter(n, 0, None)
    grad_normed, copies = scatter_sum(n, partial_ref, recv, send_sem, recv_sem, 0.0)
    residual = hidden_ref[...].astype(jnp.float32)
    centred = residual - jnp.mean(residual, axis=-1, keepdims=True)
    inv_std = lax.rsqrt(jnp.mean(centred * centred, axis=-1, keepdims=True) + NORM_EPS)
    standard = centred * inv_std
    scaled = grad_normed * gain_ref[...][None]
    grad_in = inv_std * (
        scaled
        - jnp.mean(scaled, axis=-1, keepdims=True)
        - standard * jnp.mean(scaled * standard, axis=-1, keepdims=True)
    )
    out_ref[...] = (up_ref[:, t].astype(jnp.float32) + grad_in).astype(jnp.bfloat16)
    if not last:
        hop = pltpu.make_async_remote_copy(
            src_ref=out_ref,
            dst_ref=full_ref.at[:, t],
            send_sem=hop_send,
            recv_sem=hop_recv,
            device_id={"section": 1 - sec},
            device_id_type=MESH,
        )

        @pl.when(sec == 1)
        def _():
            hop.start()
            full_ref[...] = cot_ref[...]
            hop.wait_send()

        @pl.when(sec == 0)
        def _():
            hop.wait_recv()
            spread(n, full_ref, ag_send, ag_recv)

    ggain_ref[...] = jnp.sum(jnp.sum(grad_normed * standard, axis=0), axis=0, keepdims=True)
    gshift_ref[...] = jnp.sum(jnp.sum(grad_normed, axis=0), axis=0, keepdims=True)
    for _, copy in copies:
        copy.wait_send()


def relay_call(kernel, n, last, ident, args, outs, rows_shape):
    sems = [pltpu.SemaphoreType.DMA((n - 1,)), pltpu.SemaphoreType.DMA((n - 1,))]
    scratch = [pltpu.VMEM((n - 1,) + rows_shape, jnp.bfloat16)] + sems
    if not last:
        scratch += [pltpu.SemaphoreType.DMA, pltpu.SemaphoreType.DMA] + sems
    vmem = pl.BlockSpec(memory_space=pltpu.VMEM)
    return pl.pallas_call(
        functools.partial(kernel, n, last),
        out_shape=outs,
        in_specs=[vmem] * len(args),
        out_specs=[vmem] * len(outs),
        scratch_shapes=scratch,
        compiler_params=pltpu.CompilerParams(
            collective_id=ident, has_side_effects=True, vmem_limit_bytes=32 * 1024 * 1024
        ),
    )(*args)


def small_kernel(axes, x_ref, out_ref, gathered, send_sem, recv_sem):
    sizes = [lax.axis_size(a) for a in axes]
    index = [lax.axis_index(a) for a in axes]
    count = 1
    for s in sizes:
        count *= s

    def shifted(k):
        ids, parts = {}, []
        for a, s, i in zip(reversed(axes), reversed(sizes), reversed(index)):
            ids[a] = lax.rem(i + k % s, s)
            k //= s
        return ids

    mine = 0
    for s, i in zip(sizes, index):
        mine = mine * s + i
    barrier = pltpu.get_barrier_semaphore()
    for k in range(1, count):
        pl.semaphore_signal(barrier, inc=1, device_id=shifted(k), device_id_type=MESH)
    pl.semaphore_wait(barrier, count - 1)
    copies = []
    for k in range(1, count):
        copy = pltpu.make_async_remote_copy(
            src_ref=x_ref,
            dst_ref=gathered.at[mine],
            send_sem=send_sem.at[k],
            recv_sem=recv_sem.at[k],
            device_id=shifted(k),
            device_id_type=MESH,
        )
        copy.start()
        copies.append(copy)
    gathered[mine] = x_ref[...]
    for copy in copies:
        copy.wait()
    total = gathered[0]
    for i in range(1, count):
        total = total + gathered[i]
    out_ref[...] = total


def small_sum(x, axes, ident):
    count = 1
    for a in axes:
        count *= lax.axis_size(a)
    vmem = pl.BlockSpec(memory_space=pltpu.VMEM)
    return pl.pallas_call(
        functools.partial(small_kernel, axes),
        out_shape=jax.ShapeDtypeStruct(x.shape, x.dtype),
        in_specs=[vmem],
        out_specs=vmem,
        scratch_shapes=[
            pltpu.VMEM((count,) + x.shape, x.dtype),
            pltpu.SemaphoreType.DMA((count,)),
            pltpu.SemaphoreType.DMA((count,)),
        ],
        compiler_params=pltpu.CompilerParams(collective_id=ident, has_side_effects=True),
    )(x)


def per_device(
    block_input,
    cotangent,
    segments,
    ln_gain,
    ln_bias,
    qkv_weight,
    qv_bias,
    dense_weight,
    out_bias,
    fc1_weight,
    fc1_bias,
    fc2_weight,
):
    micro, rows, width = block_input.shape
    n = lax.axis_size("tensor")
    n_dp = lax.axis_size("dp")
    share = rows // n
    group = 2 if micro % 2 == 0 else 1
    count = micro // group
    is_first = lax.axis_index("section") == 0
    row_start = lax.axis_index("tensor") * share
    norm_gain, norm_shift = ln_gain, ln_bias
    proj_qkv, proj_dense, fc_one, fc_two = (
        qkv_weight[0], dense_weight[0], fc1_weight[0], fc2_weight[0]
    )
    bias_qv, bias_fc = qv_bias[0], fc1_bias[0]
    bf16, f32 = jnp.bfloat16, jnp.float32

    live = (segments >= 0)[:, :, None].astype(bf16)
    top = cotangent * live
    own_rows = lambda x: lax.dynamic_slice_in_dim(x, row_start, share, 1)
    first_normed = normalize(block_input, norm_gain, norm_shift)
    x_rows = own_rows(block_input)
    all_segments = lax.all_gather(segments, "dp", axis=1)

    def gather(x):
        return lax.all_gather(x, ("dp", "tensor"), axis=1, tiled=True)

    early = gather(jnp.where(is_first, own_rows(first_normed), own_rows(top)))

    cut = lambda x, i: x[i * group : (i + 1) * group]
    four = lambda x: x.reshape(group, n, share, width)
    flat = lambda x: x.reshape(group * rows, width)
    sds = jax.ShapeDtypeStruct
    rows_shape = (group, share, width)

    normed = four(cut(first_normed, 0))
    hidden = cut(x_rows, 0)
    stored, outputs = [], []
    for moment in range(count + 1):
        last = moment == count
        segment = jnp.where(
            is_first, cut(segments, min(moment, count - 1)), cut(segments, max(moment - 1, 0))
        )
        tables = rotary_tables(segment)
        attended, kept = attention_forward(flat(normed), segment, tables, proj_qkv, bias_qv)
        pre_act = mm(flat(normed), fc_one) + bias_fc
        activation = jax.nn.gelu(pre_act, approximate=True).astype(bf16)
        partial = (mm(attended, proj_dense) + mm(activation, fc_two)).astype(bf16)
        stored.append((segment, tables, hidden, normed, kept, pre_act))
        args = [four(partial), hidden, out_bias, norm_gain, norm_shift]
        if last:
            (out,) = relay_call(
                forward_kernel, n, True, 1, args, [sds(rows_shape, bf16)], rows_shape
            )
        else:
            ahead = min(moment + 1, count - 1)
            args += [four(cut(first_normed, ahead)), cut(x_rows, ahead)]
            out, hidden, normed = relay_call(
                forward_kernel, n, False, 0, args,
                [sds(rows_shape, bf16), sds(rows_shape, bf16),
                 sds((group, n, share, width), bf16)],
                rows_shape,
            )
        outputs.append(out)

    up = jnp.where(is_first, jnp.zeros((), bf16), four(cut(top, count - 1)))
    in_grads, late = [], []
    gain_sum = jnp.zeros((1, width), f32)
    shift_sum = jnp.zeros((1, width), f32)
    for moment in range(count + 1):
        last = moment == count
        segment, tables, hidden, normed, kept, pre_act = stored[count - moment]
        up_flat = flat(up)
        grad_pre = gelu_grad(pre_act, mm(up_flat, fc_two, ((1,), (1,)))).astype(bf16)
        pieces = attention_backward(up_flat, segment, tables, proj_dense, kept)
        grad_normed = mm(grad_pre, fc_one, ((1,), (1,)))
        for which in range(3):
            grad_normed = grad_normed + mm(
                pieces[which].astype(bf16), proj_qkv[which], ((1,), (1,))
            )
        args = [four(grad_normed.astype(bf16)), up, hidden, norm_gain]
        outs = [sds(rows_shape, bf16), sds((1, width), f32), sds((1, width), f32)]
        if last:
            passed, g_gain, g_shift = relay_call(
                backward_kernel, n, True, 3, args, outs, rows_shape
            )
        else:
            args.append(
                four(cut(top, count - 2 - moment))
                if moment < count - 1
                else jnp.zeros((group, n, share, width), bf16)
            )
            passed, g_gain, g_shift, up = relay_call(
                backward_kernel, n, False, 2, args,
                outs + [sds((group, n, share, width), bf16)], rows_shape,
            )
            up_rows = lax.dynamic_index_in_dim(up, lax.axis_index("tensor"), 1, keepdims=False)
            normed_rows = lax.dynamic_index_in_dim(
                normed, lax.axis_index("tensor"), 1, keepdims=False
            )
            late.append(gather(jnp.where(is_first, up_rows, normed_rows)))
        in_grads.append(passed)
        gain_sum = gain_sum + g_gain
        shift_sum = shift_sum + g_shift
    late = late[::-1]

    column = lax.axis_index("dp") * (width // n_dp)
    slice_of = lambda x: lax.dynamic_slice_in_dim(x, column, width // n_dp, 1)
    total = None
    for index in range(count):
        now, then = cut(early, index), late[index]
        blocks = group * n_dp
        normed_all = jnp.where(is_first, now, then).reshape(blocks * rows, width)
        up_all = jnp.where(is_first, then, now).reshape(blocks * rows, width)
        segment = cut(all_segments, index).reshape(blocks, rows)
        tables = rotary_tables(segment)
        attended, kept = attention_forward(normed_all, segment, tables, proj_qkv, bias_qv)
        pieces = attention_backward(up_all, segment, tables, proj_dense, kept)
        pre_act = mm(normed_all, fc_one) + bias_fc
        activation = jax.nn.gelu(pre_act, approximate=True).astype(bf16)
        grad_pre = gelu_grad(pre_act, mm(up_all, fc_two, ((1,), (1,))))
        normed_part, up_part = slice_of(normed_all), slice_of(up_all)
        inner = ((0,), (0,))
        terms = [mm(normed_part, p.astype(bf16), inner) for p in pieces] + [
            mm(attended, up_part, inner),
            mm(normed_part, grad_pre.astype(bf16), inner),
            mm(activation, up_part, inner),
            jnp.sum(pieces[0], axis=0),
            jnp.sum(pieces[2], axis=0),
            jnp.sum(up_all.astype(f32), axis=0),
            jnp.sum(grad_pre, axis=0),
        ]
        total = terms if total is None else [a + b for a, b in zip(total, terms)]
    g_q, g_k, g_v, grad_dense, grad_fc_one, grad_fc_two, s_q, s_v, grad_out, grad_fc_bias = total
    norms = small_sum(jnp.concatenate([gain_sum, shift_sum], axis=0), ("dp", "tensor"), 4)

    layer_out = jnp.concatenate(
        [jnp.where(is_first, outputs[i], outputs[i + 1]) for i in range(count)], axis=0
    )
    in_grad = jnp.concatenate(
        [jnp.where(is_first, in_grads[count - i], in_grads[count - 1 - i]) for i in range(count)],
        axis=0,
    )
    return (
        layer_out[None],
        in_grad[None],
        norms[:1],
        norms[1:],
        jnp.stack([g_q, g_k, g_v])[None],
        jnp.stack([s_q, s_v])[None],
        grad_dense[None],
        grad_out[None],
        grad_fc_one[None],
        grad_fc_bias[None],
        grad_fc_two[None],
    )


def solution(mesh):
    return jax.shard_map(
        per_device,
        mesh=mesh,
        in_specs=(
            P(None, "dp", None),
            P(None, "dp", None),
            P(None, "dp"),
            P("section", None),
            P("section", None),
            P("section", None, None, "tensor"),
            P("section", None, "tensor"),
            P("section", "tensor", None),
            P("section", None),
            P("section", None, "tensor"),
            P("section", "tensor"),
            P("section", "tensor", None),
        ),
        out_specs=(
            P("section", None, ("dp", "tensor"), None),
            P("section", None, ("dp", "tensor"), None),
            P("section", None),
            P("section", None),
            P("section", None, "dp", "tensor"),
            P("section", None, "tensor"),
            P("section", "tensor", "dp"),
            P("section", None),
            P("section", "dp", "tensor"),
            P("section", "tensor"),
            P("section", "tensor", "dp"),
        ),
        check_vma=False,
    )
```

time: 1310 us -> 835 us (0.64)
  waiting for transfers between devices: 711 us -> 107 us
  local copies, waits for them, and re-layouts: 44.1 us -> 190 us
  Pallas kernels: 0 us -> 140 us
  matrix products: 366 us -> 298 us
  other arithmetic: 107 us -> 63.9 us
  starting transfers between devices: 27.7 us -> 0.12 us
    psum x9 -> x0, waiting for transfers between devices: 412 us -> none  [the longest x5 213 us: per_device(): mixture = lax.psum(partial_sum, 'tensor')]
    reduce_scatter x4 -> x0, waiting for transfers between devices: 291 us -> none  [the longest x1 144 us: per_device(): lax.psum_scatter(big_total[2].astype(jnp.bfloat16), 'dp', scatter_dimensi...]
    pallas_call x0 -> x7, Pallas kernels: none -> 140 us  [the longest x6 127 us: relay_call(): pl.pallas_call(functools.partial(kernel, n, last), out_shape=outs, in_spe...]
    all_gather x0 -> x3, waiting for transfers between devices: none -> 107 us  [gather(): return lax.all_gather(x, ('dp', 'tensor'), axis=1, tiled=True)]
    dot_general x120 -> x87, matrix products: 366 us -> 298 us  [the longest x57 261 us: mm(): lax.dot_general(left, right, (dims, ((), ())), preferred_element_type=jnp...]
    reshape x0 -> x27, local copies, waits for them, and re-layouts: none -> 57.3 us  [the longest x10 21.8 us: attention_forward(): (mm(normed, proj_qkv[2]) + bias_qv[1]).astype(jnp.bfloat16).reshape(shape)]
    unnamed x579 -> x369, local copies, waits for them, and re-layouts: 14.2 us -> 64.7 us
    ppermute x8 -> x0, starting transfers between devices: 26 us -> none  [from_behind(): return lax.ppermute(x, axis, pairs)]
  transfers between devices with their start and end apart: 21 -> 3, of which waited for: 16 -> 1; matrix products, arithmetic and copies ran while one was open for 18% -> 10% of each run, Pallas kernels for 0% -> 9%
where the time goes in v1:
time: 835 us; the launch traced here: 828 us
  matrix products  298 us (36%)
  local copies, waits for them, and re-layouts  190 us (23%)
  Pallas kernels  140 us (17%)
  waiting for transfers between devices  107 us (13%)
  other arithmetic  63.9 us (8%)
  between operations  16.4 us (2%)
  blocking collectives  12.7 us (2%)
    dot_general x57, matrix products, mm(): lax.dot_general(left, right, (dims, ((), ())), preferred_element_type=jnp...  261 us
    pallas_call x6, Pallas kernels, relay_call(): pl.pallas_call(functools.partial(kernel, n, last), out_shape=outs, in_spe...  127 us
    all_gather x3, waiting for transfers between devices, gather(): return lax.all_gather(x, ('dp', 'tensor'), axis=1, tiled=True)  107 us
    unnamed x369, local copies, waits for them, and re-layouts  64.7 us
    slice x20, local copies, waits for them, and re-layouts, rotate_pairs(): heads_in[..., ROT:]  22.1 us
    reshape x10, local copies, waits for them, and re-layouts, attention_forward(): (mm(normed, proj_qkv[2]) + bias_qv[1]).astype(jnp.bfloat16).reshape(shape)  21.8 us
    reshape x10, local copies, waits for them, and re-layouts, attention_backward(): mm(upstream, proj_dense, ((1,), (1,))).astype(jnp.bfloat16).reshape(shape)  21 us
  transfers between devices with their start and end apart: 3, of which 1 were waited for; matrix products, arithmetic and copies ran while one was open for 10% of the time, Pallas kernels for 9%

profile of v1, /device:TPU:0, one launch (start us, length us, event | category | flops | bytes accessed | tf_op | source)
XLA Modules:
  0.0 828.2 jit_solution(9953517947967929312)
XLA Ops:
  61.4 6.3 fusion.64
  71.2 17.7 %shard_map.203 = (bf16[2,32,2048]{2,1,0:T(8,128)(2,1)S(1)}, bf16[2,32,2048]{2,1,0:T(8,128)(2,1)S(1)}, bf16[2,4,32,2048]{3,2,1,0:T(8,128)(2,1)S(1)}) custom-call(bf16[2,4,32,2048]{3,2,1,0:T(8,128)(2,1)S(1)} %bitcast.503, bf16[2,32,2048]{2,1,0:T(8,128)(2,1)S(1)} %get-tuple-element.72.resid_ref.hidden_ref, f32[1,2048]{1,0:T(1,128)S(1)} %copy-done.23, ...), custom_call_target="tpu_custom_call" | custom-call | tf_op jit(solution)/shard_map/pallas_call | solution.py:307
  98.1 7.1 fusion.67
  131.6 23.1 %shard_map.204 = (bf16[2,32,2048]{2,1,0:T(8,128)(2,1)S(1)}, bf16[2,32,2048]{2,1,0:T(8,128)(2,1)S(1)}, bf16[2,4,32,2048]{3,2,1,0:T(8,128)(2,1)S(1)}) custom-call(bf16[2,4,32,2048]{3,2,1,0:T(8,128)(2,1)S(1)} %bitcast.504, bf16[2,32,2048]{2,1,0:T(8,128)(2,1)S(1)} %copy-done.13, f32[1,2048]{1,0:T(1,128)S(1)} %copy-done.23, f32[1,2048]{1,0:T(1,128)S(1)} %copy-done.16, ...), custom_call_target="tpu_custom_call" | custom-call | tf_op jit(solution)/shard_map/pallas_call | solution.py:307
  192.4 7.1 fusion.70
  206.5 13.5 %fusion.36 = f32[256,2048]{1,0:T(8,128)} fusion(bf16[1,2048,2048]{2,1,0:T(8,128)(2,1)} %param.21, f32[256,2048]{1,0:T(8,128)} %fusion.70, bf16[256,2048]{1,0:T(8,128)(2,1)} %bitcast.499, bf16[1,2048,2048]{2,1,0:T(8,128)(2,1)} %param.23), kind=kOutput, calls=%fused_computation.40 | convolution fusion | flops 4305453056 | bytes 22020096 | tf_op jit(solution)/shard_map/dot_general | solution.py:45
  228.1 27.4 %shard_map.206 = (bf16[2,32,2048]{2,1,0:T(8,128)(2,1)S(1)}, f32[1,2048]{1,0:T(1,128)S(1)}, f32[1,2048]{1,0:T(1,128)S(1)}, bf16[2,4,32,2048]{3,2,1,0:T(8,128)(2,1)S(1)}) custom-call(bf16[2,4,32,2048]{3,2,1,0:T(8,128)(2,1)S(1)} %bitcast.502, bf16[2,4,32,2048]{3,2,1,0:T(8,128)(2,1)S(1)} %bitcast.500, bf16[2,32,2048]{2,1,0:T(8,128)(2,1)S(1)} %copy-done.10, ...), custom_call_target="tpu_custom_call" | custom-call | tf_op jit(solution)/shard_map/pallas_call | solution.py:307
  272.3 13.1 %fusion.34 = f32[256,2048]{1,0:T(8,128)} fusion(bf16[1,2048,2048]{2,1,0:T(8,128)(2,1)} %param.21, f32[256,2048]{1,0:T(8,128)} %fusion.67, bf16[256,2048]{1,0:T(8,128)(2,1)S(1)} %bitcast.510, bf16[1,2048,2048]{2,1,0:T(8,128)(2,1)} %param.23), kind=kOutput, calls=%fused_computation.38 | convolution fusion | flops 4305453056 | bytes 22020096 | tf_op jit(solution)/shard_map/dot_general | solution.py:45
  293.6 35.2 %shard_map.207 = (bf16[2,32,2048]{2,1,0:T(8,128)(2,1)S(1)}, f32[1,2048]{1,0:T(1,128)S(1)}, f32[1,2048]{1,0:T(1,128)S(1)}, bf16[2,4,32,2048]{3,2,1,0:T(8,128)(2,1)S(1)}) custom-call(bf16[2,4,32,2048]{3,2,1,0:T(8,128)(2,1)S(1)} %bitcast.501, bf16[2,4,32,2048]{3,2,1,0:T(8,128)(2,1)S(1)} %copy-done.8, bf16[2,32,2048]{2,1,0:T(8,128)(2,1)S(1)} %copy-done.14, ...), custom_call_target="tpu_custom_call" | custom-call | tf_op jit(solution)/shard_map/pallas_call | solution.py:307
  333.5 12.7 %all-gather.1 = s32[4,512]{1,0:T(4,128)S(1)} all-gather(s32[4,128]{1,0:T(4,128)S(1)} %copy-done.140), channel_id=3, replica_groups=mesh['section'=2,'dp'=4,'tensor'=4] {'dp'}, dimensions={1}, use_global_device_ids=true | all-gather | bytes 10240 | tf_op jit(solution)/shard_map/all_gather | solution.py:414
  356.1 9.4 %shard_map.205 = bf16[2,32,2048]{2,1,0:T(8,128)(2,1)S(1)} custom-call(bf16[2,4,32,2048]{3,2,1,0:T(8,128)(2,1)S(1)} %bitcast.506, bf16[2,32,2048]{2,1,0:T(8,128)(2,1)S(1)} %copy-done.11, f32[1,2048]{1,0:T(1,128)S(1)} %copy-done.23, f32[1,2048]{1,0:T(1,128)S(1)} %copy-done.16, f32[1,2048]{1,0:T(1,128)S(1)} %copy-done.22), custom_call_target="tpu_custom_call" | custom-call | tf_op jit(solution)/shard_map/pallas_call | solution.py:307
  378.6 13.3 %fusion.32 = f32[256,2048]{1,0:T(8,128)} fusion(bf16[1,2048,2048]{2,1,0:T(8,128)(2,1)} %param.21, f32[256,2048]{1,0:T(8,128)} %copy-done.161, bf16[256,2048]{1,0:T(8,128)(2,1)S(1)} %bitcast.508, bf16[1,2048,2048]{2,1,0:T(8,128)(2,1)} %param.23), kind=kOutput, calls=%fused_computation.36 | convolution fusion | flops 4305453056 | bytes 22020096 | tf_op jit(solution)/shard_map/dot_general | solution.py:45
  399.9 14.6 %shard_map.208 = (bf16[2,32,2048]{2,1,0:T(8,128)(2,1)S(1)}, f32[1,2048]{1,0:T(1,128)S(1)}, f32[1,2048]{1,0:T(1,128)S(1)}) custom-call(bf16[2,4,32,2048]{3,2,1,0:T(8,128)(2,1)S(1)} %bitcast.505, bf16[2,4,32,2048]{3,2,1,0:T(8,128)(2,1)S(1)} %get-tuple-element.35.up_ref, bf16[2,32,2048]{2,1,0:T(8,128)(2,1)S(1)} %get-tuple-element.72.resid_ref.hidden_ref, ...), custom_call_target="tpu_custom_call" | custom-call | tf_op jit(solution)/shard_map/pallas_call | solution.py:307
  415.8 12.2 %shard_map.209 = f32[2,2048]{1,0:T(2,128)} custom-call(f32[2,2048]{1,0:T(2,128)} %pad_maximum_fusion.40.x_ref), custom_call_target="tpu_custom_call" | custom-call | tf_op jit(solution)/shard_map/pallas_call | solution.py:366
  433.3 106.7 %all-gather.7.cloned.1.call-done = bf16[4,512,2048]{2,1,0:T(8,128)(2,1)} async-done(((bf16[4,32,2048]{2,1,0:T(8,128)(2,1)}), bf16[4,512,2048]{2,1,0:T(8,128)(2,1)}) %all-gather.7.cloned.1.call-update) | async-done | bytes 8388624 | tf_op jit(solution)/shard_map/all_gather | solution.py:417
  540.0 6.3 bitcast_select_fusion.1
  546.3 6.6 add_convert_fusion.1
  593.8 8.4 %convert_reduce_fusion = (f32[2048]{0:T(1024)}, bf16[2,512,2048]{2,1,0:T(8,128)(2,1)}, f32[2048]{0:T(1024)}, bf16[2,512,2048]{2,1,0:T(8,128)(2,1)S(1)}) fusion(bf16[4,512,2048]{2,1,0:T(8,128)(2,1)S(1)} %bitcast.528, bf16[2,1,512,2048]{3,2,0,1:T(8,128)(2,1)S(1)} %copy-done.38, pred[]{:T(512)S(6)} %eq.67, bf16[2,1,512,2048]{3,2,1,0:T(8,128)(2,1)} %all-gather.9.cloned.1.call-done), kind=kLoop, calls=%fused_computation.50 | loop fusion | flops 12578816 | bytes 25182208 | tf_op jit(solution)/shard_map/reduce_sum | solution.py:521
  704.6 11.3 %fusion.30 = f32[1024,2048]{1,0:T(8,128)} fusion(bf16[1024,2048]{1,0:T(8,128)(2,1)S(1)} %bitcast.543, bf16[1,2048,2048]{2,1,0:T(8,128)(2,1)S(1)} %bitcast.600), kind=kOutput, calls=%fused_computation.34 | convolution fusion | flops 8589934592 | bytes 20971520 | tf_op jit(solution)/shard_map/dot_general | solution.py:45
  715.9 11.1 %fusion.28 = f32[1024,2048]{1,0:T(8,128)} fusion(bf16[1024,2048]{1,0:T(8,128)(2,1)S(1)} %bitcast.532, bf16[1,2048,2048]{2,1,0:T(8,128)(2,1)S(1)} %bitcast.600), kind=kOutput, calls=%fused_computation.32 | convolution fusion | flops 8589934592 | bytes 20971520 | tf_op jit(solution)/shard_map/dot_general | solution.py:45
  727.7 20.2 %fusion.427 = (f32[2048]{0:T(1024)S(1)}, bf16[1024,2048]{1,0:T(8,128)(2,1)}) fusion(f32[1024,2048]{1,0:T(8,128)} %fusion.30, f32[2048]{0:T(1024)S(1)} %bitcast.606, bf16[1024,2048]{1,0:T(8,128)(2,1)S(1)} %bitcast.550, bf16[1,2048,2048]{2,1,0:T(8,128)(2,1)} %param.23), kind=kOutput, calls=%fused_computation.578 | convolution fusion | flops 8636069888 | bytes 25182208 | tf_op jit(solution)/shard_map/dot_general | solution.py:45
  748.0 9.7 %fusion.58 = f32[2048,512]{1,0:T(8,128)} fusion(f32[1024,2048]{1,0:T(8,128)} %fusion.30, f32[2048]{0:T(1024)S(1)} %bitcast.607, bf16[1024,2048]{1,0:T(8,128)(2,1)S(1)} %bitcast.551, s32[]{:T(128)S(6)} %select_n.179), kind=kOutput, calls=%fused_computation.80 | convolution fusion | flops 2168455168 | bytes 13639684 | tf_op jit(solution)/shard_map/dot_general | solution.py:45
  775.7 17.7 %fusion.428 = (f32[2048]{0:T(1024)S(1)}, bf16[1024,2048]{1,0:T(8,128)(2,1)S(1)}) fusion(f32[1024,2048]{1,0:T(8,128)} %fusion.28, f32[2048]{0:T(1024)S(1)} %bitcast.608, bf16[1024,2048]{1,0:T(8,128)(2,1)S(1)} %bitcast.546, bf16[1,2048,2048]{2,1,0:T(8,128)(2,1)} %param.23), kind=kOutput, calls=%fused_computation.579 | convolution fusion | flops 8636069888 | bytes 25182208 | tf_op jit(solution)/shard_map/dot_general | solution.py:45
  793.4 10.4 %add_bitcast_fusion = f32[1,2048,512]{2,1,0:T(8,128)} fusion(f32[2048,512]{1,0:T(8,128)S(1)} %copy-done.164, f32[1024,2048]{1,0:T(8,128)} %fusion.28, f32[2048]{0:T(1024)S(1)} %bitcast.609, bf16[1024,2048]{1,0:T(8,128)(2,1)S(1)} %bitcast.547, s32[]{:T(128)S(6)} %select_n.179), kind=kOutput, calls=%fused_computation.64 | convolution fusion | flops 2169503744 | bytes 17833988 | tf_op jit(solution)/shard_map/dot_general | solution.py:45
  (620 shorter events, 390.5 us)
Async XLA Ops:
  7.2 63.2 %copy-start = (bf16[1,512,2048]{2,1,0:T(8,128)(2,1)S(1)}, bf16[1,512,2048]{2,1,0:T(8,128)(2,1)}, u32[]{:S(2)}) copy-start(bf16[1,512,2048]{2,1,0:T(8,128)(2,1)} %param.19) | copy-start | bytes 6291460
  7.2 426.1 %all-gather.11.cloned.1.call-start = ((), (), s32[]{:S(2)}) async-start(), calls=%async_computation.2 | async-start | bytes 4456448 | tf_op jit(solution)/shard_map/all_gather | solution.py:417
  7.3 24.7 %copy-start.144 = (pred[128]{0:T(512)(128)(4,1)}, pred[128]{0:T(512)(128)(4,1)S(1)}, u32[]{:S(2)}) copy-start(pred[128]{0:T(512)(128)(4,1)S(1)} %iota_compare_fusion.1) | copy-start | bytes 388
  14.1 27.4 %copy-start.153 = (f32[1,1,512]{2,1,0:T(1,128)}, f32[1,1,512]{2,1,0:T(1,128)S(1)}, u32[]{:S(2)}) copy-start(f32[1,1,512]{2,1,0:T(1,128)S(1)} %get-tuple-element.149) | copy-start | bytes 6148
  46.2 11.8 %copy-start.60 = (bf16[2,128,8,64]{1,3,2,0:T(8,128)(2,1)}, bf16[2,128,8,64]{1,3,2,0:T(8,128)(2,1)S(1)}, u32[]{:S(2)}) copy-start(bf16[2,128,8,64]{1,3,2,0:T(8,128)(2,1)S(1)} %copy.82) | copy-start | bytes 786436
  61.4 27.6 %slice-start = ((s8[6291456]{0:T(1024)(128)(4,1)}), s8[4194304]{0:T(1024)(128)(4,1)S(1)}, s32[]{:S(2)}) async-start(s8[6291456]{0:T(1024)(128)(4,1)} %bitcast.521), calls=%async_computation.3 | async-start | bytes 8388608
  67.7 21.2 %slice-start.1 = ((s8[6291456]{0:T(1024)(128)(4,1)}), s8[2097152]{0:T(1024)(128)(4,1)S(1)}, s32[]{:S(2)}) async-start(s8[6291456]{0:T(1024)(128)(4,1)} %bitcast.521), calls=%async_computation.4 | async-start | bytes 4194304
  71.1 17.8 %copy-start.154 = (f32[1,1,512]{2,1,0:T(1,128)S(1)}, f32[1,1,512]{2,1,0:T(1,128)}, u32[]{:S(2)}) copy-start(f32[1,1,512]{2,1,0:T(1,128)} %copy-done.153) | copy-start | bytes 6148
  123.4 31.4 %slice-start.2 = ((s8[6291456]{0:T(1024)(128)(4,1)}), s8[4194304]{0:T(1024)(128)(4,1)S(1)}, s32[]{:S(2)}) async-start(s8[6291456]{0:T(1024)(128)(4,1)} %bitcast.523), calls=%async_computation.5 | async-start | bytes 8388608
  124.4 30.4 %slice-start.3 = ((s8[6291456]{0:T(1024)(128)(4,1)}), s8[2097152]{0:T(1024)(128)(4,1)S(1)}, s32[]{:S(2)}) async-start(s8[6291456]{0:T(1024)(128)(4,1)} %bitcast.523), calls=%async_computation.6 | async-start | bytes 4194304
  131.4 23.5 %copy-start.155 = (f32[1,1,512]{2,1,0:T(1,128)S(1)}, f32[1,1,512]{2,1,0:T(1,128)}, u32[]{:S(2)}) copy-start(f32[1,1,512]{2,1,0:T(1,128)} %copy-done.153) | copy-start | bytes 6148
  259.0 174.2 %all-gather.9.cloned.1.call-start = ((), (), s32[]{:S(2)}) async-start(), calls=%async_computation.1 | async-start | bytes 4456448 | tf_op jit(solution)/shard_map/all_gather | solution.py:417
  329.5 16.7 %copy-start.145 = (pred[128]{0:T(512)(128)(4,1)S(1)}, pred[128]{0:T(512)(128)(4,1)}, u32[]{:S(2)}) copy-start(pred[128]{0:T(512)(128)(4,1)} %copy-done.144) | copy-start | bytes 388
  331.3 208.7 %all-gather.7.cloned.1.call-start = ((), (), s32[]{:S(2)}) async-start(), calls=%async_computation | async-start | bytes 8912896 | tf_op jit(solution)/shard_map/all_gather | solution.py:417
  399.8 28.2 %copy-start.133 = (pred[128,128]{0,1:T(8,128)(4,1)S(1)}, pred[128,128]{0,1:T(8,128)(4,1)}, u32[]{:S(2)}) copy-start(pred[128,128]{0,1:T(8,128)(4,1)} %iota_compare_fusion) | copy-start | bytes 49156
  399.8 28.6 %copy-start.148 = (f32[16]{0:T(128)S(1)}, f32[16]{0:T(128)}, u32[]{:S(2)}) copy-start(f32[16]{0:T(128)} %multiply_power_fusion) | copy-start | bytes 196
  433.2 113.1 %copy-start.156 = (f32[1,1,512]{2,1,0:T(1,128)S(1)}, f32[1,1,512]{2,1,0:T(1,128)}, u32[]{:S(2)}) copy-start(f32[1,1,512]{2,1,0:T(1,128)} %copy-done.153) | copy-start | bytes 6148
  546.3 15.3 %copy-start.42 = (bf16[2,512,2048]{2,1,0:T(8,128)(2,1)}, bf16[2,512,2048]{2,1,0:T(8,128)(2,1)S(1)}, u32[]{:S(2)}) copy-start(bf16[2,512,2048]{2,1,0:T(8,128)(2,1)S(1)} %get-tuple-element.49) | copy-start | bytes 12582916
  546.3 12.0 %slice-start.4 = ((s8[6291456]{0:T(1024)(128)(4,1)}), s8[4194304]{0:T(1024)(128)(4,1)S(1)}, s32[]{:S(2)}) async-start(s8[6291456]{0:T(1024)(128)(4,1)} %bitcast.525), calls=%async_computation.7 | async-start | bytes 8388608
  704.6 11.3 %copy-start.43 = (bf16[2,512,2048]{2,1,0:T(8,128)(2,1)S(1)}, bf16[2,512,2048]{2,1,0:T(8,128)(2,1)}, u32[]{:S(2)}) copy-start(bf16[2,512,2048]{2,1,0:T(8,128)(2,1)} %copy-done.42) | copy-start | bytes 12582916
  715.9 11.1 %copy-start.90 = (bf16[8,128,8,64]{1,3,2,0:T(8,128)(2,1)S(1)}, bf16[8,128,8,64]{1,3,2,0:T(8,128)(2,1)}, u32[]{:S(2)}) copy-start(bf16[8,128,8,64]{1,3,2,0:T(8,128)(2,1)} %fusion.170) | copy-start | bytes 3145732
  715.9 11.8 %copy-start.54 = (bf16[2,512,2048]{2,1,0:T(8,128)(2,1)S(1)}, bf16[2,512,2048]{2,1,0:T(8,128)(2,1)}, u32[]{:S(2)}) copy-start(bf16[2,512,2048]{2,1,0:T(8,128)(2,1)} %copy-done.53) | copy-start | bytes 12582916
  775.7 17.7 %copy-start.164 = (f32[2048,512]{1,0:T(8,128)S(1)}, f32[2048,512]{1,0:T(8,128)}, u32[]{:S(2)}) copy-start(f32[2048,512]{1,0:T(8,128)} %fusion.58) | copy-start | bytes 12582916
  793.4 10.4 %copy-start.44 = (bf16[2,512,2048]{2,1,0:T(8,128)(2,1)S(1)}, bf16[2,512,2048]{2,1,0:T(8,128)(2,1)}, u32[]{:S(2)}) copy-start(bf16[2,512,2048]{2,1,0:T(8,128)(2,1)} %copy-done.42) | copy-start | bytes 12582916
  (156 other events, 421.6 us)
Sparse Core Ops, SparseCore 0:
  259.1 81.5 all-gather.10
  343.5 81.3 all-gather.8
  428.3 111.6 all-gather.6

commit v2 on v1

--- a/solution.py
+++ b/solution.py
@@ -16,7 +16,7 @@
 
 
 def rotary_tables(segment):
-    length = segment.shape[-1]
+    blocks, length = segment.shape
     row_index = jnp.arange(length, dtype=jnp.int32)[None, :]
     previous = jnp.concatenate([segment[:, :1], segment[:, :-1]], axis=1)
     starts = jnp.where((row_index == 0) | (segment != previous), row_index, 0)
@@ -24,37 +24,159 @@
     half_rot = ROT // 2
     frequency = 10000.0 ** (-2.0 * jnp.arange(half_rot, dtype=jnp.float32) / ROT)
     phase_angle = position[..., None] * frequency
-    return (jnp.cos(phase_angle)[:, :, None, :], jnp.sin(phase_angle)[:, :, None, :])
-
-
-def rotate_pairs(heads_in, cos_part, sin_part):
-    half_rot = ROT // 2
-    lower_half = heads_in[..., :half_rot]
-    upper_half = heads_in[..., half_rot:ROT]
-    return jnp.concatenate(
-        [
-            lower_half * cos_part - upper_half * sin_part,
-            upper_half * cos_part + lower_half * sin_part,
-            heads_in[..., ROT:],
-        ],
-        axis=-1,
-    )
-
-
-def mm(left, right, dims=((1,), (0,))):
-    return lax.dot_general(left, right, (dims, ((), ())), preferred_element_type=jnp.float32)
-
-
-def score_blocks(queries, key_rows, segment):
+    cos_part, sin_part = jnp.cos(phase_angle), jnp.sin(phase_angle)
+    none = jnp.zeros((blocks, length, half_rot), jnp.float32)
+    rest = jnp.ones((blocks, length, HEAD_DIM - ROT), jnp.float32)
+    straight = jnp.concatenate([cos_part, cos_part, rest], axis=-1)
+    from_upper = jnp.concatenate([-sin_part, none, 0.0 * rest], axis=-1)
+    from_lower = jnp.concatenate([none, sin_part, 0.0 * rest], axis=-1)
+    tables = jnp.stack([straight, from_upper, from_lower], axis=1)
+    return jnp.concatenate([tables, tables], axis=-1)
+
+
+def allowed_of(segment):
     length = segment.shape[-1]
     row_index = jnp.arange(length, dtype=jnp.int32)
     allowed = (segment[:, :, None] == segment[:, None, :]) & (
         row_index[None, :] <= row_index[:, None]
     )
-    scores = jnp.einsum(
-        "bqhd,bkhd->bhqk", queries, key_rows, preferred_element_type=jnp.float32
-    ) * HEAD_DIM ** (-0.5)
-    return jnp.where(allowed[:, None, :, :], scores, MASKED)
+    return allowed.astype(jnp.float32)
+
+
+def mm(left, right, dims=((1,), (0,))):
+    return lax.dot_general(left, right, (dims, ((), ())), preferred_element_type=jnp.float32)
+
+
+def rotated(x, table, sign):
+    half, lanes = ROT // 2, x.shape[-1]
+    return (
+        x * table[0]
+        + pltpu.roll(x, lanes - half, 1) * (sign * table[1])
+        + pltpu.roll(x, half, 1) * (sign * table[2])
+    )
+
+
+def softmax_of(query, key, allowed):
+    scores = mm(query, key, ((1,), (1,))) * HEAD_DIM ** (-0.5)
+    scores = jnp.where(allowed, scores, MASKED)
+    row_max = jnp.max(scores, axis=-1, keepdims=True)
+    log_total = row_max + jnp.log(jnp.sum(jnp.exp(scores - row_max), axis=-1, keepdims=True))
+    return jnp.exp(scores - log_total)
+
+
+def lane_masks(lanes):
+    lane = lax.broadcasted_iota(jnp.int32, (1, lanes), 1)
+    return [
+        jnp.where(lane // HEAD_DIM == h, 1.0, 0.0).astype(jnp.bfloat16)
+        for h in range(lanes // HEAD_DIM)
+    ]
+
+
+def attention_forward_kernel(qf_ref, kf_ref, vf_ref, table_ref, allowed_ref, q_ref, k_ref, v_ref, out_ref):
+    bf16 = jnp.bfloat16
+    table = table_ref[0]
+    lanes = table.shape[-1]
+    allowed = allowed_ref[0] > 0.5
+    masks = lane_masks(lanes)
+    v_ref[...] = vf_ref[...].astype(bf16)
+    for pair in range(qf_ref.shape[-1] // lanes):
+        at = slice(pair * lanes, (pair + 1) * lanes)
+        query = rotated(qf_ref[:, at], table, 1.0).astype(bf16)
+        key = rotated(kf_ref[:, at], table, 1.0).astype(bf16)
+        q_ref[:, at] = query
+        k_ref[:, at] = key
+        value = v_ref[:, at]
+        total = 0.0
+        for mask in masks:
+            prob = softmax_of(query * mask, key, allowed).astype(bf16)
+            total = total + mm(prob, value * mask)
+        out_ref[:, at] = total.astype(bf16)
+
+
+def attention_backward_kernel(again, q_ref, k_ref, v_ref, ga_ref, table_ref, allowed_ref, *outs):
+    bf16 = jnp.bfloat16
+    table = table_ref[0]
+    lanes = table.shape[-1]
+    allowed = allowed_ref[0] > 0.5
+    masks = lane_masks(lanes)
+    scale = HEAD_DIM ** (-0.5)
+    if again:
+        gq_ref, gk_ref, gv_ref, out_ref, sq_ref, sv_ref = outs
+
+        @pl.when(pl.program_id(0) == 0)
+        def _():
+            sq_ref[...] = jnp.zeros_like(sq_ref)
+            sv_ref[...] = jnp.zeros_like(sv_ref)
+    else:
+        gq_ref, gk_ref, gv_ref = outs
+    for pair in range(q_ref.shape[-1] // lanes):
+        at = slice(pair * lanes, (pair + 1) * lanes)
+        if again:
+            query = rotated(q_ref[:, at], table, 1.0).astype(bf16)
+            key = rotated(k_ref[:, at], table, 1.0).astype(bf16)
+            value = v_ref[:, at].astype(bf16)
+        else:
+            query, key, value = q_ref[:, at], k_ref[:, at], v_ref[:, at]
+        grad = ga_ref[:, at]
+        total = g_query = g_key = g_value = 0.0
+        for mask in masks:
+            prob_f = softmax_of(query * mask, key, allowed)
+            prob_b = prob_f.astype(bf16)
+            grad_m = grad * mask
+            grad_prob = mm(grad_m, value, ((1,), (1,)))
+            row_dot = jnp.sum(prob_f * grad_prob, axis=-1, keepdims=True)
+            grad_score = (prob_f * (grad_prob - row_dot)).astype(bf16)
+            if again:
+                total = total + mm(prob_b, value * mask)
+            g_query = g_query + mm(grad_score, key * mask)
+            g_key = g_key + mm(grad_score, query * mask, ((0,), (0,)))
+            g_value = g_value + mm(prob_b, grad_m, ((0,), (0,)))
+        g_query = rotated(g_query * scale, table, -1.0)
+        g_key = rotated(g_key * scale, table, -1.0)
+        gq_ref[:, at] = g_query.astype(bf16)
+        gk_ref[:, at] = g_key.astype(bf16)
+        gv_ref[:, at] = g_value.astype(bf16)
+        if again:
+            out_ref[:, at] = total.astype(bf16)
+            sq_ref[:, at] += jnp.sum(g_query, axis=0, keepdims=True)
+            sv_ref[:, at] += jnp.sum(g_value, axis=0, keepdims=True)
+
+
+def attention_call(kernel, arrays, tables, allowed, outs, sums):
+    blocks, _, rows, lanes = tables.shape
+    features = arrays[0].shape[-1]
+    block = pl.BlockSpec((rows, features), lambda i: (i, 0))
+    one = pl.BlockSpec((1, features), lambda i: (0, 0))
+    flat = (blocks * rows, features)
+    return pl.pallas_call(
+        kernel,
+        grid=(blocks,),
+        in_specs=[block] * len(arrays)
+        + [
+            pl.BlockSpec((1, 3, rows, lanes), lambda i: (i, 0, 0, 0)),
+            pl.BlockSpec((1, rows, rows), lambda i: (i, 0, 0)),
+        ],
+        out_specs=[block] * outs + [one] * sums,
+        out_shape=[jax.ShapeDtypeStruct(flat, jnp.bfloat16)] * outs
+        + [jax.ShapeDtypeStruct((1, features), jnp.float32)] * sums,
+        cost_estimate=pl.CostEstimate(
+            flops=20 * blocks * rows * rows * features,
+            bytes_accessed=blocks * rows * features * 16,
+            transcendentals=0,
+        ),
+    )(*arrays, tables, allowed)
+
+
+def projections(normed, proj_qkv, bias_qv):
+    return [
+        mm(normed, proj_qkv[0]) + bias_qv[0],
+        mm(normed, proj_qkv[1]),
+        mm(normed, proj_qkv[2]) + bias_qv[1],
+    ]
+
+
+def settled(x):
+    return lax.optimization_barrier(x)
 
 
 def gelu_grad(pre_act, grad_act):
@@ -67,61 +189,6 @@
     centred = residual - jnp.mean(residual, axis=-1, keepdims=True)
     inv_std = lax.rsqrt(jnp.mean(centred * centred, axis=-1, keepdims=True) + NORM_EPS)
     return (centred * inv_std * norm_gain + norm_shift).astype(jnp.bfloat16)
-
-
-def attention_forward(normed, segment, tables, proj_qkv, bias_qv):
-    blocks, rows = segment.shape
-    heads = proj_qkv.shape[-1] // HEAD_DIM
-    shape = (blocks, rows, heads, HEAD_DIM)
-    cos_part, sin_part = tables
-    query_f = (mm(normed, proj_qkv[0]) + bias_qv[0]).reshape(shape)
-    key_f = mm(normed, proj_qkv[1]).reshape(shape)
-    values = (mm(normed, proj_qkv[2]) + bias_qv[1]).astype(jnp.bfloat16).reshape(shape)
-    queries = rotate_pairs(query_f, cos_part, sin_part).astype(jnp.bfloat16)
-    key_rows = rotate_pairs(key_f, cos_part, sin_part).astype(jnp.bfloat16)
-    scores = score_blocks(queries, key_rows, segment)
-    row_max = jnp.max(scores, axis=-1, keepdims=True)
-    log_total = row_max + jnp.log(jnp.sum(jnp.exp(scores - row_max), axis=-1, keepdims=True))
-    prob_f = jnp.exp(scores - log_total)
-    attended = (
-        jnp.einsum(
-            "bhqk,bkhd->bqhd", prob_f.astype(jnp.bfloat16), values,
-            preferred_element_type=jnp.float32,
-        )
-        .astype(jnp.bfloat16)
-        .reshape(blocks * rows, heads * HEAD_DIM)
-    )
-    return attended, (queries, key_rows, values, log_total)
-
-
-def attention_backward(upstream, segment, tables, proj_dense, kept):
-    queries, key_rows, values, log_total = kept
-    shape = queries.shape
-    flat = (shape[0] * shape[1], shape[2] * shape[3])
-    cos_part, sin_part = tables
-    grad_att = mm(upstream, proj_dense, ((1,), (1,))).astype(jnp.bfloat16).reshape(shape)
-    prob_f = jnp.exp(score_blocks(queries, key_rows, segment) - log_total)
-    prob_b = prob_f.astype(jnp.bfloat16)
-    grad_prob = jnp.einsum("bqhd,bkhd->bhqk", grad_att, values, preferred_element_type=jnp.float32)
-    row_dot = jnp.sum(prob_f * grad_prob, axis=-1, keepdims=True)
-    grad_score = (prob_f * (grad_prob - row_dot)).astype(jnp.bfloat16)
-    scale = HEAD_DIM ** (-0.5)
-    grad_query = rotate_pairs(
-        jnp.einsum("bhqk,bkhd->bqhd", grad_score, key_rows, preferred_element_type=jnp.float32)
-        * scale,
-        cos_part,
-        -sin_part,
-    ).reshape(flat)
-    grad_key = rotate_pairs(
-        jnp.einsum("bhqk,bqhd->bkhd", grad_score, queries, preferred_element_type=jnp.float32)
-        * scale,
-        cos_part,
-        -sin_part,
-    ).reshape(flat)
-    grad_value = jnp.einsum(
-        "bhqk,bqhd->bkhd", prob_b, grad_att, preferred_element_type=jnp.float32
-    ).reshape(flat)
-    return grad_query, grad_key, grad_value
 
 
 def partner(t, k):
@@ -316,23 +383,23 @@
     )(*args)
 
 
-def small_kernel(axes, x_ref, out_ref, gathered, send_sem, recv_sem):
+def exchange_kernel(axes, add, x_ref, out_ref, *rest):
+    gathered, send_sem, recv_sem = rest if add else (out_ref,) + rest
     sizes = [lax.axis_size(a) for a in axes]
     index = [lax.axis_index(a) for a in axes]
     count = 1
-    for s in sizes:
+    mine = 0
+    for s, i in zip(sizes, index):
         count *= s
+        mine = mine * s + i
 
     def shifted(k):
-        ids, parts = {}, []
+        ids = {}
         for a, s, i in zip(reversed(axes), reversed(sizes), reversed(index)):
             ids[a] = lax.rem(i + k % s, s)
             k //= s
         return ids
 
-    mine = 0
-    for s, i in zip(sizes, index):
-        mine = mine * s + i
     barrier = pltpu.get_barrier_semaphore()
     for k in range(1, count):
         pl.semaphore_signal(barrier, inc=1, device_id=shifted(k), device_id_type=MESH)
@@ -352,27 +419,26 @@
     gathered[mine] = x_ref[...]
     for copy in copies:
         copy.wait()
-    total = gathered[0]
-    for i in range(1, count):
-        total = total + gathered[i]
-    out_ref[...] = total
-
-
-def small_sum(x, axes, ident):
+    if add:
+        total = gathered[0]
+        for i in range(1, count):
+            total = total + gathered[i]
+        out_ref[...] = total
+
+
+def small_exchange(x, axes, ident, add):
     count = 1
     for a in axes:
         count *= lax.axis_size(a)
     vmem = pl.BlockSpec(memory_space=pltpu.VMEM)
+    stacked = (count,) + x.shape
     return pl.pallas_call(
-        functools.partial(small_kernel, axes),
-        out_shape=jax.ShapeDtypeStruct(x.shape, x.dtype),
+        functools.partial(exchange_kernel, axes, add),
+        out_shape=jax.ShapeDtypeStruct(x.shape if add else stacked, x.dtype),
         in_specs=[vmem],
         out_specs=vmem,
-        scratch_shapes=[
-            pltpu.VMEM((count,) + x.shape, x.dtype),
-            pltpu.SemaphoreType.DMA((count,)),
-            pltpu.SemaphoreType.DMA((count,)),
-        ],
+        scratch_shapes=([pltpu.VMEM(stacked, x.dtype)] if add else [])
+        + [pltpu.SemaphoreType.DMA((count,)), pltpu.SemaphoreType.DMA((count,))],
         compiler_params=pltpu.CompilerParams(collective_id=ident, has_side_effects=True),
     )(x)
 
@@ -411,7 +477,7 @@
     own_rows = lambda x: lax.dynamic_slice_in_dim(x, row_start, share, 1)
     first_normed = normalize(block_input, norm_gain, norm_shift)
     x_rows = own_rows(block_input)
-    all_segments = lax.all_gather(segments, "dp", axis=1)
+    all_segments = small_exchange(segments, ("dp",), 5, False)
 
     def gather(x):
         return lax.all_gather(x, ("dp", "tensor"), axis=1, tiled=True)
@@ -429,15 +495,20 @@
     stored, outputs = [], []
     for moment in range(count + 1):
         last = moment == count
+        if last:
+            normed, early = settled((normed, early))
         segment = jnp.where(
             is_first, cut(segments, min(moment, count - 1)), cut(segments, max(moment - 1, 0))
         )
-        tables = rotary_tables(segment)
-        attended, kept = attention_forward(flat(normed), segment, tables, proj_qkv, bias_qv)
+        tables, allowed = rotary_tables(segment), allowed_of(segment)
+        *kept, attended = attention_call(
+            attention_forward_kernel,
+            projections(flat(normed), proj_qkv, bias_qv), tables, allowed, 4, 0,
+        )
         pre_act = mm(flat(normed), fc_one) + bias_fc
-        activation = jax.nn.gelu(pre_act, approximate=True).astype(bf16)
+        activation = settled(jax.nn.gelu(pre_act, approximate=True).astype(bf16))
         partial = (mm(attended, proj_dense) + mm(activation, fc_two)).astype(bf16)
-        stored.append((segment, tables, hidden, normed, kept, pre_act))
+        stored.append((tables, allowed, hidden, normed, kept, pre_act))
         args = [four(partial), hidden, out_bias, norm_gain, norm_shift]
         if last:
             (out,) = relay_call(
@@ -460,14 +531,20 @@
     shift_sum = jnp.zeros((1, width), f32)
     for moment in range(count + 1):
         last = moment == count
-        segment, tables, hidden, normed, kept, pre_act = stored[count - moment]
+        tables, allowed, hidden, normed, kept, pre_act = stored[count - moment]
         up_flat = flat(up)
-        grad_pre = gelu_grad(pre_act, mm(up_flat, fc_two, ((1,), (1,)))).astype(bf16)
-        pieces = attention_backward(up_flat, segment, tables, proj_dense, kept)
+        grad_pre = settled(
+            gelu_grad(pre_act, mm(up_flat, fc_two, ((1,), (1,)))).astype(bf16)
+        )
+        grad_att = mm(up_flat, proj_dense, ((1,), (1,))).astype(bf16)
+        pieces = attention_call(
+            functools.partial(attention_backward_kernel, False),
+            kept + [grad_att], tables, allowed, 3, 0,
+        )
         grad_normed = mm(grad_pre, fc_one, ((1,), (1,)))
         for which in range(3):
             grad_normed = grad_normed + mm(
-                pieces[which].astype(bf16), proj_qkv[which], ((1,), (1,))
+                pieces[which], proj_qkv[which], ((1,), (1,))
             )
         args = [four(grad_normed.astype(bf16)), up, hidden, norm_gain]
         outs = [sds(rows_shape, bf16), sds((1, width), f32), sds((1, width), f32)]
@@ -501,29 +578,37 @@
     for index in range(count):
         now, then = cut(early, index), late[index]
         blocks = group * n_dp
-        normed_all = jnp.where(is_first, now, then).reshape(blocks * rows, width)
-        up_all = jnp.where(is_first, then, now).reshape(blocks * rows, width)
-        segment = cut(all_segments, index).reshape(blocks, rows)
-        tables = rotary_tables(segment)
-        attended, kept = attention_forward(normed_all, segment, tables, proj_qkv, bias_qv)
-        pieces = attention_backward(up_all, segment, tables, proj_dense, kept)
+        normed_all = settled(jnp.where(is_first, now, then).reshape(blocks * rows, width))
+        up_all = settled(jnp.where(is_first, then, now).reshape(blocks * rows, width))
+        segment = all_segments[:, index * group : (index + 1) * group]
+        segment = jnp.swapaxes(segment, 0, 1).reshape(blocks, rows)
+        tables, allowed = rotary_tables(segment), allowed_of(segment)
+        grad_att = mm(up_all, proj_dense, ((1,), (1,))).astype(bf16)
+        *pieces, attended, s_q, s_v = attention_call(
+            functools.partial(attention_backward_kernel, True),
+            projections(normed_all, proj_qkv, bias_qv) + [grad_att], tables, allowed, 4, 2,
+        )
         pre_act = mm(normed_all, fc_one) + bias_fc
-        activation = jax.nn.gelu(pre_act, approximate=True).astype(bf16)
+        activation = settled(jax.nn.gelu(pre_act, approximate=True).astype(bf16))
         grad_pre = gelu_grad(pre_act, mm(up_all, fc_two, ((1,), (1,))))
+        grad_fc_bias = jnp.sum(grad_pre, axis=0)
+        grad_pre, grad_fc_bias = settled((grad_pre.astype(bf16), grad_fc_bias))
         normed_part, up_part = slice_of(normed_all), slice_of(up_all)
         inner = ((0,), (0,))
-        terms = [mm(normed_part, p.astype(bf16), inner) for p in pieces] + [
+        terms = [mm(normed_part, p, inner) for p in pieces] + [
             mm(attended, up_part, inner),
-            mm(normed_part, grad_pre.astype(bf16), inner),
+            mm(normed_part, grad_pre, inner),
             mm(activation, up_part, inner),
-            jnp.sum(pieces[0], axis=0),
-            jnp.sum(pieces[2], axis=0),
+            s_q[0],
+            s_v[0],
             jnp.sum(up_all.astype(f32), axis=0),
-            jnp.sum(grad_pre, axis=0),
+            grad_fc_bias,
         ]
         total = terms if total is None else [a + b for a, b in zip(total, terms)]
     g_q, g_k, g_v, grad_dense, grad_fc_one, grad_fc_two, s_q, s_v, grad_out, grad_fc_bias = total
-    norms = small_sum(jnp.concatenate([gain_sum, shift_sum], axis=0), ("dp", "tensor"), 4)
+    norms = small_exchange(
+        jnp.concatenate([gain_sum, shift_sum], axis=0), ("dp", "tensor"), 4, True
+    )
 
     layer_out = jnp.concatenate(
         [jnp.where(is_first, outputs[i], outputs[i + 1]) for i in range(count)], axis=0

time: 835 us -> 607 us (0.73)
  local copies, waits for them, and re-layouts: 190 us -> 18.1 us
  Pallas kernels: 140 us -> 251 us
  waiting for transfers between devices: 107 us -> 10.8 us
  matrix products: 298 us -> 263 us
  other arithmetic: 63.9 us -> 44.9 us
  blocking collectives: 12.7 us -> 0 us
    all_gather x3, waiting for transfers between devices: 107 us -> 10.8 us  [gather(): return lax.all_gather(x, ('dp', 'tensor'), axis=1, tiled=True)]
    pallas_call x1 -> x10, Pallas kernels: 12.2 us -> 105 us  [the longest x8 85.8 us: attention_call(): pl.pallas_call(kernel, grid=(blocks,), in_specs=[block] * len(arrays) + [...]
    reshape x27 -> x0, local copies, waits for them, and re-layouts: 57.3 us -> none  [the longest x10 21.8 us: attention_forward(): (mm(normed, proj_qkv[2]) + bias_qv[1]).astype(jnp.bfloat16).reshape(shape)]
    unnamed x369 -> x178, local copies, waits for them, and re-layouts: 64.7 us -> 12.2 us
    dot_general x30 -> x0, matrix products: 37.6 us -> none  [the longest x5 9.37 us: attention_backward(): jnp.einsum('bhqk,bqhd->bkhd', prob_b, grad_att, preferred_element_type=jn...]
    slice x26 -> x1, local copies, waits for them, and re-layouts: 37.1 us -> 0.01 us  [projections(): bias_qv[1]]
    pallas_call x6, Pallas kernels: 127 us -> 146 us  [relay_call(): pl.pallas_call(functools.partial(kernel, n, last), out_shape=outs, in_spe...]
    all_gather x1 -> x0, blocking collectives: 12.7 us -> none  [per_device(): all_segments = lax.all_gather(segments, 'dp', axis=1)]
  transfers between devices with their start and end apart: 3 -> 3, of which waited for: 1 -> 1; matrix products, arithmetic and copies ran while one was open for 10% -> 21% of each run, Pallas kernels for 9% -> 28%
where the time goes in v2:
time: 607 us; the launch traced here: 603 us
  matrix products  263 us (43%)
  Pallas kernels  251 us (41%)
  other arithmetic  44.9 us (7%)
  local copies, waits for them, and re-layouts  18.1 us (3%)
  between operations  15.2 us (3%)
  waiting for transfers between devices  10.8 us (2%)
    dot_general x60, matrix products, mm(): lax.dot_general(left, right, (dims, ((), ())), preferred_element_type=jnp...  263 us
    pallas_call x6, Pallas kernels, relay_call(): pl.pallas_call(functools.partial(kernel, n, last), out_shape=outs, in_spe...  146 us
    pallas_call x8, Pallas kernels, attention_call(): pl.pallas_call(kernel, grid=(blocks,), in_specs=[block] * len(arrays) + [...  85.8 us
    pallas_call x2, Pallas kernels, small_exchange(): pl.pallas_call(functools.partial(exchange_kernel, axes, add), out_shape=j...  19.5 us
    unnamed x178, local copies, waits for them, and re-layouts  12.2 us
  transfers between devices with their start and end apart: 3, of which 1 were waited for; matrix products, arithmetic and copies ran while one was open for 21% of the time, Pallas kernels for 28%

profile of v2, /device:TPU:0, one launch (start us, length us, event | category | flops | bytes accessed | tf_op | source)
XLA Modules:
  0.0 603.4 jit_solution(17836824378698772951)
XLA Ops:
  22.0 8.0 %multiply_convert_fusion.4 = (bf16[256,2048]{1,0:T(8,128)(2,1)}, f32[256,2048]{1,0:T(8,128)}) fusion(f32[2048]{0:T(1024)S(1)} %bitcast.416, bf16[256,2048]{1,0:T(8,128)(2,1)S(1)} %bitcast.380, bf16[1,2048,2048]{2,1,0:T(8,128)(2,1)} %param.21), kind=kOutput, calls=%fused_computation.169 | convolution fusion | flops 2152726528 | bytes 12591104 | tf_op jit(solution)/shard_map/dot_general | solution.py:47
  50.9 27.3 %shard_map.204 = (bf16[2,32,2048]{2,1,0:T(8,128)(2,1)S(1)}, bf16[2,32,2048]{2,1,0:T(8,128)(2,1)S(1)}, bf16[2,4,32,2048]{3,2,1,0:T(8,128)(2,1)S(1)}) custom-call(bf16[2,4,32,2048]{3,2,1,0:T(8,128)(2,1)S(1)} %bitcast.332, bf16[2,32,2048]{2,1,0:T(8,128)(2,1)S(1)} %get-tuple-element.136.resid_ref.hidden_ref, f32[1,2048]{1,0:T(1,128)S(1)} %copy-done.24, ...), custom_call_target="tpu_custom_call" | custom-call | tf_op jit(solution)/shard_map/pallas_call | solution.py:374
  106.3 28.6 %shard_map.206 = (bf16[2,32,2048]{2,1,0:T(8,128)(2,1)S(1)}, bf16[2,32,2048]{2,1,0:T(8,128)(2,1)S(1)}, bf16[2,4,32,2048]{3,2,1,0:T(8,128)(2,1)S(1)}) custom-call(bf16[2,4,32,2048]{3,2,1,0:T(8,128)(2,1)S(1)} %bitcast.333, bf16[2,32,2048]{2,1,0:T(8,128)(2,1)S(1)} %copy-done.14, f32[1,2048]{1,0:T(1,128)S(1)} %copy-done.24, f32[1,2048]{1,0:T(1,128)S(1)} %copy-done.17, ...), custom_call_target="tpu_custom_call" | custom-call | tf_op jit(solution)/shard_map/pallas_call | solution.py:374
  138.5 10.8 %all-gather.6.cloned.1.call-done = bf16[4,512,2048]{2,1,0:T(8,128)(2,1)} async-done(((bf16[4,32,2048]{2,1,0:T(8,128)(2,1)}), bf16[4,512,2048]{2,1,0:T(8,128)(2,1)}) %all-gather.6.cloned.1.call-update) | async-done | bytes 8388624 | tf_op jit(solution)/shard_map/all_gather | solution.py:483
  159.2 7.4 %multiply_convert_fusion.2 = (bf16[256,2048]{1,0:T(8,128)(2,1)}, f32[256,2048]{1,0:T(8,128)S(1)}) fusion(f32[2048]{0:T(1024)S(1)} %bitcast.418, bf16[256,2048]{1,0:T(8,128)(2,1)S(1)} %bitcast.349, bf16[1,2048,2048]{2,1,0:T(8,128)(2,1)} %param.21), kind=kOutput, calls=%fused_computation.167 | convolution fusion | flops 2152726528 | bytes 12591104 | tf_op jit(solution)/shard_map/dot_general | solution.py:47
  180.0 6.7 %shard_map.209 = (bf16[256,512]{1,0:T(8,128)(2,1)}, bf16[256,512]{1,0:T(8,128)(2,1)}, bf16[256,512]{1,0:T(8,128)(2,1)}) custom-call(bf16[256,512]{1,0:T(8,128)(2,1)} %get-tuple-element.77.q_ref, bf16[256,512]{1,0:T(8,128)(2,1)} %get-tuple-element.78.k_ref, bf16[256,512]{1,0:T(8,128)(2,1)} %get-tuple-element.79.v_ref, bf16[256,512]{1,0:T(8,128)(2,1)} %fusion.188.ga_ref, ...), custom_call_target="tpu_custom_call" | custom-call | flops 335544320 | bytes 2097152 | tf_op jit(solution)/shard_map/pallas_call | solution.py:151
  194.7 23.1 %shard_map.210 = (bf16[2,32,2048]{2,1,0:T(8,128)(2,1)S(1)}, f32[1,2048]{1,0:T(1,128)S(1)}, f32[1,2048]{1,0:T(1,128)S(1)}, bf16[2,4,32,2048]{3,2,1,0:T(8,128)(2,1)S(1)}) custom-call(bf16[2,4,32,2048]{3,2,1,0:T(8,128)(2,1)S(1)} %bitcast.331, bf16[2,4,32,2048]{3,2,1,0:T(8,128)(2,1)S(1)} %bitcast.329, bf16[2,32,2048]{2,1,0:T(8,128)(2,1)S(1)} %copy-done.11, ...), custom_call_target="tpu_custom_call" | custom-call | tf_op jit(solution)/shard_map/pallas_call | solution.py:374
  221.3 7.2 %shard_map.216 = s32[4,4,128]{2,1,0:T(4,128)} custom-call(s32[4,128]{1,0:T(4,128)} %x_ref.1), custom_call_target="tpu_custom_call" | custom-call | tf_op jit(solution)/shard_map/pallas_call | solution.py:435
  229.7 8.8 %fusion.82 = bf16[256,2048]{1,0:T(8,128)(2,1)} fusion(f32[256,2048]{1,0:T(8,128)} %get-tuple-element.211, bf16[256,2048]{1,0:T(8,128)(2,1)} %bitcast.338, bf16[1,2048,2048]{2,1,0:T(8,128)(2,1)} %param.23), kind=kOutput, calls=%fused_computation.107 | convolution fusion | flops 2157969408 | bytes 12582912 | tf_op jit(solution)/shard_map/dot_general | solution.py:47
  240.0 6.7 %shard_map.211 = (bf16[256,512]{1,0:T(8,128)(2,1)}, bf16[256,512]{1,0:T(8,128)(2,1)}, bf16[256,512]{1,0:T(8,128)(2,1)}) custom-call(bf16[256,512]{1,0:T(8,128)(2,1)} %get-tuple-element.84.q_ref, bf16[256,512]{1,0:T(8,128)(2,1)} %get-tuple-element.85.k_ref, bf16[256,512]{1,0:T(8,128)(2,1)} %get-tuple-element.86.v_ref, bf16[256,512]{1,0:T(8,128)(2,1)} %fusion.191.ga_ref, ...), custom_call_target="tpu_custom_call" | custom-call | flops 335544320 | bytes 2097152 | tf_op jit(solution)/shard_map/pallas_call | solution.py:151
  260.4 34.9 %shard_map.212 = (bf16[2,32,2048]{2,1,0:T(8,128)(2,1)S(1)}, f32[1,2048]{1,0:T(1,128)S(1)}, f32[1,2048]{1,0:T(1,128)S(1)}, bf16[2,4,32,2048]{3,2,1,0:T(8,128)(2,1)S(1)}) custom-call(bf16[2,4,32,2048]{3,2,1,0:T(8,128)(2,1)S(1)} %bitcast.330, bf16[2,4,32,2048]{3,2,1,0:T(8,128)(2,1)S(1)} %copy-done.9, bf16[2,32,2048]{2,1,0:T(8,128)(2,1)S(1)} %copy-done.15, ...), custom_call_target="tpu_custom_call" | custom-call | tf_op jit(solution)/shard_map/pallas_call | solution.py:374
  317.1 9.8 %shard_map.208 = bf16[2,32,2048]{2,1,0:T(8,128)(2,1)S(1)} custom-call(bf16[2,4,32,2048]{3,2,1,0:T(8,128)(2,1)S(1)} %bitcast.335, bf16[2,32,2048]{2,1,0:T(8,128)(2,1)S(1)} %copy-done.12, f32[1,2048]{1,0:T(1,128)S(1)} %copy-done.24, f32[1,2048]{1,0:T(1,128)S(1)} %copy-done.17, f32[1,2048]{1,0:T(1,128)S(1)} %copy-done.23), custom_call_target="tpu_custom_call" | custom-call | tf_op jit(solution)/shard_map/pallas_call | solution.py:374
  327.7 8.0 %fusion.75 = bf16[256,2048]{1,0:T(8,128)(2,1)} fusion(f32[256,2048]{1,0:T(8,128)S(1)} %copy-done.74, bf16[256,2048]{1,0:T(8,128)(2,1)S(1)} %bitcast.336, bf16[1,2048,2048]{2,1,0:T(8,128)(2,1)} %param.23), kind=kOutput, calls=%fused_computation.100 | convolution fusion | flops 2157969408 | bytes 12582912 | tf_op jit(solution)/shard_map/dot_general | solution.py:47
  337.1 6.7 %shard_map.213 = (bf16[256,512]{1,0:T(8,128)(2,1)}, bf16[256,512]{1,0:T(8,128)(2,1)}, bf16[256,512]{1,0:T(8,128)(2,1)}) custom-call(bf16[256,512]{1,0:T(8,128)(2,1)} %get-tuple-element.91.q_ref, bf16[256,512]{1,0:T(8,128)(2,1)} %get-tuple-element.92.k_ref, bf16[256,512]{1,0:T(8,128)(2,1)} %get-tuple-element.93.v_ref, bf16[256,512]{1,0:T(8,128)(2,1)} %fusion.194.ga_ref, ...), custom_call_target="tpu_custom_call" | custom-call | flops 335544320 | bytes 2097152 | tf_op jit(solution)/shard_map/pallas_call | solution.py:151
  357.1 21.9 %shard_map.214 = (bf16[2,32,2048]{2,1,0:T(8,128)(2,1)S(1)}, f32[1,2048]{1,0:T(1,128)S(1)}, f32[1,2048]{1,0:T(1,128)S(1)}) custom-call(bf16[2,4,32,2048]{3,2,1,0:T(8,128)(2,1)S(1)} %bitcast.334, bf16[2,4,32,2048]{3,2,1,0:T(8,128)(2,1)S(1)} %get-tuple-element.90.up_ref, bf16[2,32,2048]{2,1,0:T(8,128)(2,1)S(1)} %get-tuple-element.136.resid_ref.hidden_ref, ...), custom_call_target="tpu_custom_call" | custom-call | tf_op jit(solution)/shard_map/pallas_call | solution.py:374
  380.4 12.3 %shard_map.215 = f32[2,2048]{1,0:T(2,128)} custom-call(f32[2,2048]{1,0:T(2,128)} %pad_maximum_fusion.10.x_ref), custom_call_target="tpu_custom_call" | custom-call | tf_op jit(solution)/shard_map/pallas_call | solution.py:435
  396.3 6.6 %bitcast_select_fusion = (bf16[2,512,2048]{2,1,0:T(8,128)(2,1)S(1)}, bf16[2,512,2048]{2,1,0:T(8,128)(2,1)S(1)}, bf16[2,512,2048]{2,1,0:T(8,128)(2,1)S(1)}, bf16[2,512,2048]{2,1,0:T(8,128)(2,1)S(1)}) fusion(bf16[2,1,512,2048]{3,2,0,1:T(8,128)(2,1)} %all-gather.10.cloned.1.call-done, pred[]{:T(512)S(6)} %eq.88, ...), kind=kLoop, calls=%fused_computation.60 | loop fusion | flops 8388608 | bytes 33554432 | tf_op jit(solution)/shard_map/jit(_where)/select_n | solution.py:582
  434.4 11.0 %fusion.30 = f32[1024,2048]{1,0:T(8,128)} fusion(bf16[1024,2048]{1,0:T(8,128)(2,1)S(1)} %bitcast.375, bf16[1,2048,2048]{2,1,0:T(8,128)(2,1)S(1)} %bitcast.411), kind=kOutput, calls=%fused_computation.34 | convolution fusion | flops 8589934592 | bytes 20971520 | tf_op jit(solution)/shard_map/dot_general | solution.py:47
  445.4 20.0 %fusion.279 = (f32[2048]{0:T(1024)S(1)}, bf16[1024,2048]{1,0:T(8,128)(2,1)}) fusion(f32[1024,2048]{1,0:T(8,128)} %fusion.30, f32[2048]{0:T(1024)S(1)} %bitcast.419, bf16[1024,2048]{1,0:T(8,128)(2,1)S(1)} %bitcast.361, bf16[1,2048,2048]{2,1,0:T(8,128)(2,1)} %param.23), kind=kOutput, calls=%fused_computation.348 | convolution fusion | flops 8636069888 | bytes 25182208 | tf_op jit(solution)/shard_map/dot_general | solution.py:47
  465.4 20.6 %multiply_convert_fusion = (bf16[1024,2048]{1,0:T(8,128)(2,1)}, bf16[1024,2048]{1,0:T(8,128)(2,1)}, f32[1024,2048]{1,0:T(8,128)}) fusion(f32[2048]{0:T(1024)S(1)} %bitcast.420, f32[1024,2048]{1,0:T(8,128)} %fusion.30, bf16[1024,2048]{1,0:T(8,128)(2,1)S(1)} %bitcast.367, bf16[1,2048,2048]{2,1,0:T(8,128)(2,1)} %param.21), kind=kOutput, calls=%fused_computation.48 | convolution fusion | flops 8631877632 | bytes 37756928 | tf_op jit(solution)/shard_map/dot_general | solution.py:47
  486.0 23.6 %shard_map.217 = (bf16[1024,512]{1,0:T(8,128)(2,1)}, bf16[1024,512]{1,0:T(8,128)(2,1)}, bf16[1024,512]{1,0:T(8,128)(2,1)}, bf16[1024,512]{1,0:T(8,128)(2,1)}, f32[1,512]{1,0:T(1,128)}, /*index=5*/f32[1,512]{1,0:T(1,128)}) custom-call(f32[1024,512]{1,0:T(8,128)} %fusion.148.q_ref, f32[1024,512]{1,0:T(8,128)} %fusion.118.k_ref, f32[1024,512]{1,0:T(8,128)} %fusion.154.v_ref, ...), custom_call_target="tpu_custom_call" | custom-call | flops 1342177280 | bytes 8388608 | tf_op jit(solution)/shard_map/pallas_call | solution.py:151
  529.3 17.2 %fusion.278 = (f32[2048]{0:T(1024)S(1)}, bf16[1024,2048]{1,0:T(8,128)(2,1)}) fusion(f32[1024,2048]{1,0:T(8,128)} %get-tuple-element.216, f32[2048]{0:T(1024)S(1)} %bitcast.421, bf16[1024,2048]{1,0:T(8,128)(2,1)S(1)} %bitcast.356, bf16[1,2048,2048]{2,1,0:T(8,128)(2,1)S(1)} %bitcast.415), kind=kOutput, calls=%fused_computation.347 | convolution fusion | flops 8636069888 | bytes 25182208 | tf_op jit(solution)/shard_map/dot_general | solution.py:47
  547.1 23.7 %shard_map.218 = (bf16[1024,512]{1,0:T(8,128)(2,1)}, bf16[1024,512]{1,0:T(8,128)(2,1)}, bf16[1024,512]{1,0:T(8,128)(2,1)}, bf16[1024,512]{1,0:T(8,128)(2,1)}, f32[1,512]{1,0:T(1,128)}, /*index=5*/f32[1,512]{1,0:T(1,128)}) custom-call(f32[1024,512]{1,0:T(8,128)} %fusion.151.q_ref, f32[1024,512]{1,0:T(8,128)} %fusion.116.k_ref, f32[1024,512]{1,0:T(8,128)} %fusion.157.v_ref, ...), custom_call_target="tpu_custom_call" | custom-call | flops 1342177280 | bytes 8388608 | tf_op jit(solution)/shard_map/pallas_call | solution.py:151
  582.5 6.9 %add_bitcast_fusion = f32[1,2048,512]{2,1,0:T(8,128)} fusion(f32[2048,512]{1,0:T(8,128)} %fusion.199, bf16[1024,2048]{1,0:T(8,128)(2,1)S(1)} %copy-done.71, bf16[1024,2048]{1,0:T(8,128)(2,1)S(1)} %bitcast.358, s32[]{:T(128)S(6)} %select_n.154), kind=kOutput, calls=%fused_computation.64 | convolution fusion | flops 2148532224 | bytes 13631492 | tf_op jit(solution)/shard_map/dot_general | solution.py:47
  (317 shorter events, 230.4 us)
Async XLA Ops:
  7.2 42.8 %copy-start = (bf16[1,512,2048]{2,1,0:T(8,128)(2,1)S(1)}, bf16[1,512,2048]{2,1,0:T(8,128)(2,1)}, u32[]{:S(2)}) copy-start(bf16[1,512,2048]{2,1,0:T(8,128)(2,1)} %param.19) | copy-start | bytes 6291460
  7.2 142.1 %all-gather.6.cloned.1.call-start = ((), (), s32[]{:S(2)}) async-start(), calls=%async_computation | async-start | bytes 8912896 | tf_op jit(solution)/shard_map/all_gather | solution.py:483
  16.5 379.9 %all-gather.10.cloned.1.call-start = ((), (), s32[]{:S(2)}) async-start(), calls=%async_computation.2 | async-start | bytes 4456448 | tf_op jit(solution)/shard_map/all_gather | solution.py:483
  21.8 10.1 %slice-start = ((s8[6291456]{0:T(1024)(128)(4,1)}), s8[4194304]{0:T(1024)(128)(4,1)S(1)}, s32[]{:S(2)}) async-start(s8[6291456]{0:T(1024)(128)(4,1)} %bitcast.350), calls=%async_computation.3 | async-start | bytes 8388608
  21.9 9.0 %copy-start.59 = (f32[1,2,512]{2,1,0:T(2,128)S(1)}, f32[1,2,512]{2,1,0:T(2,128)}, u32[]{:S(2)}) copy-start(f32[1,2,512]{2,1,0:T(2,128)} %param.18) | copy-start | bytes 12292
  21.9 9.9 %slice-start.1 = ((s8[6291456]{0:T(1024)(128)(4,1)}), s8[2097152]{0:T(1024)(128)(4,1)S(1)}, s32[]{:S(2)}) async-start(s8[6291456]{0:T(1024)(128)(4,1)} %bitcast.350), calls=%async_computation.4 | async-start | bytes 4194304
  42.4 35.8 %slice-start.4 = ((s8[8388608]{0:T(1024)(128)(4,1)}), s8[4194304]{0:T(1024)(128)(4,1)S(1)}, s32[]{:S(2)}) async-start(s8[8388608]{0:T(1024)(128)(4,1)} %bitcast.406), calls=%async_computation.7 | async-start | bytes 8388608
  43.7 34.5 %slice-start.5 = ((s8[8388608]{0:T(1024)(128)(4,1)}), s8[4194304]{0:T(1024)(128)(4,1)S(1)}, s32[]{:S(2)}) async-start(s8[8388608]{0:T(1024)(128)(4,1)} %bitcast.406), calls=%async_computation.8 | async-start | bytes 8388608
  106.0 28.8 %copy-start.37 = (bf16[4,128,2048]{2,1,0:T(8,128)(2,1)S(1)}, bf16[4,128,2048]{2,1,0:T(8,128)(2,1)}, u32[]{:S(2)}) copy-start(bf16[4,128,2048]{2,1,0:T(8,128)(2,1)} %copy-done.36) | copy-start | bytes 6291460
  155.9 10.6 %slice-start.10 = ((s8[8388608]{0:T(1024)(128)(4,1)}), s8[4194304]{0:T(1024)(128)(4,1)S(1)}, s32[]{:S(2)}) async-start(s8[8388608]{0:T(1024)(128)(4,1)} %bitcast.412), calls=%async_computation.13 | async-start | bytes 8388608
  159.1 7.4 %copy-start.3 = (bf16[2,128,2048]{2,1,0:T(8,128)(2,1)S(1)}, bf16[2,128,2048]{2,1,0:T(8,128)(2,1)}, u32[]{:S(2)}) copy-start(bf16[2,128,2048]{2,1,0:T(8,128)(2,1)} %copy-done.2) | copy-start | bytes 3145732
  159.1 7.4 %slice-start.11 = ((s8[8388608]{0:T(1024)(128)(4,1)}), s8[4194304]{0:T(1024)(128)(4,1)S(1)}, s32[]{:S(2)}) async-start(s8[8388608]{0:T(1024)(128)(4,1)} %bitcast.412), calls=%async_computation.14 | async-start | bytes 8388608
  159.2 10.9 %slice-start.6 = ((s8[8388608]{0:T(1024)(128)(4,1)}), s8[4194304]{0:T(1024)(128)(4,1)S(1)}, s32[]{:S(2)}) async-start(s8[8388608]{0:T(1024)(128)(4,1)} %bitcast.408), calls=%async_computation.9 | async-start | bytes 8388608
  221.3 175.1 %all-gather.8.cloned.1.call-start = ((), (), s32[]{:S(2)}) async-start(), calls=%async_computation.1 | async-start | bytes 4456448 | tf_op jit(solution)/shard_map/all_gather | solution.py:483
  229.7 8.8 %copy-start.8 = (bf16[2,4,32,2048]{3,2,1,0:T(8,128)(2,1)S(1)}, bf16[2,4,32,2048]{3,2,1,0:T(8,128)(2,1)}, u32[]{:S(2)}) copy-start(bf16[2,4,32,2048]{3,2,1,0:T(8,128)(2,1)} %copy-done.7) | copy-start | bytes 3145732
  316.2 11.5 %copy-start.74 = (f32[256,2048]{1,0:T(8,128)S(1)}, f32[256,2048]{1,0:T(8,128)}, u32[]{:S(2)}) copy-start(f32[256,2048]{1,0:T(8,128)} %get-tuple-element.209) | copy-start | bytes 6291460
  403.0 31.4 %copy-start.44 = (bf16[2,512,2048]{2,1,0:T(8,128)(2,1)}, bf16[2,512,2048]{2,1,0:T(8,128)(2,1)S(1)}, u32[]{:S(2)}) copy-start(bf16[2,512,2048]{2,1,0:T(8,128)(2,1)S(1)} %get-tuple-element.131) | copy-start | bytes 12582916
  403.0 42.4 %copy-start.34 = (bf16[2,512,2048]{2,1,0:T(8,128)(2,1)}, bf16[2,512,2048]{2,1,0:T(8,128)(2,1)S(1)}, u32[]{:S(2)}) copy-start(bf16[2,512,2048]{2,1,0:T(8,128)(2,1)S(1)} %get-tuple-element.132) | copy-start | bytes 12582916
  403.0 62.4 %copy-start.40 = (bf16[2,512,2048]{2,1,0:T(8,128)(2,1)}, bf16[2,512,2048]{2,1,0:T(8,128)(2,1)S(1)}, u32[]{:S(2)}) copy-start(bf16[2,512,2048]{2,1,0:T(8,128)(2,1)S(1)} %get-tuple-element.124) | copy-start | bytes 12582916
  423.0 11.3 %slice-start.8 = ((s8[8388608]{0:T(1024)(128)(4,1)}), s8[4194304]{0:T(1024)(128)(4,1)S(1)}, s32[]{:S(2)}) async-start(s8[8388608]{0:T(1024)(128)(4,1)} %bitcast.410), calls=%async_computation.11 | async-start | bytes 8388608
  520.3 8.9 %slice-start.12 = ((s8[8388608]{0:T(1024)(128)(4,1)}), s8[4194304]{0:T(1024)(128)(4,1)S(1)}, s32[]{:S(2)}) async-start(s8[8388608]{0:T(1024)(128)(4,1)} %bitcast.414), calls=%async_computation.15 | async-start | bytes 8388608
  547.1 23.7 %copy-start.61 = (f32[1,512]{1,0:T(1,128)S(1)}, f32[1,512]{1,0:T(1,128)}, u32[]{:S(2)}) copy-start(f32[1,512]{1,0:T(1,128)} %get-tuple-element.115) | copy-start | bytes 6148
  547.1 24.4 %copy-start.60 = (f32[1,512]{1,0:T(1,128)S(1)}, f32[1,512]{1,0:T(1,128)}, u32[]{:S(2)}) copy-start(f32[1,512]{1,0:T(1,128)} %get-tuple-element.113) | copy-start | bytes 6148
  547.1 28.1 %copy-start.70 = (f32[512,512]{1,0:T(8,128)S(1)}, f32[512,512]{1,0:T(8,128)}, u32[]{:S(2)}) copy-start(f32[512,512]{1,0:T(8,128)} %fusion.211) | copy-start | bytes 3145732
  (68 other events, 211.0 us)
Sparse Core Ops, SparseCore 0:
  16.6 132.6 all-gather.5
  221.4 84.2 all-gather.9
  308.4 83.5 all-gather.7

commit v3 on v2

--- a/solution.py
+++ b/solution.py
@@ -200,137 +200,135 @@
     return out
 
 
-def enter(n, section_target, is_waiter):
-    t = lax.axis_index("tensor")
-    sec = lax.axis_index("section")
+def enter(n):
+    t, sec = lax.axis_index("tensor"), lax.axis_index("section")
     barrier = pltpu.get_barrier_semaphore()
     for k in range(1, n):
         pl.semaphore_signal(
             barrier, inc=1, device_id={"tensor": partner(t, k)}, device_id_type=MESH
         )
-    if section_target is None:
-        pl.semaphore_wait(barrier, n - 1)
-        return
-
-    @pl.when(sec == section_target)
-    def _():
-        pl.semaphore_signal(barrier, inc=1, device_id={"section": 1 - sec}, device_id_type=MESH)
-        pl.semaphore_wait(barrier, n - 1)
-
-    @pl.when(sec != section_target)
-    def _():
-        pl.semaphore_wait(barrier, n)
-
-
-def scatter_sum(n, partial_ref, recv, send_sem, recv_sem, own_rows):
-    t = lax.axis_index("tensor")
-    copies = []
-    for k in range(n - 1, 0, -1):
-        peer = partner(t, k)
-        copy = pltpu.make_async_remote_copy(
-            src_ref=partial_ref.at[:, peer],
-            dst_ref=recv.at[k - 1],
-            send_sem=send_sem.at[k - 1],
-            recv_sem=recv_sem.at[k - 1],
-            device_id={"tensor": peer},
-            device_id_type=MESH,
+    pl.semaphore_signal(barrier, inc=1, device_id={"section": 1 - sec}, device_id_type=MESH)
+    pl.semaphore_wait(barrier, n)
+
+
+def send(src, dst, sems, device):
+    copy = pltpu.make_async_remote_copy(
+        src_ref=src, dst_ref=dst, send_sem=sems[0], recv_sem=sems[1],
+        device_id=device, device_id_type=MESH,
+    )
+    copy.start()
+    return copy
+
+
+def halves_of(width):
+    sec = lax.axis_index("section")
+    half = width // 2
+    return (
+        pl.ds(pl.multiple_of(sec * half, half), half),
+        pl.ds(pl.multiple_of((1 - sec) * half, half), half),
+    )
+
+
+def reduced_half(n, partial_ref, scratch):
+    pair, out_buf, recv, pair_sems, rs_sems = scratch
+    t, sec = lax.axis_index("tensor"), lax.axis_index("section")
+    mine, other = halves_of(partial_ref.shape[-1])
+    enter(n)
+    order = list(range(n - 1, -1, -1))
+    swaps = {}
+    for k in order:
+        at = partner(t, k)
+        swaps[k] = send(
+            partial_ref.at[:, at, :, other], pair.at[k],
+            [x.at[k] for x in pair_sems], {"section": 1 - sec},
         )
-        copy.start()
-        copies.append((k, copy))
-    total = partial_ref[:, t].astype(jnp.float32) + own_rows
-    for k, copy in copies:
+    sends = []
+    for k in order:
+        at = partner(t, k)
+        swaps[k].wait_recv()
+        both = partial_ref[:, at, :, mine].astype(jnp.float32) + pair[k].astype(jnp.float32)
+        if k == 0:
+            total = both
+        else:
+            out_buf[k - 1] = both.astype(jnp.bfloat16)
+            sends.append(
+                (k, send(out_buf.at[k - 1], recv.at[k - 1],
+                         [x.at[k - 1] for x in rs_sems], {"tensor": at}))
+            )
+    for k, copy in sends:
         copy.wait_recv()
         total = total + recv[k - 1].astype(jnp.float32)
-    return total, copies
-
-
-def spread(n, full_ref, send_sem, recv_sem):
-    t = lax.axis_index("tensor")
-    copies = []
-    for k in range(n - 1, 0, -1):
-        copy = pltpu.make_async_remote_copy(
-            src_ref=full_ref.at[:, t],
-            dst_ref=full_ref.at[:, t],
-            send_sem=send_sem.at[k - 1],
-            recv_sem=recv_sem.at[k - 1],
-            device_id={"tensor": partner(t, k)},
-            device_id_type=MESH,
+    return total, list(swaps.values()) + [copy for _, copy in sends]
+
+
+def spread(n, full_ref, ag_sems, fw_sems):
+    t, sec = lax.axis_index("tensor"), lax.axis_index("section")
+    mine, _ = halves_of(full_ref.shape[-1])
+    own = full_ref.at[:, t, :, mine]
+    copies = [
+        send(own, own, [x.at[k - 1] for x in ag_sems], {"tensor": partner(t, k)})
+        for k in range(n - 1, 0, -1)
+    ]
+    passed = []
+    for k, copy in zip(range(n - 1, 0, -1), copies):
+        copy.wait_recv()
+        part = full_ref.at[:, partner(t, k), :, mine]
+        passed.append(send(part, part, [x.at[k - 1] for x in fw_sems], {"section": 1 - sec}))
+    for copy in copies:
+        copy.wait_send()
+    for copy in passed:
+        copy.wait()
+
+
+def standard_of(rows):
+    centred = rows - jnp.mean(rows, axis=-1, keepdims=True)
+    inv_std = lax.rsqrt(jnp.mean(centred * centred, axis=-1, keepdims=True) + NORM_EPS)
+    return centred * inv_std, inv_std
+
+
+def forward_kernel(n, last, partial_ref, resid_ref, bias_ref, *rest):
+    if last:
+        out_ref, *scratch = rest
+    else:
+        gain_ref, shift_ref, out_ref, full_ref, *scratch = rest
+    t, sec = lax.axis_index("tensor"), lax.axis_index("section")
+    mine, _ = halves_of(partial_ref.shape[-1])
+    total, copies = reduced_half(n, partial_ref, unpack(scratch))
+    total = total + resid_ref[:, :, mine].astype(jnp.float32) + bias_ref[:, mine][None]
+    out_ref[:, :, mine] = total.astype(jnp.bfloat16)
+    part = out_ref.at[:, :, mine]
+    hop = send(part, part, scratch[7:9], {"section": 1 - sec})
+    hop.wait()
+    if not last:
+        standard, _ = standard_of(out_ref[...].astype(jnp.float32))
+        full_ref[:, t] = (standard * gain_ref[...][None] + shift_ref[...][None]).astype(
+            jnp.bfloat16
         )
-        copy.start()
-        copies.append(copy)
+        spread(n, full_ref, scratch[9:11], scratch[11:13])
     for copy in copies:
-        copy.wait()
-
-
-def forward_kernel(
-    n, last, partial_ref, resid_ref, bias_ref, gain_ref, shift_ref, *rest
-):
+        copy.wait_send()
+
+
+def unpack(scratch):
+    pair, out_buf, recv, pair_s, pair_r, rs_s, rs_r = scratch[:7]
+    return pair, out_buf, recv, (pair_s, pair_r), (rs_s, rs_r)
+
+
+def backward_kernel(n, last, partial_ref, up_ref, hidden_ref, gain_ref, *rest):
     if last:
-        out_ref, recv, send_sem, recv_sem = rest
-        enter(n, None, None)
-        total, copies = scatter_sum(
-            n, partial_ref, recv, send_sem, recv_sem,
-            resid_ref[...].astype(jnp.float32) + bias_ref[...][None],
-        )
-        out_ref[...] = total.astype(jnp.bfloat16)
-        for _, copy in copies:
-            copy.wait_send()
-        return
-    (n0_ref, x_ref, out_ref, hidden_ref, full_ref, recv, send_sem, recv_sem,
-     hop_send, hop_recv, ag_send, ag_recv) = rest
-    sec = lax.axis_index("section")
-    t = lax.axis_index("tensor")
-    enter(n, 1, None)
-    total, copies = scatter_sum(
-        n, partial_ref, recv, send_sem, recv_sem,
-        resid_ref[...].astype(jnp.float32) + bias_ref[...][None],
-    )
-    out_ref[...] = total.astype(jnp.bfloat16)
-    hop = pltpu.make_async_remote_copy(
-        src_ref=out_ref,
-        dst_ref=hidden_ref,
-        send_sem=hop_send,
-        recv_sem=hop_recv,
-        device_id={"section": 1 - sec},
-        device_id_type=MESH,
-    )
-
-    @pl.when(sec == 0)
-    def _():
-        hop.start()
-        full_ref[...] = n0_ref[...]
-        hidden_ref[...] = x_ref[...]
-        hop.wait_send()
-
-    @pl.when(sec == 1)
-    def _():
-        hop.wait_recv()
-        residual = hidden_ref[...].astype(jnp.float32)
-        centred = residual - jnp.mean(residual, axis=-1, keepdims=True)
-        inv_std = lax.rsqrt(jnp.mean(centred * centred, axis=-1, keepdims=True) + NORM_EPS)
-        normed = centred * inv_std * gain_ref[...][None] + shift_ref[...][None]
-        full_ref[:, t] = normed.astype(jnp.bfloat16)
-        spread(n, full_ref, ag_send, ag_recv)
-
-    for _, copy in copies:
-        copy.wait_send()
-
-
-def backward_kernel(n, last, partial_ref, up_ref, hidden_ref, gain_ref, *rest):
-    t = lax.axis_index("tensor")
-    sec = lax.axis_index("section")
-    if last:
-        out_ref, ggain_ref, gshift_ref, recv, send_sem, recv_sem = rest
-        enter(n, None, None)
+        out_ref, ggain_ref, gshift_ref, *scratch = rest
     else:
-        (cot_ref, out_ref, ggain_ref, gshift_ref, full_ref, recv, send_sem, recv_sem,
-         hop_send, hop_recv, ag_send, ag_recv) = rest
-        enter(n, 0, None)
-    grad_normed, copies = scatter_sum(n, partial_ref, recv, send_sem, recv_sem, 0.0)
-    residual = hidden_ref[...].astype(jnp.float32)
-    centred = residual - jnp.mean(residual, axis=-1, keepdims=True)
-    inv_std = lax.rsqrt(jnp.mean(centred * centred, axis=-1, keepdims=True) + NORM_EPS)
-    standard = centred * inv_std
+        out_ref, ggain_ref, gshift_ref, full_ref, *scratch = rest
+    *scratch, whole = scratch
+    t, sec = lax.axis_index("tensor"), lax.axis_index("section")
+    mine, _ = halves_of(partial_ref.shape[-1])
+    total, copies = reduced_half(n, partial_ref, unpack(scratch))
+    whole[:, :, mine] = total
+    part = whole.at[:, :, mine]
+    hop = send(part, part, scratch[7:9], {"section": 1 - sec})
+    standard, inv_std = standard_of(hidden_ref[...].astype(jnp.float32))
+    hop.wait()
+    grad_normed = whole[...]
     scaled = grad_normed * gain_ref[...][None]
     grad_in = inv_std * (
         scaled
@@ -339,37 +337,27 @@
     )
     out_ref[...] = (up_ref[:, t].astype(jnp.float32) + grad_in).astype(jnp.bfloat16)
     if not last:
-        hop = pltpu.make_async_remote_copy(
-            src_ref=out_ref,
-            dst_ref=full_ref.at[:, t],
-            send_sem=hop_send,
-            recv_sem=hop_recv,
-            device_id={"section": 1 - sec},
-            device_id_type=MESH,
-        )
-
-        @pl.when(sec == 1)
-        def _():
-            hop.start()
-            full_ref[...] = cot_ref[...]
-            hop.wait_send()
-
-        @pl.when(sec == 0)
-        def _():
-            hop.wait_recv()
-            spread(n, full_ref, ag_send, ag_recv)
-
+        full_ref[:, t] = out_ref[...]
+        spread(n, full_ref, scratch[9:11], scratch[11:13])
     ggain_ref[...] = jnp.sum(jnp.sum(grad_normed * standard, axis=0), axis=0, keepdims=True)
     gshift_ref[...] = jnp.sum(jnp.sum(grad_normed, axis=0), axis=0, keepdims=True)
-    for _, copy in copies:
+    for copy in copies:
         copy.wait_send()
 
 
-def relay_call(kernel, n, last, ident, args, outs, rows_shape):
-    sems = [pltpu.SemaphoreType.DMA((n - 1,)), pltpu.SemaphoreType.DMA((n - 1,))]
-    scratch = [pltpu.VMEM((n - 1,) + rows_shape, jnp.bfloat16)] + sems
+def sum_call(kernel, n, last, ident, args, outs, rows_shape):
+    dma = pltpu.SemaphoreType.DMA
+    half = rows_shape[:-1] + (rows_shape[-1] // 2,)
+    scratch = [
+        pltpu.VMEM((n,) + half, jnp.bfloat16),
+        pltpu.VMEM((n - 1,) + half, jnp.bfloat16),
+        pltpu.VMEM((n - 1,) + half, jnp.bfloat16),
+        dma((n,)), dma((n,)), dma((n - 1,)), dma((n - 1,)), dma, dma,
+    ]
     if not last:
-        scratch += [pltpu.SemaphoreType.DMA, pltpu.SemaphoreType.DMA] + sems
+        scratch += [dma((n - 1,))] * 4
+    if kernel is backward_kernel:
+        scratch.append(pltpu.VMEM(rows_shape, jnp.float32))
     vmem = pl.BlockSpec(memory_space=pltpu.VMEM)
     return pl.pallas_call(
         functools.partial(kernel, n, last),
@@ -463,120 +451,122 @@
     share = rows // n
     group = 2 if micro % 2 == 0 else 1
     count = micro // group
-    is_first = lax.axis_index("section") == 0
+    sec = lax.axis_index("section")
+    is_first = sec == 0
     row_start = lax.axis_index("tensor") * share
-    norm_gain, norm_shift = ln_gain, ln_bias
     proj_qkv, proj_dense, fc_one, fc_two = (
         qkv_weight[0], dense_weight[0], fc1_weight[0], fc2_weight[0]
     )
     bias_qv, bias_fc = qv_bias[0], fc1_bias[0]
     bf16, f32 = jnp.bfloat16, jnp.float32
+    features, hidden_units = proj_qkv.shape[-1], fc_one.shape[-1]
+
+    swap = lambda x: lax.ppermute(x, "section", [(0, 1), (1, 0)])
+
+    def half(x, axis, which):
+        size = x.shape[axis] // 2
+        return lax.dynamic_slice_in_dim(x, which * size, size, axis)
+
+    def both(x, axis):
+        return half(x, axis, sec), swap(half(x, axis, 1 - sec))
+
+    def of_layer(index, pair):
+        return jnp.where(sec == index, pair[0], pair[1])
+
+    small = jnp.concatenate(
+        [ln_gain[0], ln_bias[0], out_bias[0], bias_qv.reshape(-1), bias_fc]
+    )[None]
+    small_pair = (small, swap(small))
+    weight_pairs = [
+        both(proj_qkv, 2), both(fc_one, 1), both(proj_dense, 0), both(fc_two, 0)
+    ]
+
+    def parameters(index):
+        vector = of_layer(index, small_pair)[0]
+        gain, shift, bias = [vector[None, i * width : (i + 1) * width] for i in range(3)]
+        at = 3 * width
+        b_qv = half(vector[at : at + 2 * features].reshape(2, features), 1, sec)
+        b_fc = half(vector[at + 2 * features :], 0, sec)
+        return gain, shift, bias, b_qv, b_fc, [of_layer(index, p) for p in weight_pairs]
+
+    layers = [parameters(0), parameters(1)]
 
     live = (segments >= 0)[:, :, None].astype(bf16)
     top = cotangent * live
     own_rows = lambda x: lax.dynamic_slice_in_dim(x, row_start, share, 1)
-    first_normed = normalize(block_input, norm_gain, norm_shift)
+    first_normed = normalize(block_input, layers[0][0], layers[0][1])
     x_rows = own_rows(block_input)
     all_segments = small_exchange(segments, ("dp",), 5, False)
+    tables, allowed = rotary_tables(segments), allowed_of(segments)
 
     def gather(x):
         return lax.all_gather(x, ("dp", "tensor"), axis=1, tiled=True)
 
     early = gather(jnp.where(is_first, own_rows(first_normed), own_rows(top)))
 
-    cut = lambda x, i: x[i * group : (i + 1) * group]
-    four = lambda x: x.reshape(group, n, share, width)
-    flat = lambda x: x.reshape(group * rows, width)
+    four = lambda x: x.reshape(micro, n, share, width)
+    flat = lambda x: x.reshape(micro * rows, width)
     sds = jax.ShapeDtypeStruct
-    rows_shape = (group, share, width)
-
-    normed = four(cut(first_normed, 0))
-    hidden = cut(x_rows, 0)
-    stored, outputs = [], []
-    for moment in range(count + 1):
-        last = moment == count
-        if last:
-            normed, early = settled((normed, early))
-        segment = jnp.where(
-            is_first, cut(segments, min(moment, count - 1)), cut(segments, max(moment - 1, 0))
+    rows_shape = (micro, share, width)
+    rows_out, full_out = sds(rows_shape, bf16), sds((micro, n, share, width), bf16)
+    line = sds((1, width), f32)
+
+    def branch_forward(normed, layer):
+        _, _, _, b_qv, b_fc, (w_qkv, w_one, w_dense, w_two) = layer
+        *kept, attended = attention_call(
+            attention_forward_kernel, projections(normed, w_qkv, b_qv), tables, allowed, 4, 0,
         )
-        tables, allowed = rotary_tables(segment), allowed_of(segment)
-        *kept, attended = attention_call(
-            attention_forward_kernel,
-            projections(flat(normed), proj_qkv, bias_qv), tables, allowed, 4, 0,
-        )
-        pre_act = mm(flat(normed), fc_one) + bias_fc
+        pre_act = mm(normed, w_one) + b_fc
         activation = settled(jax.nn.gelu(pre_act, approximate=True).astype(bf16))
-        partial = (mm(attended, proj_dense) + mm(activation, fc_two)).astype(bf16)
-        stored.append((tables, allowed, hidden, normed, kept, pre_act))
-        args = [four(partial), hidden, out_bias, norm_gain, norm_shift]
-        if last:
-            (out,) = relay_call(
-                forward_kernel, n, True, 1, args, [sds(rows_shape, bf16)], rows_shape
-            )
-        else:
-            ahead = min(moment + 1, count - 1)
-            args += [four(cut(first_normed, ahead)), cut(x_rows, ahead)]
-            out, hidden, normed = relay_call(
-                forward_kernel, n, False, 0, args,
-                [sds(rows_shape, bf16), sds(rows_shape, bf16),
-                 sds((group, n, share, width), bf16)],
-                rows_shape,
-            )
-        outputs.append(out)
-
-    up = jnp.where(is_first, jnp.zeros((), bf16), four(cut(top, count - 1)))
-    in_grads, late = [], []
-    gain_sum = jnp.zeros((1, width), f32)
-    shift_sum = jnp.zeros((1, width), f32)
-    for moment in range(count + 1):
-        last = moment == count
-        tables, allowed, hidden, normed, kept, pre_act = stored[count - moment]
-        up_flat = flat(up)
-        grad_pre = settled(
-            gelu_grad(pre_act, mm(up_flat, fc_two, ((1,), (1,)))).astype(bf16)
-        )
-        grad_att = mm(up_flat, proj_dense, ((1,), (1,))).astype(bf16)
+        partial = (mm(attended, w_dense) + mm(activation, w_two)).astype(bf16)
+        return four(partial), (kept, pre_act)
+
+    def branch_backward(up, layer, stored):
+        kept, pre_act = stored
+        w_qkv, w_one, w_dense, w_two = layer[-1]
+        grad_pre = settled(gelu_grad(pre_act, mm(up, w_two, ((1,), (1,)))).astype(bf16))
+        grad_att = mm(up, w_dense, ((1,), (1,))).astype(bf16)
         pieces = attention_call(
             functools.partial(attention_backward_kernel, False),
             kept + [grad_att], tables, allowed, 3, 0,
         )
-        grad_normed = mm(grad_pre, fc_one, ((1,), (1,)))
+        grad_normed = mm(grad_pre, w_one, ((1,), (1,)))
         for which in range(3):
-            grad_normed = grad_normed + mm(
-                pieces[which], proj_qkv[which], ((1,), (1,))
-            )
-        args = [four(grad_normed.astype(bf16)), up, hidden, norm_gain]
-        outs = [sds(rows_shape, bf16), sds((1, width), f32), sds((1, width), f32)]
-        if last:
-            passed, g_gain, g_shift = relay_call(
-                backward_kernel, n, True, 3, args, outs, rows_shape
-            )
-        else:
-            args.append(
-                four(cut(top, count - 2 - moment))
-                if moment < count - 1
-                else jnp.zeros((group, n, share, width), bf16)
-            )
-            passed, g_gain, g_shift, up = relay_call(
-                backward_kernel, n, False, 2, args,
-                outs + [sds((group, n, share, width), bf16)], rows_shape,
-            )
-            up_rows = lax.dynamic_index_in_dim(up, lax.axis_index("tensor"), 1, keepdims=False)
-            normed_rows = lax.dynamic_index_in_dim(
-                normed, lax.axis_index("tensor"), 1, keepdims=False
-            )
-            late.append(gather(jnp.where(is_first, up_rows, normed_rows)))
-        in_grads.append(passed)
-        gain_sum = gain_sum + g_gain
-        shift_sum = shift_sum + g_shift
-    late = late[::-1]
+            grad_normed = grad_normed + mm(pieces[which], w_qkv[which], ((1,), (1,)))
+        return four(grad_normed.astype(bf16))
+
+    partial, stored_0 = branch_forward(flat(first_normed), layers[0])
+    out_0, normed = sum_call(
+        forward_kernel, n, False, 0,
+        [partial, x_rows, layers[0][2], layers[1][0], layers[1][1]],
+        [rows_out, full_out], rows_shape,
+    )
+    normed, early = settled((normed, early))
+    partial, stored_1 = branch_forward(flat(normed), layers[1])
+    (out_1,) = sum_call(
+        forward_kernel, n, True, 1, [partial, out_0, layers[1][2]], [rows_out], rows_shape
+    )
+    partial = branch_backward(flat(top), layers[1], stored_1)
+    grad_1, gain_1, shift_1, up = sum_call(
+        backward_kernel, n, False, 2, [partial, four(top), out_0, layers[1][0]],
+        [rows_out, line, line, full_out], rows_shape,
+    )
+    own = lambda x: lax.dynamic_index_in_dim(x, lax.axis_index("tensor"), 1, keepdims=False)
+    late = gather(jnp.where(is_first, grad_1, own(normed)))
+    partial = branch_backward(flat(up), layers[0], stored_0)
+    grad_0, gain_0, shift_0 = sum_call(
+        backward_kernel, n, True, 3, [partial, up, x_rows, layers[0][0]],
+        [rows_out, line, line], rows_shape,
+    )
+    gain_sum = jnp.where(is_first, gain_0, gain_1)
+    shift_sum = jnp.where(is_first, shift_0, shift_1)
+    cut = lambda x, i: x[i * group : (i + 1) * group]
 
     column = lax.axis_index("dp") * (width // n_dp)
     slice_of = lambda x: lax.dynamic_slice_in_dim(x, column, width // n_dp, 1)
     total = None
     for index in range(count):
-        now, then = cut(early, index), late[index]
+        now, then = cut(early, index), cut(late, index)
         blocks = group * n_dp
         normed_all = settled(jnp.where(is_first, now, then).reshape(blocks * rows, width))
         up_all = settled(jnp.where(is_first, then, now).reshape(blocks * rows, width))
@@ -610,13 +600,8 @@
         jnp.concatenate([gain_sum, shift_sum], axis=0), ("dp", "tensor"), 4, True
     )
 
-    layer_out = jnp.concatenate(
-        [jnp.where(is_first, outputs[i], outputs[i + 1]) for i in range(count)], axis=0
-    )
-    in_grad = jnp.concatenate(
-        [jnp.where(is_first, in_grads[count - i], in_grads[count - 1 - i]) for i in range(count)],
-        axis=0,
-    )
+    layer_out = jnp.where(is_first, out_0, out_1)
+    in_grad = jnp.where(is_first, grad_0, grad_1)
     return (
         layer_out[None],
         in_grad[None],

time: 607 us -> 618 us (1.018)
  waiting for transfers between devices: 10.8 us -> 77.6 us
  matrix products: 263 us -> 215 us
  Pallas kernels: 251 us -> 228 us
  local copies, waits for them, and re-layouts: 18.1 us -> 28.8 us
    all_gather x3 -> x2, waiting for transfers between devices: 10.8 us -> 74.4 us  [gather(): return lax.all_gather(x, ('dp', 'tensor'), axis=1, tiled=True)]
    dot_general x60 -> x48, matrix products: 263 us -> 215 us  [mm(): lax.dot_general(left, right, (dims, ((), ())), preferred_element_type=jnp...]
    dynamic_slice x0 -> x7, local copies, waits for them, and re-layouts: none -> 15.7 us  [the longest x6 14.6 us: half(): return lax.dynamic_slice_in_dim(x, which * size, size, axis)]
    pallas_call x8 -> x6, Pallas kernels: 85.8 us -> 73.4 us  [attention_call(): pl.pallas_call(kernel, grid=(blocks,), in_specs=[block] * len(arrays) + [...]
    pallas_call x6 -> x4, Pallas kernels: 146 us -> 137 us  [sum_call(): pl.pallas_call(functools.partial(kernel, n, last), out_shape=outs, in_spe...]
  transfers between devices with their start and end apart: 3 -> 7, of which waited for: 1 -> 3; matrix products, arithmetic and copies ran while one was open for 21% -> 12% of each run, Pallas kernels for 28% -> 17%
where the time goes in v3:
time: 618 us; the launch traced here: 610 us
  Pallas kernels  228 us (37%)
  matrix products  215 us (35%)
  waiting for transfers between devices  77.6 us (13%)
  other arithmetic  44.1 us (7%)
  local copies, waits for them, and re-layouts  28.8 us (5%)
  between operations  15.6 us (3%)
    dot_general x48, matrix products, mm(): lax.dot_general(left, right, (dims, ((), ())), preferred_element_type=jnp...  215 us
    pallas_call x4, Pallas kernels, sum_call(): pl.pallas_call(functools.partial(kernel, n, last), out_shape=outs, in_spe...  137 us
    all_gather x2, waiting for transfers between devices, gather(): return lax.all_gather(x, ('dp', 'tensor'), axis=1, tiled=True)  74.4 us
    pallas_call x6, Pallas kernels, attention_call(): pl.pallas_call(kernel, grid=(blocks,), in_specs=[block] * len(arrays) + [...  73.4 us
    pallas_call x2, Pallas kernels, small_exchange(): pl.pallas_call(functools.partial(exchange_kernel, axes, add), out_shape=j...  17.6 us
    dynamic_slice x6, local copies, waits for them, and re-layouts, half(): return lax.dynamic_slice_in_dim(x, which * size, size, axis)  14.6 us
  transfers between devices with their start and end apart: 7, of which 3 were waited for; matrix products, arithmetic and copies ran while one was open for 12% of the time, Pallas kernels for 17%

profile of v3, /device:TPU:0, one launch (start us, length us, event | category | flops | bytes accessed | tf_op | source)
XLA Modules:
  0.0 610.0 jit_solution(6134122944689672218)
XLA Ops:
  58.5 5.9 shard_map.203
  64.4 7.0 %multiply_convert_fusion.3 = (bf16[512,1024]{1,0:T(8,128)(2,1)S(1)}, f32[512,1024]{1,0:T(8,128)}) fusion(f32[1024]{0:T(1024)S(1)} %bitcast.334, bf16[512,2048]{1,0:T(8,128)(2,1)} %bitcast.300, bf16[2048,1024]{1,0:T(8,128)(2,1)} %collective-permute-done.3, pred[]{:T(512)S(6)} %eq.33, bf16[1,2048,2048]{2,1,0:T(8,128)(2,1)} %param.21, s32[]{:T(128)S(6)} %select_n.187), kind=kOutput, calls=%fused_computation.91 | convolution fusion | flops 2154823680 | bytes 13635589 | tf_op jit(solution)/shard_map/dot_general | solution.py:47
  76.9 60.6 %shard_map.204 = (bf16[4,32,2048]{2,1,0:T(8,128)(2,1)S(1)}, bf16[4,4,32,2048]{3,2,1,0:T(8,128)(2,1)S(1)}) custom-call(bf16[4,4,32,2048]{3,2,1,0:T(8,128)(2,1)S(1)} %bitcast.261, bf16[4,32,2048]{2,1,0:T(8,128)(2,1)S(1)} %constant_dynamic-slice_fusion.3.resid_ref.hidden_ref, f32[1,2048]{1,0:T(1,128)S(1)} %get-tuple-element.117.bias_ref, ...), custom_call_target="tpu_custom_call" | custom-call | tf_op jit(solution)/shard_map/pallas_call | solution.py:362
  138.9 19.2 %all-gather.3.cloned.1.call-done = bf16[4,512,2048]{2,1,0:T(8,128)(2,1)} async-done(((bf16[4,32,2048]{2,1,0:T(8,128)(2,1)}), bf16[4,512,2048]{2,1,0:T(8,128)(2,1)}) %all-gather.3.cloned.1.call-update) | async-done | bytes 8388624 | tf_op jit(solution)/shard_map/all_gather | solution.py:503
  170.4 7.2 %shard_map.207 = (bf16[512,256]{1,0:T(8,128)(2,1)}, bf16[512,256]{1,0:T(8,128)(2,1)}, bf16[512,256]{1,0:T(8,128)(2,1)}) custom-call(bf16[512,256]{1,0:T(8,128)(2,1)} %get-tuple-element.57.q_ref, bf16[512,256]{1,0:T(8,128)(2,1)} %get-tuple-element.58.k_ref, bf16[512,256]{1,0:T(8,128)(2,1)} %get-tuple-element.59.v_ref, ...), custom_call_target="tpu_custom_call" | custom-call | flops 335544320 | bytes 2097152 | tf_op jit(solution)/shard_map/pallas_call | solution.py:151
  179.8 7.5 %multiply_convert_fusion.2 = (bf16[512,1024]{1,0:T(8,128)(2,1)}, f32[512,1024]{1,0:T(8,128)S(1)}) fusion(f32[1024]{0:T(1024)S(1)} %bitcast.336, bf16[512,2048]{1,0:T(8,128)(2,1)S(1)} %bitcast.270, bf16[2048,1024]{1,0:T(8,128)(2,1)} %collective-permute-done.3, pred[]{:T(512)S(6)} %eq.73, bf16[1,2048,2048]{2,1,0:T(8,128)(2,1)} %param.21, s32[]{:T(128)S(6)} %select_n.187), kind=kOutput, calls=%fused_computation.90 | convolution fusion | flops 2154823680 | bytes 13635589 | tf_op jit(solution)/shard_map/dot_general | solution.py:47
  187.3 7.2 %fusion.43 = bf16[512,1024]{1,0:T(8,128)(2,1)S(1)} fusion(f32[512,1024]{1,0:T(8,128)S(1)} %get-tuple-element.154, bf16[512,2048]{1,0:T(8,128)(2,1)S(1)} %bitcast.259, bf16[1024,2048]{1,0:T(8,128)(2,1)} %collective-permute-done.4, pred[]{:T(512)S(6)} %eq.73, bf16[1,2048,2048]{2,1,0:T(8,128)(2,1)} %param.23, s32[]{:T(128)S(6)} %select_n.187, ...), kind=kOutput, calls=%fused_computation.73 | convolution fusion | flops 2160590848 | bytes 13635589 | tf_op jit(solution)/shard_map/dot_general | solution.py:47
  200.7 33.3 %shard_map.208 = (bf16[4,32,2048]{2,1,0:T(8,128)(2,1)S(1)}, f32[1,2048]{1,0:T(1,128)S(1)}, f32[1,2048]{1,0:T(1,128)S(1)}, bf16[4,4,32,2048]{3,2,1,0:T(8,128)(2,1)S(1)}) custom-call(bf16[4,4,32,2048]{3,2,1,0:T(8,128)(2,1)S(1)} %bitcast.262, bf16[4,4,32,2048]{3,2,1,0:T(8,128)(2,1)S(1)} %bitcast.260, ...), custom_call_target="tpu_custom_call" | custom-call | tf_op jit(solution)/shard_map/pallas_call | solution.py:362
  236.9 7.2 %shard_map.209 = (bf16[512,256]{1,0:T(8,128)(2,1)}, bf16[512,256]{1,0:T(8,128)(2,1)}, bf16[512,256]{1,0:T(8,128)(2,1)}) custom-call(bf16[512,256]{1,0:T(8,128)(2,1)} %get-tuple-element.64.q_ref, bf16[512,256]{1,0:T(8,128)(2,1)} %get-tuple-element.65.k_ref, bf16[512,256]{1,0:T(8,128)(2,1)} %get-tuple-element.66.v_ref, ...), custom_call_target="tpu_custom_call" | custom-call | flops 335544320 | bytes 2097152 | tf_op jit(solution)/shard_map/pallas_call | solution.py:151
  246.3 5.9 fusion.36
  256.3 22.9 %shard_map.210 = (bf16[4,32,2048]{2,1,0:T(8,128)(2,1)S(1)}, f32[1,2048]{1,0:T(1,128)S(1)}, f32[1,2048]{1,0:T(1,128)S(1)}) custom-call(bf16[4,4,32,2048]{3,2,1,0:T(8,128)(2,1)S(1)} %bitcast.263, bf16[4,4,32,2048]{3,2,1,0:T(8,128)(2,1)S(1)} %copy-done.1, bf16[4,32,2048]{2,1,0:T(8,128)(2,1)S(1)} %constant_dynamic-slice_fusion.3.resid_ref.hidden_ref, ...), custom_call_target="tpu_custom_call" | custom-call | tf_op jit(solution)/shard_map/pallas_call | solution.py:362
  281.4 6.8 %shard_map.212 = s32[4,4,128]{2,1,0:T(4,128)} custom-call(s32[4,128]{1,0:T(4,128)} %x_ref.1), custom_call_target="tpu_custom_call" | custom-call | tf_op jit(solution)/shard_map/pallas_call | solution.py:423
  299.9 10.8 %shard_map.211 = f32[2,2048]{1,0:T(2,128)} custom-call(f32[2,2048]{1,0:T(2,128)} %pad_maximum_fusion.4.x_ref), custom_call_target="tpu_custom_call" | custom-call | tf_op jit(solution)/shard_map/pallas_call | solution.py:423
  310.7 6.3 %fusion.95 = f32[512,2048]{1,0:T(8,128)S(1)} fusion(bf16[512,1024]{1,0:T(8,128)(2,1)} %get-tuple-element.153, bf16[1024,2048]{1,0:T(8,128)(2,1)} %collective-permute-done.4, pred[]{:T(512)S(6)} %eq.73, bf16[1,2048,2048]{2,1,0:T(8,128)(2,1)} %param.23, s32[]{:T(128)S(6)} %select_n.187), kind=kOutput, calls=%fused_computation.127 | convolution fusion | flops 2149580800 | bytes 13631493 | tf_op jit(solution)/shard_map/dot_general | solution.py:47
  319.1 19.8 %shard_map.206 = bf16[4,32,2048]{2,1,0:T(8,128)(2,1)S(1)} custom-call(bf16[4,4,32,2048]{3,2,1,0:T(8,128)(2,1)S(1)} %bitcast.264, bf16[4,32,2048]{2,1,0:T(8,128)(2,1)S(1)} %get-tuple-element.53.resid_ref.hidden_ref, f32[1,2048]{1,0:T(1,128)S(1)} %get-tuple-element.113.bias_ref), custom_call_target="tpu_custom_call" | custom-call | tf_op jit(solution)/shard_map/pallas_call | solution.py:362
  340.4 55.2 %all-gather.5.cloned.1.call-done = bf16[4,512,2048]{2,1,0:T(8,128)(2,1)} async-done(((bf16[4,32,2048]{2,1,0:T(8,128)(2,1)}), bf16[4,512,2048]{2,1,0:T(8,128)(2,1)}) %all-gather.5.cloned.1.call-update) | async-done | bytes 8388624 | tf_op jit(solution)/shard_map/all_gather | solution.py:503
  395.5 8.7 %broadcast_select_fusion = (bf16[2,512,2048]{2,1,0:T(8,128)(2,1)S(1)}, bf16[2,512,2048]{2,1,0:T(8,128)(2,1)S(1)}, bf16[2,512,2048]{2,1,0:T(8,128)(2,1)S(1)}, bf16[2,512,2048]{2,1,0:T(8,128)(2,1)}) fusion(pred[]{:T(512)S(6)} %eq.33, bf16[4,512,2048]{2,1,0:T(8,128)(2,1)} %all-gather.5.cloned.1.call-done, bf16[4,512,2048]{2,1,0:T(8,128)(2,1)} %all-gather.3.cloned.1.call-done), kind=kLoop, calls=%fused_computation.48 | loop fusion | flops 8388608 | bytes 33554432 | tf_op jit(solution)/shard_map/jit(_where)/select_n | solution.py:572
  404.3 10.9 %fusion.54.k_ref = f32[1024,512]{1,0:T(8,128)} fusion(bf16[1024,2048]{1,0:T(8,128)(2,1)} %bitcast.292, bf16[1,3,2048,512]{3,2,1,0:T(8,128)(2,1)} %param.17), kind=kOutput, calls=%fused_computation.84 | convolution fusion | flops 2147483648 | bytes 8388608 | tf_op jit(solution)/shard_map/dot_general | solution.py:47
  444.0 11.0 %fusion.14 = f32[1024,2048]{1,0:T(8,128)} fusion(bf16[1024,2048]{1,0:T(8,128)(2,1)S(1)} %bitcast.297, bf16[1,2048,2048]{2,1,0:T(8,128)(2,1)S(1)} %bitcast.309), kind=kOutput, calls=%fused_computation.18 | convolution fusion | flops 8589934592 | bytes 20971520 | tf_op jit(solution)/shard_map/dot_general | solution.py:47
  455.1 20.1 %fusion.160 = (f32[2048]{0:T(1024)S(1)}, bf16[1024,2048]{1,0:T(8,128)(2,1)}) fusion(f32[1024,2048]{1,0:T(8,128)} %fusion.14, f32[2048]{0:T(1024)S(1)} %bitcast.331, bf16[1024,2048]{1,0:T(8,128)(2,1)S(1)} %bitcast.279, bf16[1,2048,2048]{2,1,0:T(8,128)(2,1)} %param.23), kind=kOutput, calls=%fused_computation.260 | convolution fusion | flops 8636069888 | bytes 25182208 | tf_op jit(solution)/shard_map/dot_general | solution.py:47
  475.2 20.7 %multiply_convert_fusion = (bf16[1024,2048]{1,0:T(8,128)(2,1)}, bf16[1024,2048]{1,0:T(8,128)(2,1)}, f32[1024,2048]{1,0:T(8,128)}) fusion(f32[2048]{0:T(1024)S(1)} %bitcast.332, f32[1024,2048]{1,0:T(8,128)} %fusion.14, bf16[1024,2048]{1,0:T(8,128)(2,1)S(1)} %bitcast.285, bf16[1,2048,2048]{2,1,0:T(8,128)(2,1)} %param.21), kind=kOutput, calls=%fused_computation.24 | convolution fusion | flops 8631877632 | bytes 37756928 | tf_op jit(solution)/shard_map/dot_general | solution.py:47
  495.9 23.6 %shard_map.213 = (bf16[1024,512]{1,0:T(8,128)(2,1)}, bf16[1024,512]{1,0:T(8,128)(2,1)}, bf16[1024,512]{1,0:T(8,128)(2,1)}, bf16[1024,512]{1,0:T(8,128)(2,1)}, f32[1,512]{1,0:T(1,128)}, /*index=5*/f32[1,512]{1,0:T(1,128)}) custom-call(f32[1024,512]{1,0:T(8,128)} %fusion.66.q_ref, f32[1024,512]{1,0:T(8,128)} %fusion.54.k_ref, f32[1024,512]{1,0:T(8,128)} %fusion.72.v_ref, ...), custom_call_target="tpu_custom_call" | custom-call | flops 1342177280 | bytes 8388608 | tf_op jit(solution)/shard_map/pallas_call | solution.py:151
  532.8 20.5 %fusion.159 = (f32[2048]{0:T(1024)S(1)}, bf16[1024,2048]{1,0:T(8,128)(2,1)}) fusion(f32[1024,2048]{1,0:T(8,128)} %get-tuple-element.157, f32[2048]{0:T(1024)S(1)} %bitcast.333, bf16[1024,2048]{1,0:T(8,128)(2,1)S(1)} %bitcast.274, bf16[1,2048,2048]{2,1,0:T(8,128)(2,1)} %param.23), kind=kOutput, calls=%fused_computation.259 | convolution fusion | flops 8636069888 | bytes 25182208 | tf_op jit(solution)/shard_map/dot_general | solution.py:47
  557.8 23.7 %shard_map.214 = (bf16[1024,512]{1,0:T(8,128)(2,1)}, bf16[1024,512]{1,0:T(8,128)(2,1)}, bf16[1024,512]{1,0:T(8,128)(2,1)}, bf16[1024,512]{1,0:T(8,128)(2,1)}, f32[1,512]{1,0:T(1,128)}, /*index=5*/f32[1,512]{1,0:T(1,128)}) custom-call(f32[1024,512]{1,0:T(8,128)} %fusion.69.q_ref, f32[1024,512]{1,0:T(8,128)} %fusion.52.k_ref, f32[1024,512]{1,0:T(8,128)} %fusion.75.v_ref, ...), custom_call_target="tpu_custom_call" | custom-call | flops 1342177280 | bytes 8388608 | tf_op jit(solution)/shard_map/pallas_call | solution.py:151
  (252 shorter events, 172.6 us)
Async XLA Ops:
  7.2 8.4 %copy-start.35 = (s32[4,128]{1,0:T(4,128)S(1)}, s32[4,128]{1,0:T(4,128)}, u32[]{:S(2)}) copy-start(s32[4,128]{1,0:T(4,128)} %x_ref.1) | copy-start | bytes 6148
  7.2 150.9 %all-gather.3.cloned.1.call-start = ((), (), s32[]{:S(2)}) async-start(), calls=%async_computation | async-start | bytes 8912896 | tf_op jit(solution)/shard_map/all_gather | solution.py:503
  7.2 8.4 %copy-start.28 = (bf16[4,128,2048]{2,1,0:T(8,128)(2,1)S(1)}, bf16[4,128,2048]{2,1,0:T(8,128)(2,1)}, u32[]{:S(2)}) copy-start(bf16[4,128,2048]{2,1,0:T(8,128)(2,1)} %param.13) | copy-start | bytes 6291460
  10.9 5.0 collective-permute-start
  20.7 374.8 %all-gather.5.cloned.1.call-start = ((), (), s32[]{:S(2)}) async-start(), calls=%async_computation.1 | async-start | bytes 8912896 | tf_op jit(solution)/shard_map/all_gather | solution.py:503
  25.4 39.0 %collective-permute-start.3 = (bf16[2048,1024]{1,0:T(8,128)(2,1)}, bf16[2048,1024]{1,0:T(8,128)(2,1)}, u32[]{:S(2)}, u32[]{:S(2)}) collective-permute-start(bf16[2048,1024]{1,0:T(8,128)(2,1)} %dynamic-slice_bitcast_fusion.1), channel_id=1, source_target_pairs={{0,16},{16,0},{1,17},{17,1},{2,18},{18,2},{3,19},{19,3},{4,20},{20... | collective-permute-start | bytes 12582920 | tf_op jit(solution)/shard_map/ppermute | solution.py:464
  30.2 41.2 %collective-permute-start.4 = (bf16[1024,2048]{1,0:T(8,128)(2,1)}, bf16[1024,2048]{1,0:T(8,128)(2,1)}, u32[]{:S(2)}, u32[]{:S(2)}) collective-permute-start(bf16[1024,2048]{1,0:T(8,128)(2,1)} %dynamic-slice_bitcast_fusion), channel_id=1, source_target_pairs={{0,16},{16,0},{1,17},{17,1},{2,18},{18,2},{3,19},{19,3},{4,20},{20... | collective-permute-start | bytes 12582920 | tf_op jit(solution)/shard_map/ppermute | solution.py:464
  34.8 13.1 %collective-permute-start.1 = (bf16[3,2048,256]{2,1,0:T(8,128)(2,1)}, bf16[3,2048,256]{2,1,0:T(8,128)(2,1)}, u32[]{:S(2)}, u32[]{:S(2)}) collective-permute-start(bf16[3,2048,256]{2,1,0:T(8,128)(2,1)} %dynamic-slice_bitcast_fusion.2), channel_id=1, source_target_pairs={{0,16},{16,0},{1,17},{17,1},{2,18},{18,2},{3,19},{19,3},{4,20},{20... | collective-permute-start | bytes 9437192 | tf_op jit(solution)/shard_map/ppermute | solution.py:464
  36.0 9.0 %collective-permute-start.2 = (bf16[256,2048]{1,0:T(8,128)(2,1)}, bf16[256,2048]{1,0:T(8,128)(2,1)}, u32[]{:S(2)}, u32[]{:S(2)}) collective-permute-start(bf16[256,2048]{1,0:T(8,128)(2,1)} %dynamic-slice_bitcast_fusion.3), channel_id=1, source_target_pairs={{0,16},{16,0},{1,17},{17,1},{2,18},{18,2},{3,19},{19,3},{4,20},{20... | collective-permute-start | bytes 3145736 | tf_op jit(solution)/shard_map/ppermute | solution.py:464
  179.8 15.4 %slice-start.2 = ((s8[8388608]{0:T(1024)(128)(4,1)}), s8[4194304]{0:T(1024)(128)(4,1)S(1)}, s32[]{:S(2)}) async-start(s8[8388608]{0:T(1024)(128)(4,1)} %bitcast.304), calls=%async_computation.4 | async-start | bytes 8388608
  187.3 7.9 %slice-start.3 = ((s8[8388608]{0:T(1024)(128)(4,1)}), s8[4194304]{0:T(1024)(128)(4,1)S(1)}, s32[]{:S(2)}) async-start(s8[8388608]{0:T(1024)(128)(4,1)} %bitcast.304), calls=%async_computation.5 | async-start | bytes 8388608
  200.7 34.7 %copy-start.21 = (bf16[1,512,2048]{2,1,0:T(8,128)(2,1)S(1)}, bf16[1,512,2048]{2,1,0:T(8,128)(2,1)}, u32[]{:S(2)}) copy-start(bf16[1,512,2048]{2,1,0:T(8,128)(2,1)} %param.19) | copy-start | bytes 6291460
  236.9 9.4 %copy-start.1 = (bf16[4,4,32,2048]{3,2,1,0:T(8,128)(2,1)S(1)}, bf16[4,4,32,2048]{3,2,1,0:T(8,128)(2,1)}, u32[]{:S(2)}) copy-start(bf16[4,4,32,2048]{3,2,1,0:T(8,128)(2,1)} %copy-done) | copy-start | bytes 6291460
  244.0 8.9 %slice-start.4 = ((s8[8388608]{0:T(1024)(128)(4,1)}), s8[4194304]{0:T(1024)(128)(4,1)S(1)}, s32[]{:S(2)}) async-start(s8[8388608]{0:T(1024)(128)(4,1)} %bitcast.306), calls=%async_computation.6 | async-start | bytes 8388608
  256.3 23.0 %copy-start.3 = (bf16[4,32,2048]{2,1,0:T(8,128)(2,1)S(1)}, bf16[4,32,2048]{2,1,0:T(8,128)(2,1)}, u32[]{:S(2)}) copy-start(bf16[4,32,2048]{2,1,0:T(8,128)(2,1)} %copy-done.2) | copy-start | bytes 1572868
  317.0 21.9 %copy-start.36 = (f32[2,2048]{1,0:T(2,128)S(1)}, f32[2,2048]{1,0:T(2,128)}, u32[]{:S(2)}) copy-start(f32[2,2048]{1,0:T(2,128)} %shard_map.211) | copy-start | bytes 49156
  404.2 37.9 %copy-start.7 = (bf16[2,512,2048]{2,1,0:T(8,128)(2,1)}, bf16[2,512,2048]{2,1,0:T(8,128)(2,1)S(1)}, u32[]{:S(2)}) copy-start(bf16[2,512,2048]{2,1,0:T(8,128)(2,1)S(1)} %get-tuple-element.93) | copy-start | bytes 12582916
  404.2 50.9 %copy-start.10 = (bf16[2,512,2048]{2,1,0:T(8,128)(2,1)}, bf16[2,512,2048]{2,1,0:T(8,128)(2,1)S(1)}, u32[]{:S(2)}) copy-start(bf16[2,512,2048]{2,1,0:T(8,128)(2,1)S(1)} %get-tuple-element.94) | copy-start | bytes 12582916
  404.2 70.9 %copy-start.16 = (bf16[2,512,2048]{2,1,0:T(8,128)(2,1)}, bf16[2,512,2048]{2,1,0:T(8,128)(2,1)S(1)}, u32[]{:S(2)}) copy-start(bf16[2,512,2048]{2,1,0:T(8,128)(2,1)S(1)} %get-tuple-element.95) | copy-start | bytes 12582916
  404.2 10.9 %copy-start.24 = (bf16[2,512,2048]{2,1,0:T(8,128)(2,1)S(1)}, bf16[2,512,2048]{2,1,0:T(8,128)(2,1)}, u32[]{:S(2)}) copy-start(bf16[2,512,2048]{2,1,0:T(8,128)(2,1)} %get-tuple-element.96) | copy-start | bytes 12582916
  404.2 16.3 %slice-start = ((s8[6291456]{0:T(1024)(128)(4,1)}), s8[4194304]{0:T(1024)(128)(4,1)S(1)}, s32[]{:S(2)}) async-start(s8[6291456]{0:T(1024)(128)(4,1)} %bitcast.290), calls=%async_computation.2 | async-start | bytes 8388608
  435.1 8.9 %slice-start.6 = ((s8[8388608]{0:T(1024)(128)(4,1)}), s8[4194304]{0:T(1024)(128)(4,1)S(1)}, s32[]{:S(2)}) async-start(s8[8388608]{0:T(1024)(128)(4,1)} %bitcast.308), calls=%async_computation.8 | async-start | bytes 8388608
  444.0 11.1 %copy-start.38 = (f32[1,2048]{1,0:T(1,128)S(1)}, f32[1,2048]{1,0:T(1,128)}, u32[]{:S(2)}) copy-start(f32[1,2048]{1,0:T(1,128)} %param.22) | copy-start | bytes 24580
  532.8 20.5 %copy-start.50 = (bf16[1024,2048]{1,0:T(8,128)(2,1)S(1)}, bf16[1024,2048]{1,0:T(8,128)(2,1)}, u32[]{:S(2)}) copy-start(bf16[1024,2048]{1,0:T(8,128)(2,1)} %get-tuple-element.126) | copy-start | bytes 12582916
  (43 other events, 169.1 us)
Sparse Core Ops, SparseCore 0:
  20.8 137.2 all-gather.2
  281.6 113.9 all-gather.4

commit v4 on v3

--- a/solution.py
+++ b/solution.py
@@ -59,46 +59,51 @@
 def softmax_of(query, key, allowed):
     scores = mm(query, key, ((1,), (1,))) * HEAD_DIM ** (-0.5)
     scores = jnp.where(allowed, scores, MASKED)
-    row_max = jnp.max(scores, axis=-1, keepdims=True)
-    log_total = row_max + jnp.log(jnp.sum(jnp.exp(scores - row_max), axis=-1, keepdims=True))
-    return jnp.exp(scores - log_total)
-
-
-def lane_masks(lanes):
-    lane = lax.broadcasted_iota(jnp.int32, (1, lanes), 1)
-    return [
-        jnp.where(lane // HEAD_DIM == h, 1.0, 0.0).astype(jnp.bfloat16)
-        for h in range(lanes // HEAD_DIM)
-    ]
+    exps = jnp.exp(scores - jnp.max(scores, axis=-1, keepdims=True))
+    return exps * (1.0 / jnp.sum(exps, axis=-1, keepdims=True))
+
+
+def stacked_heads(x):
+    lane = lax.broadcasted_iota(jnp.int32, (1, x.shape[-1]), 1) // HEAD_DIM
+    return jnp.concatenate(
+        [
+            x * jnp.where(lane == h, 1.0, 0.0).astype(x.dtype)
+            for h in range(x.shape[-1] // HEAD_DIM)
+        ],
+        axis=0,
+    )
+
+
+def side_by_side(x, rows):
+    lane = lax.broadcasted_iota(jnp.int32, (1, x.shape[-1]), 1) // HEAD_DIM
+    out = x[:rows]
+    for h in range(1, x.shape[0] // rows):
+        out = jnp.where(lane == h, x[h * rows : (h + 1) * rows], out)
+    return out
 
 
 def attention_forward_kernel(qf_ref, kf_ref, vf_ref, table_ref, allowed_ref, q_ref, k_ref, v_ref, out_ref):
     bf16 = jnp.bfloat16
     table = table_ref[0]
-    lanes = table.shape[-1]
-    allowed = allowed_ref[0] > 0.5
-    masks = lane_masks(lanes)
-    v_ref[...] = vf_ref[...].astype(bf16)
+    rows, lanes = table.shape[-2:]
+    allowed = jnp.concatenate([allowed_ref[0] > 0.5] * (lanes // HEAD_DIM), axis=0)
     for pair in range(qf_ref.shape[-1] // lanes):
         at = slice(pair * lanes, (pair + 1) * lanes)
         query = rotated(qf_ref[:, at], table, 1.0).astype(bf16)
         key = rotated(kf_ref[:, at], table, 1.0).astype(bf16)
+        value = vf_ref[:, at].astype(bf16)
         q_ref[:, at] = query
         k_ref[:, at] = key
-        value = v_ref[:, at]
-        total = 0.0
-        for mask in masks:
-            prob = softmax_of(query * mask, key, allowed).astype(bf16)
-            total = total + mm(prob, value * mask)
-        out_ref[:, at] = total.astype(bf16)
+        v_ref[:, at] = value
+        prob = softmax_of(stacked_heads(query), key, allowed).astype(bf16)
+        out_ref[:, at] = side_by_side(mm(prob, value), rows).astype(bf16)
 
 
 def attention_backward_kernel(again, q_ref, k_ref, v_ref, ga_ref, table_ref, allowed_ref, *outs):
     bf16 = jnp.bfloat16
     table = table_ref[0]
-    lanes = table.shape[-1]
-    allowed = allowed_ref[0] > 0.5
-    masks = lane_masks(lanes)
+    rows, lanes = table.shape[-2:]
+    allowed = jnp.concatenate([allowed_ref[0] > 0.5] * (lanes // HEAD_DIM), axis=0)
     scale = HEAD_DIM ** (-0.5)
     if again:
         gq_ref, gk_ref, gv_ref, out_ref, sq_ref, sv_ref = outs
@@ -117,27 +122,23 @@
             value = v_ref[:, at].astype(bf16)
         else:
             query, key, value = q_ref[:, at], k_ref[:, at], v_ref[:, at]
-        grad = ga_ref[:, at]
-        total = g_query = g_key = g_value = 0.0
-        for mask in masks:
-            prob_f = softmax_of(query * mask, key, allowed)
-            prob_b = prob_f.astype(bf16)
-            grad_m = grad * mask
-            grad_prob = mm(grad_m, value, ((1,), (1,)))
-            row_dot = jnp.sum(prob_f * grad_prob, axis=-1, keepdims=True)
-            grad_score = (prob_f * (grad_prob - row_dot)).astype(bf16)
-            if again:
-                total = total + mm(prob_b, value * mask)
-            g_query = g_query + mm(grad_score, key * mask)
-            g_key = g_key + mm(grad_score, query * mask, ((0,), (0,)))
-            g_value = g_value + mm(prob_b, grad_m, ((0,), (0,)))
+        queries = stacked_heads(query)
+        grads = stacked_heads(ga_ref[:, at])
+        prob_f = softmax_of(queries, key, allowed)
+        prob_b = prob_f.astype(bf16)
+        grad_prob = mm(grads, value, ((1,), (1,)))
+        row_dot = jnp.sum(prob_f * grad_prob, axis=-1, keepdims=True)
+        grad_score = (prob_f * (grad_prob - row_dot)).astype(bf16)
+        g_query = side_by_side(mm(grad_score, key), rows)
+        g_key = mm(grad_score, queries, ((0,), (0,)))
+        g_value = mm(prob_b, grads, ((0,), (0,)))
         g_query = rotated(g_query * scale, table, -1.0)
         g_key = rotated(g_key * scale, table, -1.0)
         gq_ref[:, at] = g_query.astype(bf16)
         gk_ref[:, at] = g_key.astype(bf16)
         gv_ref[:, at] = g_value.astype(bf16)
         if again:
-            out_ref[:, at] = total.astype(bf16)
+            out_ref[:, at] = side_by_side(mm(prob_b, value), rows).astype(bf16)
             sq_ref[:, at] += jnp.sum(g_query, axis=0, keepdims=True)
             sv_ref[:, at] += jnp.sum(g_value, axis=0, keepdims=True)
 
@@ -449,7 +450,7 @@
     n = lax.axis_size("tensor")
     n_dp = lax.axis_size("dp")
     share = rows // n
-    group = 2 if micro % 2 == 0 else 1
+    group = micro
     count = micro // group
     sec = lax.axis_index("section")
     is_first = sec == 0
@@ -502,7 +503,9 @@
     def gather(x):
         return lax.all_gather(x, ("dp", "tensor"), axis=1, tiled=True)
 
-    early = gather(jnp.where(is_first, own_rows(first_normed), own_rows(top)))
+    early = lax.all_gather(
+        jnp.where(is_first, first_normed, top), "dp", axis=1, tiled=True
+    )
 
     four = lambda x: x.reshape(micro, n, share, width)
     flat = lambda x: x.reshape(micro * rows, width)
@@ -541,7 +544,6 @@
         [partial, x_rows, layers[0][2], layers[1][0], layers[1][1]],
         [rows_out, full_out], rows_shape,
     )
-    normed, early = settled((normed, early))
     partial, stored_1 = branch_forward(flat(normed), layers[1])
     (out_1,) = sum_call(
         forward_kernel, n, True, 1, [partial, out_0, layers[1][2]], [rows_out], rows_shape
@@ -552,7 +554,9 @@
         [rows_out, line, line, full_out], rows_shape,
     )
     own = lambda x: lax.dynamic_index_in_dim(x, lax.axis_index("tensor"), 1, keepdims=False)
-    late = gather(jnp.where(is_first, grad_1, own(normed)))
+    late_rows = jnp.where(is_first, grad_1, own(normed))
+    up, late_rows, early = settled((up, late_rows, early))
+    late = gather(late_rows)
     partial = branch_backward(flat(up), layers[0], stored_0)
     grad_0, gain_0, shift_0 = sum_call(
         backward_kernel, n, True, 3, [partial, up, x_rows, layers[0][0]],

time: 618 us -> 527 us (0.85)
  waiting for transfers between devices: 77.6 us -> 9.19 us
  Pallas kernels: 228 us -> 219 us
  matrix products: 215 us -> 207 us
    all_gather x2 -> x1, waiting for transfers between devices: 74.4 us -> 9.14 us  [gather(): return lax.all_gather(x, ('dp', 'tensor'), axis=1, tiled=True)]
    pallas_call x6 -> x5, Pallas kernels: 73.4 us -> 65 us  [attention_call(): pl.pallas_call(kernel, grid=(blocks,), in_specs=[block] * len(arrays) + [...]
    dot_general x48 -> x36, matrix products: 215 us -> 207 us  [mm(): lax.dot_general(left, right, (dims, ((), ())), preferred_element_type=jnp...]
  transfers between devices with their start and end apart: 7 -> 7, of which waited for: 3 -> 1; matrix products, arithmetic and copies ran while one was open for 12% -> 25% of each run, Pallas kernels for 17% -> 35%
where the time goes in v4:
time: 527 us; the launch traced here: 518 us
  Pallas kernels  219 us (42%)
  matrix products  207 us (39%)
  other arithmetic  41.2 us (8%)
  local copies, waits for them, and re-layouts  25.9 us (5%)
  between operations  15.1 us (3%)
  waiting for transfers between devices  9.19 us (2%)
    dot_general x36, matrix products, mm(): lax.dot_general(left, right, (dims, ((), ())), preferred_element_type=jnp...  207 us
    pallas_call x4, Pallas kernels, sum_call(): pl.pallas_call(functools.partial(kernel, n, last), out_shape=outs, in_spe...  131 us
    pallas_call x5, Pallas kernels, attention_call(): pl.pallas_call(kernel, grid=(blocks,), in_specs=[block] * len(arrays) + [...  65 us
    pallas_call x2, Pallas kernels, small_exchange(): pl.pallas_call(functools.partial(exchange_kernel, axes, add), out_shape=j...  22.6 us
    dynamic_slice x6, local copies, waits for them, and re-layouts, half(): return lax.dynamic_slice_in_dim(x, which * size, size, axis)  13.5 us
  transfers between devices with their start and end apart: 7, of which 1 were waited for; matrix products, arithmetic and copies ran while one was open for 25% of the time, Pallas kernels for 35%

profile of v4, /device:TPU:0, one launch (start us, length us, event | category | flops | bytes accessed | tf_op | source)
XLA Modules:
  0.0 518.3 jit_solution(14167866048736963456)
XLA Ops:
  40.7 6.3 %bitcast_select_fusion.4 = (bf16[3,2048,256]{2,1,0:T(8,128)(2,1)}, bf16[3,2048,256]{2,1,0:T(8,128)(2,1)S(1)}) fusion(bf16[3,2048,256]{2,1,0:T(8,128)(2,1)} %collective-permute-done.1, pred[]{:T(512)S(6)} %eq.57, bf16[1,3,2048,512]{3,2,1,0:T(8,128)(2,1)} %param.17, s32[]{:T(128)S(6)} %select_n.165, pred[]{:T(512)S(6)} %eq.25), kind=kLoop, calls=%fused_computation.38 | loop fusion | flops 3145728 | bytes 12582918 | tf_op jit(solution)/shard_map/jit(_where)/select_n | solution.py:475
  51.8 5.9 %shard_map.203 = (bf16[512,256]{1,0:T(8,128)(2,1)}, bf16[512,256]{1,0:T(8,128)(2,1)}, bf16[512,256]{1,0:T(8,128)(2,1)}, bf16[512,256]{1,0:T(8,128)(2,1)}) custom-call(f32[512,256]{1,0:T(8,128)} %convolution_add_fusion.5.qf_ref, f32[512,256]{1,0:T(8,128)} %fusion.60.kf_ref, f32[512,256]{1,0:T(8,128)} %convolution_add_fusion.4.vf_ref, ...), custom_call_target="tpu_custom_call" | custom-call | flops 335544320 | bytes 2097152 | tf_op jit(solution)/shard_map/pallas_call | solution.py:152
  57.8 7.1 %multiply_convert_fusion.2 = (bf16[512,1024]{1,0:T(8,128)(2,1)S(1)}, f32[512,1024]{1,0:T(8,128)}) fusion(f32[1024]{0:T(1024)S(1)} %bitcast.260, bf16[512,2048]{1,0:T(8,128)(2,1)} %bitcast.237, bf16[2048,1024]{1,0:T(8,128)(2,1)} %collective-permute-done.3, pred[]{:T(512)S(6)} %eq.25, bf16[1,2048,2048]{2,1,0:T(8,128)(2,1)} %param.21, s32[]{:T(128)S(6)} %select_n.172), kind=kOutput, calls=%fused_computation.71 | convolution fusion | flops 2154823680 | bytes 13635589 | tf_op jit(solution)/shard_map/dot_general | solution.py:47
  70.6 37.5 %shard_map.204 = (bf16[4,32,2048]{2,1,0:T(8,128)(2,1)S(1)}, bf16[4,4,32,2048]{3,2,1,0:T(8,128)(2,1)S(1)}) custom-call(bf16[4,4,32,2048]{3,2,1,0:T(8,128)(2,1)S(1)} %bitcast.202, bf16[4,32,2048]{2,1,0:T(8,128)(2,1)S(1)} %constant_dynamic-slice_fusion.3.resid_ref.hidden_ref, f32[1,2048]{1,0:T(1,128)S(1)} %get-tuple-element.98.bias_ref, ...), custom_call_target="tpu_custom_call" | custom-call | tf_op jit(solution)/shard_map/pallas_call | solution.py:363
  108.1 6.8 %multiply_convert_fusion.1 = (bf16[512,1024]{1,0:T(8,128)(2,1)}, f32[512,1024]{1,0:T(8,128)S(1)}) fusion(f32[1024]{0:T(1024)S(1)} %bitcast.262, bf16[512,2048]{1,0:T(8,128)(2,1)S(1)} %bitcast.211, bf16[2048,1024]{1,0:T(8,128)(2,1)} %collective-permute-done.3, pred[]{:T(512)S(6)} %eq.57, bf16[1,2048,2048]{2,1,0:T(8,128)(2,1)S(1)} %bitcast.232, s32[]{:T(128)S(6)} %select_n.172), kind=kOutput, calls=%fused_computation.70 | convolution fusion | flops 2154823680 | bytes 13635589 | tf_op jit(solution)/shard_map/dot_general | solution.py:47
  115.0 18.1 %fusion.31 = bf16[512,1024]{1,0:T(8,128)(2,1)} fusion(f32[512,1024]{1,0:T(8,128)S(1)} %get-tuple-element.119, bf16[512,2048]{1,0:T(8,128)(2,1)S(1)} %bitcast.207, bf16[1024,2048]{1,0:T(8,128)(2,1)} %collective-permute-done.4, pred[]{:T(512)S(6)} %eq.57, bf16[1,2048,2048]{2,1,0:T(8,128)(2,1)S(1)} %bitcast.234, s32[]{:T(128)S(6)} %select_n.172, ...), kind=kOutput, calls=%fused_computation.61 | convolution fusion | flops 2160590848 | bytes 13635589 | tf_op jit(solution)/shard_map/dot_general | solution.py:47
  143.3 6.5 %shard_map.207 = (bf16[512,256]{1,0:T(8,128)(2,1)}, bf16[512,256]{1,0:T(8,128)(2,1)}, bf16[512,256]{1,0:T(8,128)(2,1)}) custom-call(bf16[512,256]{1,0:T(8,128)(2,1)} %get-tuple-element.49.q_ref, bf16[512,256]{1,0:T(8,128)(2,1)} %get-tuple-element.50.k_ref, bf16[512,256]{1,0:T(8,128)(2,1)} %get-tuple-element.51.v_ref, ...), custom_call_target="tpu_custom_call" | custom-call | flops 335544320 | bytes 2097152 | tf_op jit(solution)/shard_map/pallas_call | solution.py:152
  160.0 33.4 %shard_map.208 = (bf16[4,32,2048]{2,1,0:T(8,128)(2,1)S(1)}, f32[1,2048]{1,0:T(1,128)S(1)}, f32[1,2048]{1,0:T(1,128)S(1)}, bf16[4,4,32,2048]{3,2,1,0:T(8,128)(2,1)S(1)}) custom-call(bf16[4,4,32,2048]{3,2,1,0:T(8,128)(2,1)S(1)} %bitcast.203, bf16[4,4,32,2048]{3,2,1,0:T(8,128)(2,1)S(1)} %bitcast.208, ...), custom_call_target="tpu_custom_call" | custom-call | tf_op jit(solution)/shard_map/pallas_call | solution.py:363
  197.5 7.0 %shard_map.212 = s32[4,4,128]{2,1,0:T(4,128)} custom-call(s32[4,128]{1,0:T(4,128)} %x_ref.1), custom_call_target="tpu_custom_call" | custom-call | tf_op jit(solution)/shard_map/pallas_call | solution.py:424
  221.6 25.4 %shard_map.206 = bf16[4,32,2048]{2,1,0:T(8,128)(2,1)S(1)} custom-call(bf16[4,4,32,2048]{3,2,1,0:T(8,128)(2,1)S(1)} %bitcast.205, bf16[4,32,2048]{2,1,0:T(8,128)(2,1)S(1)} %get-tuple-element.46.resid_ref.hidden_ref, f32[1,2048]{1,0:T(1,128)S(1)} %get-tuple-element.94.bias_ref), custom_call_target="tpu_custom_call" | custom-call | tf_op jit(solution)/shard_map/pallas_call | solution.py:363
  254.2 6.9 %shard_map.209 = (bf16[512,256]{1,0:T(8,128)(2,1)}, bf16[512,256]{1,0:T(8,128)(2,1)}, bf16[512,256]{1,0:T(8,128)(2,1)}) custom-call(bf16[512,256]{1,0:T(8,128)(2,1)} %get-tuple-element.58.q_ref, bf16[512,256]{1,0:T(8,128)(2,1)} %get-tuple-element.59.k_ref, bf16[512,256]{1,0:T(8,128)(2,1)} %get-tuple-element.60.v_ref, ...), custom_call_target="tpu_custom_call" | custom-call | flops 335544320 | bytes 2097152 | tf_op jit(solution)/shard_map/pallas_call | solution.py:152
  270.1 35.1 %shard_map.210 = (bf16[4,32,2048]{2,1,0:T(8,128)(2,1)S(1)}, f32[1,2048]{1,0:T(1,128)S(1)}, f32[1,2048]{1,0:T(1,128)S(1)}) custom-call(bf16[4,4,32,2048]{3,2,1,0:T(8,128)(2,1)S(1)} %bitcast.204, bf16[4,4,32,2048]{3,2,1,0:T(8,128)(2,1)S(1)} %copy-done.1, bf16[4,32,2048]{2,1,0:T(8,128)(2,1)S(1)} %constant_dynamic-slice_fusion.3.resid_ref.hidden_ref, ...), custom_call_target="tpu_custom_call" | custom-call | tf_op jit(solution)/shard_map/pallas_call | solution.py:363
  306.7 15.6 %shard_map.211 = f32[2,2048]{1,0:T(2,128)} custom-call(f32[2,2048]{1,0:T(2,128)} %pad_maximum_fusion.x_ref), custom_call_target="tpu_custom_call" | custom-call | tf_op jit(solution)/shard_map/pallas_call | solution.py:424
  325.6 9.1 %all-gather.5.cloned.1.call-done = bf16[4,512,2048]{2,1,0:T(8,128)(2,1)} async-done(((bf16[4,32,2048]{2,1,0:T(8,128)(2,1)}), bf16[4,512,2048]{2,1,0:T(8,128)(2,1)}) %all-gather.5.cloned.1.call-update) | async-done | bytes 8388624 | tf_op jit(solution)/shard_map/all_gather | solution.py:504
  334.8 6.5 %broadcast_select_fusion = (bf16[4,512,2048]{2,1,0:T(8,128)(2,1)S(1)}, bf16[4,512,2048]{2,1,0:T(8,128)(2,1)S(1)}) fusion(bf16[4,512,2048]{2,1,0:T(8,128)(2,1)} %all-gather.5.cloned.1.call-done, bf16[4,512,2048]{2,1,0:T(8,128)(2,1)} %all-gather.3.cloned.1.call-done, pred[]{:T(512)S(6)} %eq.25), kind=kLoop, calls=%fused_computation.14 | loop fusion | flops 8388608 | bytes 33554432 | tf_op jit(solution)/shard_map/jit(_where)/select_n | solution.py:576
  341.3 6.4 %convolution_convert_fusion.ga_ref = bf16[2048,512]{1,0:T(8,128)(2,1)} fusion(bf16[2048,2048]{1,0:T(8,128)(2,1)S(1)} %bitcast.216, bf16[1,512,2048]{2,1,0:T(8,128)(2,1)S(1)} %copy-done.15), kind=kOutput, calls=%fused_computation.47 | convolution fusion | flops 4296015872 | bytes 12582912 | tf_op jit(solution)/shard_map/dot_general | solution.py:47
  349.7 7.9 %fusion.34.k_ref = f32[2048,512]{1,0:T(8,128)} fusion(bf16[2048,2048]{1,0:T(8,128)(2,1)S(1)} %bitcast.221, bf16[1,3,2048,512]{3,2,1,0:T(8,128)(2,1)} %param.17), kind=kOutput, calls=%fused_computation.64 | convolution fusion | flops 4294967296 | bytes 14680064 | tf_op jit(solution)/shard_map/dot_general | solution.py:47
  357.7 27.3 %multiply_convert_fusion = (bf16[2048,2048]{1,0:T(8,128)(2,1)}, f32[2048,2048]{1,0:T(8,128)}) fusion(f32[2048]{0:T(1024)S(1)} %bitcast.258, bf16[2048,2048]{1,0:T(8,128)(2,1)S(1)} %bitcast.222, bf16[1,2048,2048]{2,1,0:T(8,128)(2,1)} %param.21), kind=kOutput, calls=%fused_computation.8 | convolution fusion | flops 17221812224 | bytes 41951232 | tf_op jit(solution)/shard_map/dot_general | solution.py:47
  385.0 6.3 %convolution_add_fusion.1.q_ref = f32[2048,512]{1,0:T(8,128)} fusion(bf16[2048,2048]{1,0:T(8,128)(2,1)S(1)} %bitcast.223, f32[512]{0:T(512)S(1)} %bitcast.265, bf16[1,3,2048,512]{3,2,1,0:T(8,128)(2,1)S(1)} %bitcast.230), kind=kOutput, calls=%fused_computation.46 | convolution fusion | flops 4296015872 | bytes 14682112 | tf_op jit(solution)/shard_map/dot_general | solution.py:47
  391.3 6.3 %convolution_add_fusion.v_ref = f32[2048,512]{1,0:T(8,128)} fusion(bf16[2048,2048]{1,0:T(8,128)(2,1)S(1)} %bitcast.224, f32[512]{0:T(512)S(1)} %bitcast.264, bf16[1,3,2048,512]{3,2,1,0:T(8,128)(2,1)S(1)} %bitcast.230), kind=kOutput, calls=%fused_computation.45 | convolution fusion | flops 4296015872 | bytes 14682112 | tf_op jit(solution)/shard_map/dot_general | solution.py:47
  397.6 39.9 %shard_map.213 = (bf16[2048,512]{1,0:T(8,128)(2,1)}, bf16[2048,512]{1,0:T(8,128)(2,1)}, bf16[2048,512]{1,0:T(8,128)(2,1)}, bf16[2048,512]{1,0:T(8,128)(2,1)}, f32[1,512]{1,0:T(1,128)}, /*index=5*/f32[1,512]{1,0:T(1,128)}) custom-call(f32[2048,512]{1,0:T(8,128)} %convolution_add_fusion.1.q_ref, f32[2048,512]{1,0:T(8,128)} %fusion.34.k_ref, ...), custom_call_target="tpu_custom_call" | custom-call | flops 2684354560 | bytes 16777216 | tf_op jit(solution)/shard_map/pallas_call | solution.py:152
  451.1 36.1 %fusion.88 = (f32[2048]{0:T(1024)}, bf16[2048,2048]{1,0:T(8,128)(2,1)}) fusion(f32[2048,2048]{1,0:T(8,128)} %get-tuple-element.122, f32[2048]{0:T(1024)S(1)} %bitcast.259, bf16[2048,2048]{1,0:T(8,128)(2,1)} %bitcast.219, bf16[1,2048,2048]{2,1,0:T(8,128)(2,1)} %param.23), kind=kOutput, calls=%fused_computation.183 | convolution fusion | flops 17272141824 | bytes 41959424 | tf_op jit(solution)/shard_map/dot_general | solution.py:47
  487.3 10.6 %convolution_bitcast_fusion.1 = f32[1,512,2048]{2,1,0:T(8,128)} fusion(bf16[2048,2048]{1,0:T(8,128)(2,1)} %get-tuple-element.77, bf16[2048,2048]{1,0:T(8,128)(2,1)} %bitcast.228, s32[]{:T(128)S(6)} %select_n.199), kind=kOutput, calls=%fused_computation.35 | convolution fusion | flops 4294967296 | bytes 14680068 | tf_op jit(solution)/shard_map/dot_general | solution.py:47
  497.9 10.6 %convolution_bitcast_fusion = f32[1,2048,512]{2,1,0:T(8,128)} fusion(bf16[2048,2048]{1,0:T(8,128)(2,1)} %get-tuple-element.121, bf16[2048,2048]{1,0:T(8,128)(2,1)} %bitcast.220, s32[]{:T(128)S(6)} %select_n.199), kind=kOutput, calls=%fused_computation.34 | convolution fusion | flops 4294967296 | bytes 14680068 | tf_op jit(solution)/shard_map/dot_general | solution.py:47
  (196 shorter events, 124.3 us)
Async XLA Ops:
  7.2 190.3 %all-gather.3.cloned.1.call-start = ((), (), s32[]{:S(2)}) async-start(), calls=%async_computation | async-start | bytes 10485760 | tf_op jit(solution)/shard_map/all_gather | solution.py:506
  10.7 14.5 %collective-permute-start = (f32[1,9216]{1,0:T(1,128)S(1)}, f32[1,9216]{1,0:T(1,128)S(1)}, u32[]{:S(2)}, u32[]{:S(2)}) collective-permute-start(f32[1,9216]{1,0:T(1,128)S(1)} %bitcast.247), channel_id=1, source_target_pairs={{0,16},{16,0},{1,17},{17,1},{2,18},{18,2},{3,19},{19,3},{4,20},{20... | collective-permute-start | bytes 110600 | tf_op jit(solution)/shard_map/ppermute | solution.py:465
  16.1 41.6 %collective-permute-start.3 = (bf16[2048,1024]{1,0:T(8,128)(2,1)}, bf16[2048,1024]{1,0:T(8,128)(2,1)}, u32[]{:S(2)}, u32[]{:S(2)}) collective-permute-start(bf16[2048,1024]{1,0:T(8,128)(2,1)} %dynamic-slice_bitcast_fusion.1), channel_id=1, source_target_pairs={{0,16},{16,0},{1,17},{17,1},{2,18},{18,2},{3,19},{19,3},{4,20},{20... | collective-permute-start | bytes 12582920 | tf_op jit(solution)/shard_map/ppermute | solution.py:465
  19.7 45.2 %collective-permute-start.4 = (bf16[1024,2048]{1,0:T(8,128)(2,1)}, bf16[1024,2048]{1,0:T(8,128)(2,1)}, u32[]{:S(2)}, u32[]{:S(2)}) collective-permute-start(bf16[1024,2048]{1,0:T(8,128)(2,1)} %dynamic-slice_bitcast_fusion), channel_id=1, source_target_pairs={{0,16},{16,0},{1,17},{17,1},{2,18},{18,2},{3,19},{19,3},{4,20},{20... | collective-permute-start | bytes 12582920 | tf_op jit(solution)/shard_map/ppermute | solution.py:465
  23.6 17.1 %collective-permute-start.1 = (bf16[3,2048,256]{2,1,0:T(8,128)(2,1)}, bf16[3,2048,256]{2,1,0:T(8,128)(2,1)}, u32[]{:S(2)}, u32[]{:S(2)}) collective-permute-start(bf16[3,2048,256]{2,1,0:T(8,128)(2,1)} %dynamic-slice_bitcast_fusion.2), channel_id=1, source_target_pairs={{0,16},{16,0},{1,17},{17,1},{2,18},{18,2},{3,19},{19,3},{4,20},{20... | collective-permute-start | bytes 9437192 | tf_op jit(solution)/shard_map/ppermute | solution.py:465
  29.7 305.0 %all-gather.5.cloned.1.call-start = ((), (), s32[]{:S(2)}) async-start(), calls=%async_computation.1 | async-start | bytes 8912896 | tf_op jit(solution)/shard_map/all_gather | solution.py:504
  32.1 5.3 %collective-permute-start.2 = (bf16[256,2048]{1,0:T(8,128)(2,1)}, bf16[256,2048]{1,0:T(8,128)(2,1)}, u32[]{:S(2)}, u32[]{:S(2)}) collective-permute-start(bf16[256,2048]{1,0:T(8,128)(2,1)} %dynamic-slice_bitcast_fusion.3), channel_id=1, source_target_pairs={{0,16},{16,0},{1,17},{17,1},{2,18},{18,2},{3,19},{19,3},{4,20},{20... | collective-permute-start | bytes 3145736 | tf_op jit(solution)/shard_map/ppermute | solution.py:465
  57.8 50.3 %slice-start.2 = ((s8[8388608]{0:T(1024)(128)(4,1)}), s8[4194304]{0:T(1024)(128)(4,1)S(1)}, s32[]{:S(2)}) async-start(s8[8388608]{0:T(1024)(128)(4,1)} %bitcast.231), calls=%async_computation.4 | async-start | bytes 8388608
  64.9 43.2 %slice-start.3 = ((s8[8388608]{0:T(1024)(128)(4,1)}), s8[4194304]{0:T(1024)(128)(4,1)S(1)}, s32[]{:S(2)}) async-start(s8[8388608]{0:T(1024)(128)(4,1)} %bitcast.231), calls=%async_computation.5 | async-start | bytes 8388608
  70.6 44.4 %slice-start.4 = ((s8[8388608]{0:T(1024)(128)(4,1)}), s8[4194304]{0:T(1024)(128)(4,1)S(1)}, s32[]{:S(2)}) async-start(s8[8388608]{0:T(1024)(128)(4,1)} %bitcast.233), calls=%async_computation.6 | async-start | bytes 8388608
  108.1 28.0 %copy-start.5 = (bf16[4,4,32,2048]{3,2,1,0:T(8,128)(2,1)}, bf16[4,4,32,2048]{3,2,1,0:T(8,128)(2,1)S(1)}, u32[]{:S(2)}) copy-start(bf16[4,4,32,2048]{3,2,1,0:T(8,128)(2,1)S(1)} %get-tuple-element.47) | copy-start | bytes 6291460
  108.1 6.9 %slice-start.5 = ((s8[8388608]{0:T(1024)(128)(4,1)}), s8[4194304]{0:T(1024)(128)(4,1)S(1)}, s32[]{:S(2)}) async-start(s8[8388608]{0:T(1024)(128)(4,1)} %bitcast.233), calls=%async_computation.7 | async-start | bytes 8388608
  115.0 18.1 %copy-start.10 = (bf16[3,2048,256]{2,1,0:T(8,128)(2,1)S(1)}, bf16[3,2048,256]{2,1,0:T(8,128)(2,1)}, u32[]{:S(2)}) copy-start(bf16[3,2048,256]{2,1,0:T(8,128)(2,1)} %get-tuple-element.86) | copy-start | bytes 9437188
  205.6 8.9 %slice-start.6 = ((s8[8388608]{0:T(1024)(128)(4,1)}), s8[4194304]{0:T(1024)(128)(4,1)S(1)}, s32[]{:S(2)}) async-start(s8[8388608]{0:T(1024)(128)(4,1)} %bitcast.235), calls=%async_computation.8 | async-start | bytes 8388608
  221.6 26.3 %copy-start.1 = (bf16[4,4,32,2048]{3,2,1,0:T(8,128)(2,1)S(1)}, bf16[4,4,32,2048]{3,2,1,0:T(8,128)(2,1)}, u32[]{:S(2)}) copy-start(bf16[4,4,32,2048]{3,2,1,0:T(8,128)(2,1)} %copy-done) | copy-start | bytes 6291460
  221.6 26.3 %copy-start.33 = (f32[512,1024]{1,0:T(8,128)S(1)}, f32[512,1024]{1,0:T(8,128)}, u32[]{:S(2)}) copy-start(f32[512,1024]{1,0:T(8,128)} %get-tuple-element.117) | copy-start | bytes 6291460
  270.1 53.5 %copy-start.3 = (bf16[4,32,2048]{2,1,0:T(8,128)(2,1)S(1)}, bf16[4,32,2048]{2,1,0:T(8,128)(2,1)}, u32[]{:S(2)}) copy-start(bf16[4,32,2048]{2,1,0:T(8,128)(2,1)} %copy-done.2) | copy-start | bytes 1572868
  325.6 15.6 %copy-start.15 = (bf16[1,512,2048]{2,1,0:T(8,128)(2,1)S(1)}, bf16[1,512,2048]{2,1,0:T(8,128)(2,1)}, u32[]{:S(2)}) copy-start(bf16[1,512,2048]{2,1,0:T(8,128)(2,1)} %param.19) | copy-start | bytes 6291460
  341.2 50.1 %copy-start.12 = (bf16[4,512,2048]{2,1,0:T(8,128)(2,1)}, bf16[4,512,2048]{2,1,0:T(8,128)(2,1)S(1)}, u32[]{:S(2)}) copy-start(bf16[4,512,2048]{2,1,0:T(8,128)(2,1)S(1)} %get-tuple-element.85) | copy-start | bytes 25165828
  349.7 7.9 %copy-start.26 = (f32[1,2048]{1,0:T(1,128)S(1)}, f32[1,2048]{1,0:T(1,128)}, u32[]{:S(2)}) copy-start(f32[1,2048]{1,0:T(1,128)} %param.22) | copy-start | bytes 24580
  349.7 35.2 %slice-start = ((s8[6291456]{0:T(1024)(128)(4,1)}), s8[4194304]{0:T(1024)(128)(4,1)S(1)}, s32[]{:S(2)}) async-start(s8[6291456]{0:T(1024)(128)(4,1)} %bitcast.229), calls=%async_computation.2 | async-start | bytes 8388608
  357.6 27.3 %slice-start.1 = ((s8[6291456]{0:T(1024)(128)(4,1)}), s8[2097152]{0:T(1024)(128)(4,1)S(1)}, s32[]{:S(2)}) async-start(s8[6291456]{0:T(1024)(128)(4,1)} %bitcast.229), calls=%async_computation.3 | async-start | bytes 4194304
  497.9 10.6 %copy-start.27 = (f32[1,512]{1,0:T(1,128)S(1)}, f32[1,512]{1,0:T(1,128)}, u32[]{:S(2)}) copy-start(f32[1,512]{1,0:T(1,128)} %get-tuple-element.74) | copy-start | bytes 6148
  497.9 10.6 %copy-start.28 = (f32[1,512]{1,0:T(1,128)S(1)}, f32[1,512]{1,0:T(1,128)}, u32[]{:S(2)}) copy-start(f32[1,512]{1,0:T(1,128)} %get-tuple-element.75) | copy-start | bytes 6148
  (27 other events, 94.5 us)
Sparse Core Ops, SparseCore 0:
  29.9 151.9 all-gather.2
  197.6 137.0 all-gather.4

commit v5 on v4

--- a/solution.py
+++ b/solution.py
@@ -99,55 +99,127 @@
         out_ref[:, at] = side_by_side(mm(prob, value), rows).astype(bf16)
 
 
-def attention_backward_kernel(again, q_ref, k_ref, v_ref, ga_ref, table_ref, allowed_ref, *outs):
+def pair_backward(query, key, value, grad, table, allowed, with_output):
+    bf16 = jnp.bfloat16
+    rows, scale = query.shape[0], HEAD_DIM ** (-0.5)
+    queries, grads = stacked_heads(query), stacked_heads(grad)
+    prob_f = softmax_of(queries, key, allowed)
+    prob_b = prob_f.astype(bf16)
+    grad_prob = mm(grads, value, ((1,), (1,)))
+    row_dot = jnp.sum(prob_f * grad_prob, axis=-1, keepdims=True)
+    grad_score = (prob_f * (grad_prob - row_dot)).astype(bf16)
+    g_query = side_by_side(mm(grad_score, key), rows)
+    g_key = mm(grad_score, queries, ((0,), (0,)))
+    g_value = mm(prob_b, grads, ((0,), (0,)))
+    g_query = rotated(g_query * scale, table, -1.0)
+    g_key = rotated(g_key * scale, table, -1.0)
+    out = side_by_side(mm(prob_b, value), rows).astype(bf16) if with_output else None
+    return g_query, g_key, g_value, out
+
+
+def attention_backward_kernel(q_ref, k_ref, v_ref, ga_ref, table_ref, allowed_ref, gq_ref, gk_ref, gv_ref):
     bf16 = jnp.bfloat16
     table = table_ref[0]
-    rows, lanes = table.shape[-2:]
+    lanes = table.shape[-1]
     allowed = jnp.concatenate([allowed_ref[0] > 0.5] * (lanes // HEAD_DIM), axis=0)
-    scale = HEAD_DIM ** (-0.5)
-    if again:
-        gq_ref, gk_ref, gv_ref, out_ref, sq_ref, sv_ref = outs
-
-        @pl.when(pl.program_id(0) == 0)
-        def _():
-            sq_ref[...] = jnp.zeros_like(sq_ref)
-            sv_ref[...] = jnp.zeros_like(sv_ref)
-    else:
-        gq_ref, gk_ref, gv_ref = outs
     for pair in range(q_ref.shape[-1] // lanes):
         at = slice(pair * lanes, (pair + 1) * lanes)
-        if again:
-            query = rotated(q_ref[:, at], table, 1.0).astype(bf16)
-            key = rotated(k_ref[:, at], table, 1.0).astype(bf16)
-            value = v_ref[:, at].astype(bf16)
-        else:
-            query, key, value = q_ref[:, at], k_ref[:, at], v_ref[:, at]
-        queries = stacked_heads(query)
-        grads = stacked_heads(ga_ref[:, at])
-        prob_f = softmax_of(queries, key, allowed)
-        prob_b = prob_f.astype(bf16)
-        grad_prob = mm(grads, value, ((1,), (1,)))
-        row_dot = jnp.sum(prob_f * grad_prob, axis=-1, keepdims=True)
-        grad_score = (prob_f * (grad_prob - row_dot)).astype(bf16)
-        g_query = side_by_side(mm(grad_score, key), rows)
-        g_key = mm(grad_score, queries, ((0,), (0,)))
-        g_value = mm(prob_b, grads, ((0,), (0,)))
-        g_query = rotated(g_query * scale, table, -1.0)
-        g_key = rotated(g_key * scale, table, -1.0)
+        g_query, g_key, g_value, _ = pair_backward(
+            q_ref[:, at], k_ref[:, at], v_ref[:, at], ga_ref[:, at], table, allowed, False
+        )
         gq_ref[:, at] = g_query.astype(bf16)
         gk_ref[:, at] = g_key.astype(bf16)
         gv_ref[:, at] = g_value.astype(bf16)
-        if again:
-            out_ref[:, at] = side_by_side(mm(prob_b, value), rows).astype(bf16)
-            sq_ref[:, at] += jnp.sum(g_query, axis=0, keepdims=True)
-            sv_ref[:, at] += jnp.sum(g_value, axis=0, keepdims=True)
-
-
-def attention_call(kernel, arrays, tables, allowed, outs, sums):
+
+
+def attention_again_kernel(
+    normed_ref, up_ref, w_ref, dense_ref, bias_ref, table_ref, allowed_ref,
+    gq_ref, gk_ref, gv_ref, out_ref, sq_ref, sv_ref, su_ref,
+):
+    bf16 = jnp.bfloat16
+    count, _, rows, lanes = table_ref.shape
+    features = gq_ref.shape[-1]
+    wide = min(2 * lanes, features)
+
+    @pl.when(pl.program_id(0) == 0)
+    def _():
+        sq_ref[...] = jnp.zeros_like(sq_ref)
+        sv_ref[...] = jnp.zeros_like(sv_ref)
+        su_ref[...] = jnp.zeros_like(su_ref)
+
+    su_ref[...] += jnp.sum(up_ref[...].astype(jnp.float32), axis=0, keepdims=True)
+
+    def products(at):
+        cols = slice(at, at + wide)
+        return (
+            mm(normed_ref[...], w_ref[0, :, cols]) + bias_ref[0:1, cols],
+            mm(normed_ref[...], w_ref[1, :, cols]),
+            (mm(normed_ref[...], w_ref[2, :, cols]) + bias_ref[1:2, cols]).astype(bf16),
+            mm(up_ref[...], dense_ref[cols, :], ((1,), (1,))).astype(bf16),
+        )
+
+    starts = list(range(0, features, wide))
+    ready = products(starts[0])
+    for index, start in enumerate(starts):
+        upcoming = products(starts[index + 1]) if index + 1 < len(starts) else None
+        for block in range(count):
+            table = table_ref[block]
+            allowed = jnp.concatenate([allowed_ref[block] > 0.5] * (lanes // HEAD_DIM), axis=0)
+            down = slice(block * rows, (block + 1) * rows)
+            for pair in range(wide // lanes):
+                inside = slice(pair * lanes, (pair + 1) * lanes)
+                query_f, key_f, value, grad = [x[down, inside] for x in ready]
+                query = rotated(query_f, table, 1.0).astype(bf16)
+                key = rotated(key_f, table, 1.0).astype(bf16)
+                g_query, g_key, g_value, out = pair_backward(
+                    query, key, value, grad, table, allowed, True
+                )
+                at = slice(start + pair * lanes, start + (pair + 1) * lanes)
+                gq_ref[down, at] = g_query.astype(bf16)
+                gk_ref[down, at] = g_key.astype(bf16)
+                gv_ref[down, at] = g_value.astype(bf16)
+                out_ref[down, at] = out
+                sq_ref[:, at] += jnp.sum(g_query, axis=0, keepdims=True)
+                sv_ref[:, at] += jnp.sum(g_value, axis=0, keepdims=True)
+        ready = upcoming
+
+
+def attention_again(normed, up, proj_qkv, proj_dense, bias_qv, tables, allowed):
+    blocks, _, rows, lanes = tables.shape
+    features, width = proj_dense.shape
+    count = 2 if blocks % 2 == 0 else 1
+    wide = pl.BlockSpec((count * rows, width), lambda i: (i, 0))
+    block = pl.BlockSpec((count * rows, features), lambda i: (i, 0))
+    one = pl.BlockSpec((1, features), lambda i: (0, 0))
+    flat = jax.ShapeDtypeStruct((blocks * rows, features), jnp.bfloat16)
+    line = jax.ShapeDtypeStruct((1, features), jnp.float32)
+    once = pl.Buffered(1)
+    return pl.pallas_call(
+        attention_again_kernel,
+        grid=(blocks // count,),
+        in_specs=[
+            wide,
+            wide,
+            pl.BlockSpec(proj_qkv.shape, lambda i: (0, 0, 0), pipeline_mode=once),
+            pl.BlockSpec(proj_dense.shape, lambda i: (0, 0), pipeline_mode=once),
+            pl.BlockSpec(bias_qv.shape, lambda i: (0, 0)),
+            pl.BlockSpec((count, 3, rows, lanes), lambda i: (i, 0, 0, 0)),
+            pl.BlockSpec((count, rows, rows), lambda i: (i, 0, 0)),
+        ],
+        out_specs=[block] * 4 + [one] * 2 + [pl.BlockSpec((1, width), lambda i: (0, 0))],
+        out_shape=[flat] * 4 + [line] * 2 + [jax.ShapeDtypeStruct((1, width), jnp.float32)],
+        cost_estimate=pl.CostEstimate(
+            flops=8 * blocks * rows * width * features,
+            bytes_accessed=blocks * rows * (width * 4 + features * 8),
+            transcendentals=0,
+        ),
+    )(normed, up, proj_qkv, proj_dense, bias_qv, tables, allowed)
+
+
+def attention_call(kernel, arrays, tables, allowed, outs):
     blocks, _, rows, lanes = tables.shape
     features = arrays[0].shape[-1]
     block = pl.BlockSpec((rows, features), lambda i: (i, 0))
-    one = pl.BlockSpec((1, features), lambda i: (0, 0))
     flat = (blocks * rows, features)
     return pl.pallas_call(
         kernel,
@@ -157,9 +229,8 @@
             pl.BlockSpec((1, 3, rows, lanes), lambda i: (i, 0, 0, 0)),
             pl.BlockSpec((1, rows, rows), lambda i: (i, 0, 0)),
         ],
-        out_specs=[block] * outs + [one] * sums,
-        out_shape=[jax.ShapeDtypeStruct(flat, jnp.bfloat16)] * outs
-        + [jax.ShapeDtypeStruct((1, features), jnp.float32)] * sums,
+        out_specs=[block] * outs,
+        out_shape=[jax.ShapeDtypeStruct(flat, jnp.bfloat16)] * outs,
         cost_estimate=pl.CostEstimate(
             flops=20 * blocks * rows * rows * features,
             bytes_accessed=blocks * rows * features * 16,
@@ -230,35 +301,50 @@
     )
 
 
-def reduced_half(n, partial_ref, scratch):
-    pair, out_buf, recv, pair_sems, rs_sems = scratch
+def start_swaps(n, partial_ref, scratch):
+    pair, _, _, pair_sems, _ = scratch
     t, sec = lax.axis_index("tensor"), lax.axis_index("section")
-    mine, other = halves_of(partial_ref.shape[-1])
-    enter(n)
-    order = list(range(n - 1, -1, -1))
-    swaps = {}
-    for k in order:
-        at = partner(t, k)
-        swaps[k] = send(
-            partial_ref.at[:, at, :, other], pair.at[k],
+    _, other = halves_of(partial_ref.shape[-1])
+    return {
+        k: send(
+            partial_ref.at[:, partner(t, k), :, other], pair.at[k],
             [x.at[k] for x in pair_sems], {"section": 1 - sec},
         )
+        for k in range(n - 1, -1, -1)
+    }
+
+
+def start_sums(n, partial_ref, scratch, swaps):
+    pair, out_buf, recv, _, rs_sems = scratch
+    t = lax.axis_index("tensor")
+    mine, _ = halves_of(partial_ref.shape[-1])
     sends = []
-    for k in order:
+    for k in range(n - 1, -1, -1):
         at = partner(t, k)
         swaps[k].wait_recv()
         both = partial_ref[:, at, :, mine].astype(jnp.float32) + pair[k].astype(jnp.float32)
-        if k == 0:
-            total = both
-        else:
+        if k:
             out_buf[k - 1] = both.astype(jnp.bfloat16)
             sends.append(
                 (k, send(out_buf.at[k - 1], recv.at[k - 1],
                          [x.at[k - 1] for x in rs_sems], {"tensor": at}))
             )
+    return both, sends
+
+
+def finish_sums(total, scratch, sends):
+    recv = scratch[2]
     for k, copy in sends:
         copy.wait_recv()
         total = total + recv[k - 1].astype(jnp.float32)
+    return total
+
+
+def reduced_half(n, partial_ref, scratch):
+    enter(n)
+    swaps = start_swaps(n, partial_ref, scratch)
+    total, sends = start_sums(n, partial_ref, scratch, swaps)
+    total = finish_sums(total, scratch, sends)
     return total, list(swaps.values()) + [copy for _, copy in sends]
 
 
@@ -287,11 +373,9 @@
     return centred * inv_std, inv_std
 
 
-def forward_kernel(n, last, partial_ref, resid_ref, bias_ref, *rest):
-    if last:
-        out_ref, *scratch = rest
-    else:
-        gain_ref, shift_ref, out_ref, full_ref, *scratch = rest
+def forward_kernel(
+    n, partial_ref, resid_ref, bias_ref, gain_ref, shift_ref, out_ref, full_ref, *scratch
+):
     t, sec = lax.axis_index("tensor"), lax.axis_index("section")
     mine, _ = halves_of(partial_ref.shape[-1])
     total, copies = reduced_half(n, partial_ref, unpack(scratch))
@@ -300,12 +384,9 @@
     part = out_ref.at[:, :, mine]
     hop = send(part, part, scratch[7:9], {"section": 1 - sec})
     hop.wait()
-    if not last:
-        standard, _ = standard_of(out_ref[...].astype(jnp.float32))
-        full_ref[:, t] = (standard * gain_ref[...][None] + shift_ref[...][None]).astype(
-            jnp.bfloat16
-        )
-        spread(n, full_ref, scratch[9:11], scratch[11:13])
+    standard, _ = standard_of(out_ref[...].astype(jnp.float32))
+    full_ref[:, t] = (standard * gain_ref[...][None] + shift_ref[...][None]).astype(jnp.bfloat16)
+    spread(n, full_ref, scratch[9:11], scratch[11:13])
     for copy in copies:
         copy.wait_send()
 
@@ -315,38 +396,73 @@
     return pair, out_buf, recv, (pair_s, pair_r), (rs_s, rs_r)
 
 
-def backward_kernel(n, last, partial_ref, up_ref, hidden_ref, gain_ref, *rest):
-    if last:
-        out_ref, ggain_ref, gshift_ref, *scratch = rest
-    else:
-        out_ref, ggain_ref, gshift_ref, full_ref, *scratch = rest
-    *scratch, whole = scratch
+def norm_backward(grad_normed, hidden_ref, gain_ref, up_rows, ggain_ref, gshift_ref):
+    standard, inv_std = standard_of(hidden_ref[...].astype(jnp.float32))
+    scaled = grad_normed * gain_ref[...][None]
+    grad_in = inv_std * (
+        scaled
+        - jnp.mean(scaled, axis=-1, keepdims=True)
+        - standard * jnp.mean(scaled * standard, axis=-1, keepdims=True)
+    )
+    ggain_ref[...] = jnp.sum(jnp.sum(grad_normed * standard, axis=0), axis=0, keepdims=True)
+    gshift_ref[...] = jnp.sum(jnp.sum(grad_normed, axis=0), axis=0, keepdims=True)
+    return (up_rows.astype(jnp.float32) + grad_in).astype(jnp.bfloat16)
+
+
+def backward_kernel(
+    n, partial_ref, up_ref, hidden_ref, gain_ref, out_ref, ggain_ref, gshift_ref, full_ref,
+    whole, *scratch
+):
     t, sec = lax.axis_index("tensor"), lax.axis_index("section")
     mine, _ = halves_of(partial_ref.shape[-1])
     total, copies = reduced_half(n, partial_ref, unpack(scratch))
     whole[:, :, mine] = total
     part = whole.at[:, :, mine]
     hop = send(part, part, scratch[7:9], {"section": 1 - sec})
-    standard, inv_std = standard_of(hidden_ref[...].astype(jnp.float32))
     hop.wait()
-    grad_normed = whole[...]
-    scaled = grad_normed * gain_ref[...][None]
-    grad_in = inv_std * (
-        scaled
-        - jnp.mean(scaled, axis=-1, keepdims=True)
-        - standard * jnp.mean(scaled * standard, axis=-1, keepdims=True)
-    )
-    out_ref[...] = (up_ref[:, t].astype(jnp.float32) + grad_in).astype(jnp.bfloat16)
-    if not last:
-        full_ref[:, t] = out_ref[...]
-        spread(n, full_ref, scratch[9:11], scratch[11:13])
-    ggain_ref[...] = jnp.sum(jnp.sum(grad_normed * standard, axis=0), axis=0, keepdims=True)
-    gshift_ref[...] = jnp.sum(jnp.sum(grad_normed, axis=0), axis=0, keepdims=True)
+    out_ref[...] = norm_backward(
+        whole[...], hidden_ref, gain_ref, up_ref[:, t], ggain_ref, gshift_ref
+    )
+    full_ref[:, t] = out_ref[...]
+    spread(n, full_ref, scratch[9:11], scratch[11:13])
     for copy in copies:
         copy.wait_send()
 
 
-def sum_call(kernel, n, last, ident, args, outs, rows_shape):
+def final_kernel(
+    n, partial_ref, resid_ref, bias_ref, grad_ref, up_ref, hidden_ref, gain_ref,
+    out_ref, down_ref, ggain_ref, gshift_ref, whole, *scratch
+):
+    t, sec = lax.axis_index("tensor"), lax.axis_index("section")
+    mine, _ = halves_of(partial_ref.shape[-1])
+    sets = [unpack(scratch[:9]), unpack(scratch[9:])]
+    hops = [scratch[7:9], scratch[16:18]]
+    refs = [grad_ref, partial_ref]
+    enter(n)
+    swaps = [start_swaps(n, ref, x) for ref, x in zip(refs, sets)]
+    sums = [start_sums(n, ref, x, w) for ref, x, w in zip(refs, sets, swaps)]
+    whole[:, :, mine] = finish_sums(sums[0][0], sets[0], sums[0][1])
+    part = whole.at[:, :, mine]
+    first = send(part, part, hops[0], {"section": 1 - sec})
+    total = finish_sums(sums[1][0], sets[1], sums[1][1])
+    total = total + resid_ref[:, :, mine].astype(jnp.float32) + bias_ref[:, mine][None]
+    out_ref[:, :, mine] = total.astype(jnp.bfloat16)
+    part = out_ref.at[:, :, mine]
+    second = send(part, part, hops[1], {"section": 1 - sec})
+    first.wait()
+    down_ref[...] = norm_backward(
+        whole[...], hidden_ref, gain_ref, up_ref[:, t], ggain_ref, gshift_ref
+    )
+    second.wait()
+    for w in swaps:
+        for copy in w.values():
+            copy.wait_send()
+    for _, sends in sums:
+        for _, copy in sends:
+            copy.wait_send()
+
+
+def sum_call(kernel, n, ident, args, outs, rows_shape):
     dma = pltpu.SemaphoreType.DMA
     half = rows_shape[:-1] + (rows_shape[-1] // 2,)
     scratch = [
@@ -355,13 +471,12 @@
         pltpu.VMEM((n - 1,) + half, jnp.bfloat16),
         dma((n,)), dma((n,)), dma((n - 1,)), dma((n - 1,)), dma, dma,
     ]
-    if not last:
-        scratch += [dma((n - 1,))] * 4
-    if kernel is backward_kernel:
-        scratch.append(pltpu.VMEM(rows_shape, jnp.float32))
+    scratch += scratch if kernel is final_kernel else [dma((n - 1,))] * 4
+    if kernel is not forward_kernel:
+        scratch = [pltpu.VMEM(rows_shape, jnp.float32)] + scratch
     vmem = pl.BlockSpec(memory_space=pltpu.VMEM)
     return pl.pallas_call(
-        functools.partial(kernel, n, last),
+        functools.partial(kernel, n),
         out_shape=outs,
         in_specs=[vmem] * len(args),
         out_specs=[vmem] * len(outs),
@@ -370,6 +485,68 @@
             collective_id=ident, has_side_effects=True, vmem_limit_bytes=32 * 1024 * 1024
         ),
     )(*args)
+
+
+GELU_A = (2.0 / jnp.pi) ** 0.5
+GELU_B = 0.044715
+
+
+def hidden_kernel(first, x_ref, known_ref, w_ref, b_ref, act_ref, grad_ref, sum_ref):
+    @pl.when(pl.program_id(1) == 0)
+    def _():
+        sum_ref[...] = jnp.zeros_like(sum_ref)
+
+    step = 256
+    starts = list(range(0, act_ref.shape[-1], step))
+
+    def product(at):
+        cols = slice(at, at + step)
+        if first:
+            return mm(x_ref[...], w_ref[cols, :], ((1,), (1,)))
+        return mm(x_ref[...], w_ref[:, cols]) + b_ref[:, cols]
+
+    ready = product(starts[0])
+    for index, at in enumerate(starts):
+        cols = slice(at, at + step)
+        upcoming = product(starts[index + 1]) if index + 1 < len(starts) else None
+        pre, grad_act = (known_ref[:, cols], ready) if first else (ready, known_ref[:, cols])
+        square = pre * pre
+        bent = jnp.tanh(pre * (GELU_A + (GELU_A * GELU_B) * square))
+        gate = 0.5 + 0.5 * bent
+        act_ref[:, cols] = (pre * gate).astype(jnp.bfloat16)
+        slope = gate + (0.5 * pre) * (1.0 - bent * bent) * (
+            GELU_A + (3.0 * GELU_A * GELU_B) * square
+        )
+        grad_pre = grad_act * slope
+        grad_ref[:, cols] = grad_pre.astype(jnp.bfloat16)
+        sum_ref[:, cols] += jnp.sum(grad_pre, axis=0, keepdims=True)
+        ready = upcoming
+
+
+def hidden_call(first, x, known, weight, bias):
+    tokens, width = x.shape
+    units = known.shape[-1]
+    tile, chunk = 256, min(1024, units)
+    flat = pl.BlockSpec((tile, chunk), lambda j, i: (i, j))
+    line = pl.BlockSpec((1, chunk), lambda j, i: (0, j))
+    w_spec = (
+        pl.BlockSpec((chunk, width), lambda j, i: (j, 0))
+        if first
+        else pl.BlockSpec((width, chunk), lambda j, i: (0, j))
+    )
+    out = jax.ShapeDtypeStruct((tokens, units), jnp.bfloat16)
+    return pl.pallas_call(
+        functools.partial(hidden_kernel, first),
+        grid=(units // chunk, tokens // tile),
+        in_specs=[pl.BlockSpec((tile, width), lambda j, i: (i, 0)), flat, w_spec, line],
+        out_specs=[flat, flat, line],
+        out_shape=[out, out, jax.ShapeDtypeStruct((1, units), jnp.float32)],
+        cost_estimate=pl.CostEstimate(
+            flops=2 * tokens * width * units,
+            bytes_accessed=tokens * (units * 8 + width * 4),
+            transcendentals=tokens * units,
+        ),
+    )(x, known, weight, bias[None])
 
 
 def exchange_kernel(axes, add, x_ref, out_ref, *rest):
@@ -450,8 +627,6 @@
     n = lax.axis_size("tensor")
     n_dp = lax.axis_size("dp")
     share = rows // n
-    group = micro
-    count = micro // group
     sec = lax.axis_index("section")
     is_first = sec == 0
     row_start = lax.axis_index("tensor") * share
@@ -517,7 +692,7 @@
     def branch_forward(normed, layer):
         _, _, _, b_qv, b_fc, (w_qkv, w_one, w_dense, w_two) = layer
         *kept, attended = attention_call(
-            attention_forward_kernel, projections(normed, w_qkv, b_qv), tables, allowed, 4, 0,
+            attention_forward_kernel, projections(normed, w_qkv, b_qv), tables, allowed, 4,
         )
         pre_act = mm(normed, w_one) + b_fc
         activation = settled(jax.nn.gelu(pre_act, approximate=True).astype(bf16))
@@ -530,8 +705,7 @@
         grad_pre = settled(gelu_grad(pre_act, mm(up, w_two, ((1,), (1,)))).astype(bf16))
         grad_att = mm(up, w_dense, ((1,), (1,))).astype(bf16)
         pieces = attention_call(
-            functools.partial(attention_backward_kernel, False),
-            kept + [grad_att], tables, allowed, 3, 0,
+            attention_backward_kernel, kept + [grad_att], tables, allowed, 3,
         )
         grad_normed = mm(grad_pre, w_one, ((1,), (1,)))
         for which in range(3):
@@ -540,17 +714,14 @@
 
     partial, stored_0 = branch_forward(flat(first_normed), layers[0])
     out_0, normed = sum_call(
-        forward_kernel, n, False, 0,
+        forward_kernel, n, 0,
         [partial, x_rows, layers[0][2], layers[1][0], layers[1][1]],
         [rows_out, full_out], rows_shape,
     )
-    partial, stored_1 = branch_forward(flat(normed), layers[1])
-    (out_1,) = sum_call(
-        forward_kernel, n, True, 1, [partial, out_0, layers[1][2]], [rows_out], rows_shape
-    )
+    last_partial, stored_1 = branch_forward(flat(normed), layers[1])
     partial = branch_backward(flat(top), layers[1], stored_1)
     grad_1, gain_1, shift_1, up = sum_call(
-        backward_kernel, n, False, 2, [partial, four(top), out_0, layers[1][0]],
+        backward_kernel, n, 2, [partial, four(top), out_0, layers[1][0]],
         [rows_out, line, line, full_out], rows_shape,
     )
     own = lambda x: lax.dynamic_index_in_dim(x, lax.axis_index("tensor"), 1, keepdims=False)
@@ -558,51 +729,69 @@
     up, late_rows, early = settled((up, late_rows, early))
     late = gather(late_rows)
     partial = branch_backward(flat(up), layers[0], stored_0)
-    grad_0, gain_0, shift_0 = sum_call(
-        backward_kernel, n, True, 3, [partial, up, x_rows, layers[0][0]],
-        [rows_out, line, line], rows_shape,
+
+    tokens = micro * n_dp * rows
+    early = early.reshape(tokens, width)
+    known = lax.cond(
+        is_first,
+        lambda x: mm(x, fc_one) + bias_fc,
+        lambda x: mm(x, fc_two, ((1,), (1,))),
+        early,
+    )
+    partial, last_partial, known = settled((partial, last_partial, known))
+    out_1, grad_0, gain_0, shift_0 = sum_call(
+        final_kernel, n, 1,
+        [last_partial, out_0, layers[1][2], partial, up, x_rows, layers[0][0]],
+        [rows_out, rows_out, line, line], rows_shape,
     )
     gain_sum = jnp.where(is_first, gain_0, gain_1)
     shift_sum = jnp.where(is_first, shift_0, shift_1)
-    cut = lambda x, i: x[i * group : (i + 1) * group]
-
+    norms = small_exchange(
+        jnp.concatenate([gain_sum, shift_sum], axis=0), ("dp", "tensor"), 4, True
+    )
+
+    blocks = micro * n_dp
+    segment = jnp.swapaxes(all_segments, 0, 1).reshape(blocks, rows)
+    all_tables, all_allowed = rotary_tables(segment), allowed_of(segment)
     column = lax.axis_index("dp") * (width // n_dp)
     slice_of = lambda x: lax.dynamic_slice_in_dim(x, column, width // n_dp, 1)
-    total = None
-    for index in range(count):
-        now, then = cut(early, index), cut(late, index)
-        blocks = group * n_dp
-        normed_all = settled(jnp.where(is_first, now, then).reshape(blocks * rows, width))
-        up_all = settled(jnp.where(is_first, then, now).reshape(blocks * rows, width))
-        segment = all_segments[:, index * group : (index + 1) * group]
-        segment = jnp.swapaxes(segment, 0, 1).reshape(blocks, rows)
-        tables, allowed = rotary_tables(segment), allowed_of(segment)
-        grad_att = mm(up_all, proj_dense, ((1,), (1,))).astype(bf16)
-        *pieces, attended, s_q, s_v = attention_call(
-            functools.partial(attention_backward_kernel, True),
-            projections(normed_all, proj_qkv, bias_qv) + [grad_att], tables, allowed, 4, 2,
-        )
-        pre_act = mm(normed_all, fc_one) + bias_fc
-        activation = settled(jax.nn.gelu(pre_act, approximate=True).astype(bf16))
-        grad_pre = gelu_grad(pre_act, mm(up_all, fc_two, ((1,), (1,))))
-        grad_fc_bias = jnp.sum(grad_pre, axis=0)
-        grad_pre, grad_fc_bias = settled((grad_pre.astype(bf16), grad_fc_bias))
+    inner = ((0,), (0,))
+
+    def weight_terms(first, early, late, known, tables, allowed):
+        normed_all, up_all = (early, late) if first else (late, early)
+        *pieces, attended, s_q, s_v, s_up = attention_again(
+            normed_all, up_all, proj_qkv, proj_dense, bias_qv, tables, allowed
+        )
+        activation, grad_pre, grad_fc_bias = hidden_call(
+            first, late, known, fc_two if first else fc_one, bias_fc
+        )
         normed_part, up_part = slice_of(normed_all), slice_of(up_all)
-        inner = ((0,), (0,))
-        terms = [mm(normed_part, p, inner) for p in pieces] + [
+        return (
+            jnp.stack([mm(normed_part, p, inner) for p in pieces]),
             mm(attended, up_part, inner),
             mm(normed_part, grad_pre, inner),
             mm(activation, up_part, inner),
-            s_q[0],
-            s_v[0],
-            jnp.sum(up_all.astype(f32), axis=0),
-            grad_fc_bias,
-        ]
-        total = terms if total is None else [a + b for a, b in zip(total, terms)]
-    g_q, g_k, g_v, grad_dense, grad_fc_one, grad_fc_two, s_q, s_v, grad_out, grad_fc_bias = total
-    norms = small_exchange(
-        jnp.concatenate([gain_sum, shift_sum], axis=0), ("dp", "tensor"), 4, True
-    )
+            jnp.concatenate([s_q, s_v], axis=0),
+            s_up[0],
+            grad_fc_bias[0],
+        )
+
+    parts = -(-tokens // 4096)
+    arrays = [early, late.reshape(tokens, width), known, all_tables, all_allowed]
+    total = None
+    for part in range(parts):
+        pick = lambda x: x[part * x.shape[0] // parts : (part + 1) * x.shape[0] // parts]
+        picked = [pick(x) for x in arrays]
+        if total is not None:
+            total, picked = settled((total, picked))
+        terms = lax.cond(
+            is_first,
+            functools.partial(weight_terms, True),
+            functools.partial(weight_terms, False),
+            *picked,
+        )
+        total = terms if total is None else [x + y for x, y in zip(total, terms)]
+    grad_qkv, grad_dense, grad_fc_one, grad_fc_two, grad_qv, grad_out, grad_fc_bias = total
 
     layer_out = jnp.where(is_first, out_0, out_1)
     in_grad = jnp.where(is_first, grad_0, grad_1)
@@ -611,8 +800,8 @@
         in_grad[None],
         norms[:1],
         norms[1:],
-        jnp.stack([g_q, g_k, g_v])[None],
-        jnp.stack([s_q, s_v])[None],
+        grad_qkv[None],
+        grad_qv[None],
         grad_dense[None],
         grad_out[None],
         grad_fc_one[None],

time: 527 us -> 486 us (0.922)
  matrix products: 207 us -> 126 us
  Pallas kernels: 219 us -> 261 us
  other arithmetic: 41.2 us -> 29.9 us
  loops' own time: 0 us -> 9.26 us
  waiting for transfers between devices: 9.19 us -> 0.71 us
  local copies, waits for them, and re-layouts: 25.9 us -> 33 us
    pallas_call x4 -> x5, Pallas kernels: 131 us -> 213 us  [the longest x3 121 us: sum_call(): pl.pallas_call(functools.partial(kernel, n), out_shape=outs, in_specs=[vm...]
    dot_general x36 -> x31, matrix products: 207 us -> 126 us  [mm(): lax.dot_general(left, right, (dims, ((), ())), preferred_element_type=jnp...]
    pallas_call x5 -> x4, Pallas kernels: 65 us -> 24.9 us  [attention_call(): pl.pallas_call(kernel, grid=(blocks,), in_specs=[block] * len(arrays) + [...]
    another operation x0 -> x2, loops' own time: none -> 9.26 us  [the longest x1 9.09 us: per_device(): lax.cond(is_first, functools.partial(weight_terms, True), functools.parti...]
    all_gather x1, waiting for transfers between devices: 9.14 us -> 0.67 us  [gather(): return lax.all_gather(x, ('dp', 'tensor'), axis=1, tiled=True)]
    select_n x1 -> x0, other arithmetic: 6.48 us -> none  [per_device(): jnp.where(is_first, then, now).reshape(blocks * rows, width)]
    unnamed x93 -> x91, local copies, waits for them, and re-layouts: 8.07 us -> 12.9 us
  transfers between devices with their start and end apart: 7 -> 7, of which waited for: 1 -> 1; matrix products, arithmetic and copies ran while one was open for 25% -> 30% of each run, Pallas kernels for 35% -> 35%
where the time goes in v5:
time: 486 us; the launch traced here: 477 us
  Pallas kernels  261 us (54%)
  matrix products  126 us (26%)
  local copies, waits for them, and re-layouts  33 us (7%)
  other arithmetic  29.9 us (6%)
  between operations  14.9 us (3%)
  loops' own time  9.26 us (2%)
    dot_general x31, matrix products, mm(): lax.dot_general(left, right, (dims, ((), ())), preferred_element_type=jnp...  126 us
    pallas_call x3, Pallas kernels, sum_call(): pl.pallas_call(functools.partial(kernel, n), out_shape=outs, in_specs=[vm...  121 us
    pallas_call x1, Pallas kernels, attention_again(): pl.pallas_call(attention_again_kernel, grid=(blocks // count,), in_specs=...  57.4 us
    pallas_call x1, Pallas kernels, hidden_call(): pl.pallas_call(functools.partial(hidden_kernel, first), grid=(units // ch...  34.7 us
    pallas_call x4, Pallas kernels, attention_call(): pl.pallas_call(kernel, grid=(blocks,), in_specs=[block] * len(arrays) + [...  24.9 us
    pallas_call x2, Pallas kernels, small_exchange(): pl.pallas_call(functools.partial(exchange_kernel, axes, add), out_shape=j...  23.2 us
    dynamic_slice x6, local copies, waits for them, and re-layouts, half(): return lax.dynamic_slice_in_dim(x, which * size, size, axis)  15.6 us
    unnamed x91, local copies, waits for them, and re-layouts  12.9 us
  transfers between devices with their start and end apart: 7, of which 1 were waited for; matrix products, arithmetic and copies ran while one was open for 30% of the time, Pallas kernels for 35%

profile of v5, /device:TPU:0, one launch (start us, length us, event | category | flops | bytes accessed | tf_op | source)
XLA Modules:
  0.0 476.5 jit_solution(4984462425614470328)
XLA Ops:
  17.8 4.9 %dynamic-slice_bitcast_fusion = bf16[1024,2048]{1,0:T(8,128)(2,1)} fusion(bf16[1,2048,2048]{2,1,0:T(8,128)(2,1)} %param.27, s32[]{:T(128)S(6)} %select_n.165), kind=kLoop, calls=%fused_computation.59 | loop fusion | bytes 8388612 | tf_op jit(solution)/shard_map/dynamic_slice | solution.py:644
  42.4 6.2 %bitcast_select_fusion.4 = (bf16[3,2048,256]{2,1,0:T(8,128)(2,1)}, bf16[3,2048,256]{2,1,0:T(8,128)(2,1)S(1)}) fusion(bf16[3,2048,256]{2,1,0:T(8,128)(2,1)} %collective-permute-done.1, pred[]{:T(512)S(6)} %eq.57, bf16[1,3,2048,512]{3,2,1,0:T(8,128)(2,1)} %param.21, s32[]{:T(128)S(6)} %select_n.157, pred[]{:T(512)S(6)} %eq.25), kind=kLoop, calls=%fused_computation.62 | loop fusion | flops 3145728 | bytes 12582918 | tf_op jit(solution)/shard_map/jit(_where)/select_n | solution.py:650
  53.4 6.2 %shard_map.203 = (bf16[512,256]{1,0:T(8,128)(2,1)}, bf16[512,256]{1,0:T(8,128)(2,1)}, bf16[512,256]{1,0:T(8,128)(2,1)}, bf16[512,256]{1,0:T(8,128)(2,1)}) custom-call(f32[512,256]{1,0:T(8,128)} %convolution_add_fusion.4.qf_ref, f32[512,256]{1,0:T(8,128)} %fusion.62.kf_ref, f32[512,256]{1,0:T(8,128)} %convolution_add_fusion.3.vf_ref, ...), custom_call_target="tpu_custom_call" | custom-call | flops 335544320 | bytes 2097152 | tf_op jit(solution)/shard_map/pallas_call | solution.py:224
  59.6 7.1 %multiply_convert_fusion.1 = (bf16[512,1024]{1,0:T(8,128)(2,1)S(1)}, f32[512,1024]{1,0:T(8,128)}) fusion(f32[1024]{0:T(1024)S(1)} %bitcast.259, bf16[512,2048]{1,0:T(8,128)(2,1)} %bitcast.236, bf16[2048,1024]{1,0:T(8,128)(2,1)} %collective-permute-done.3, pred[]{:T(512)S(6)} %eq.25, bf16[1,2048,2048]{2,1,0:T(8,128)(2,1)} %param.25, s32[]{:T(128)S(6)} %select_n.164), kind=kOutput, calls=%fused_computation.84 | convolution fusion | flops 2154823680 | bytes 13635589 | tf_op jit(solution)/shard_map/dot_general | solution.py:47
  66.7 4.7 fusion.57
  72.3 37.2 %shard_map.204 = (bf16[4,32,2048]{2,1,0:T(8,128)(2,1)S(1)}, bf16[4,4,32,2048]{3,2,1,0:T(8,128)(2,1)S(1)}) custom-call(bf16[4,4,32,2048]{3,2,1,0:T(8,128)(2,1)S(1)} %bitcast.202, bf16[4,32,2048]{2,1,0:T(8,128)(2,1)S(1)} %constant_dynamic-slice_fusion.3.resid_ref.hidden_ref, f32[1,2048]{1,0:T(1,128)S(1)} %get-tuple-element.211.bias_ref, ...), custom_call_target="tpu_custom_call" | custom-call | tf_op jit(solution)/shard_map/pallas_call | solution.py:478
  109.6 6.9 %multiply_convert_fusion = (bf16[512,1024]{1,0:T(8,128)(2,1)}, f32[512,1024]{1,0:T(8,128)S(1)}) fusion(f32[1024]{0:T(1024)S(1)} %bitcast.261, bf16[512,2048]{1,0:T(8,128)(2,1)S(1)} %bitcast.209, bf16[2048,1024]{1,0:T(8,128)(2,1)} %collective-permute-done.3, pred[]{:T(512)S(6)} %eq.57, bf16[1,2048,2048]{2,1,0:T(8,128)(2,1)S(1)} %bitcast.229, s32[]{:T(128)S(6)} %select_n.164), kind=kOutput, calls=%fused_computation.83 | convolution fusion | flops 2154823680 | bytes 13635589 | tf_op jit(solution)/shard_map/dot_general | solution.py:47
  116.5 7.1 %fusion.51 = bf16[512,1024]{1,0:T(8,128)(2,1)} fusion(f32[512,1024]{1,0:T(8,128)S(1)} %get-tuple-element.230, bf16[512,2048]{1,0:T(8,128)(2,1)S(1)} %bitcast.205, bf16[1024,2048]{1,0:T(8,128)(2,1)} %collective-permute-done.4, pred[]{:T(512)S(6)} %eq.57, bf16[1,2048,2048]{2,1,0:T(8,128)(2,1)S(1)} %bitcast.232, s32[]{:T(128)S(6)} %select_n.164, ...), kind=kOutput, calls=%fused_computation.82 | convolution fusion | flops 2160590848 | bytes 13635589 | tf_op jit(solution)/shard_map/dot_general | solution.py:47
  128.1 5.7 %shard_map.205 = (bf16[512,256]{1,0:T(8,128)(2,1)}, bf16[512,256]{1,0:T(8,128)(2,1)}, bf16[512,256]{1,0:T(8,128)(2,1)}, bf16[512,256]{1,0:T(8,128)(2,1)}) custom-call(f32[512,256]{1,0:T(8,128)} %convolution_add_fusion.2.qf_ref, f32[512,256]{1,0:T(8,128)} %fusion.66.kf_ref, f32[512,256]{1,0:T(8,128)} %convolution_add_fusion.1.vf_ref, ...), custom_call_target="tpu_custom_call" | custom-call | flops 335544320 | bytes 2097152 | tf_op jit(solution)/shard_map/pallas_call | solution.py:224
  133.8 6.5 %shard_map.206 = (bf16[512,256]{1,0:T(8,128)(2,1)}, bf16[512,256]{1,0:T(8,128)(2,1)}, bf16[512,256]{1,0:T(8,128)(2,1)}) custom-call(bf16[512,256]{1,0:T(8,128)(2,1)} %get-tuple-element.162.q_ref, bf16[512,256]{1,0:T(8,128)(2,1)} %get-tuple-element.163.k_ref, bf16[512,256]{1,0:T(8,128)(2,1)} %get-tuple-element.164.v_ref, ...), custom_call_target="tpu_custom_call" | custom-call | flops 335544320 | bytes 2097152 | tf_op jit(solution)/shard_map/pallas_call | solution.py:224
  143.8 5.9 %fusion.54 = f32[512,2048]{1,0:T(8,128)S(1)} fusion(bf16[512,1024]{1,0:T(8,128)(2,1)S(1)} %copy-done.46, bf16[2048,1024]{1,0:T(8,128)(2,1)} %collective-permute-done.3, pred[]{:T(512)S(6)} %eq.57, bf16[1,2048,2048]{2,1,0:T(8,128)(2,1)} %param.25, s32[]{:T(128)S(6)} %select_n.164), kind=kOutput, calls=%fused_computation.96 | convolution fusion | flops 2149580800 | bytes 13631493 | tf_op jit(solution)/shard_map/dot_general | solution.py:47
  150.5 37.9 %shard_map.207 = (bf16[4,32,2048]{2,1,0:T(8,128)(2,1)S(1)}, f32[1,2048]{1,0:T(1,128)S(1)}, f32[1,2048]{1,0:T(1,128)S(1)}, bf16[4,4,32,2048]{3,2,1,0:T(8,128)(2,1)S(1)}) custom-call(bf16[4,4,32,2048]{3,2,1,0:T(8,128)(2,1)S(1)} %bitcast.203, bf16[4,4,32,2048]{3,2,1,0:T(8,128)(2,1)S(1)} %bitcast.206, ...), custom_call_target="tpu_custom_call" | custom-call | tf_op jit(solution)/shard_map/pallas_call | solution.py:478
  192.4 6.9 %shard_map.211 = s32[4,4,128]{2,1,0:T(4,128)} custom-call(s32[4,128]{1,0:T(4,128)} %x_ref.1), custom_call_target="tpu_custom_call" | custom-call | tf_op jit(solution)/shard_map/pallas_call | solution.py:601
  209.7 4.9 %fusion.58 = f32[512,2048]{1,0:T(8,128)S(1)} fusion(bf16[512,1024]{1,0:T(8,128)(2,1)S(1)} %copy-done.43, bf16[1024,2048]{1,0:T(8,128)(2,1)} %collective-permute-done.4, pred[]{:T(512)S(6)} %eq.57, bf16[1,2048,2048]{2,1,0:T(8,128)(2,1)S(1)} %bitcast.234, s32[]{:T(128)S(6)} %select_n.164), kind=kOutput, calls=%fused_computation.100 | convolution fusion | flops 2149580800 | bytes 13631493 | tf_op jit(solution)/shard_map/dot_general | solution.py:47
  221.8 22.5 %conditional.2 = (f32[2048,2048]{1,0:T(8,128)}) conditional(s32[]{:T(128)} %convert_element_type.79, (bf16[2048,2048]{1,0:T(8,128)(2,1)S(1)}, bf16[2048,2048]{1,0:T(8,128)(2,1)S(1)}) %tuple.89, (bf16[2048,2048]{1,0:T(8,128)(2,1)S(1)}, bf16[2048,2048]{1,0:T(8,128)(2,1)}, f32[1,2048]{1,0:T(1,128)S(1)}) %tuple.90), branch_computations={%region_3.4_spmd, %region_4.5_spmd} | conditional | flops 17184063488 | bytes 33562632 | solution.py:735
  221.8 22.3 %convolution_add_fusion = f32[2048,2048]{1,0:T(8,128)} fusion(bf16[2048,2048]{1,0:T(8,128)(2,1)S(1)} %get-tuple-element.66, bf16[2048,2048]{1,0:T(8,128)(2,1)} %get-tuple-element.67, f32[2048]{0:T(1024)S(1)} %bitcast.255), kind=kOutput, calls=%fused_computation | convolution fusion | flops 17184063488 | bytes 33562624 | tf_op jit(solution)/shard_map/cond/branch_1_fun/dot_general | solution.py:47
  247.6 6.5 %shard_map.208 = (bf16[512,256]{1,0:T(8,128)(2,1)}, bf16[512,256]{1,0:T(8,128)(2,1)}, bf16[512,256]{1,0:T(8,128)(2,1)}) custom-call(bf16[512,256]{1,0:T(8,128)(2,1)} %get-tuple-element.171.q_ref, bf16[512,256]{1,0:T(8,128)(2,1)} %get-tuple-element.172.k_ref, bf16[512,256]{1,0:T(8,128)(2,1)} %get-tuple-element.173.v_ref, ...), custom_call_target="tpu_custom_call" | custom-call | flops 335544320 | bytes 2097152 | tf_op jit(solution)/shard_map/pallas_call | solution.py:224
  264.2 45.6 %shard_map.209 = (bf16[4,32,2048]{2,1,0:T(8,128)(2,1)S(1)}, bf16[4,32,2048]{2,1,0:T(8,128)(2,1)S(1)}, f32[1,2048]{1,0:T(1,128)S(1)}, f32[1,2048]{1,0:T(1,128)S(1)}) custom-call(bf16[4,4,32,2048]{3,2,1,0:T(8,128)(2,1)S(1)} %bitcast.200, bf16[4,32,2048]{2,1,0:T(8,128)(2,1)S(1)} %get-tuple-element.160.hidden_ref.resid_ref, ...), custom_call_target="tpu_custom_call" | custom-call | tf_op jit(solution)/shard_map/pallas_call | solution.py:478
  312.1 16.3 %shard_map.210 = f32[2,2048]{1,0:T(2,128)} custom-call(f32[2,2048]{1,0:T(2,128)} %pad_maximum_fusion.x_ref), custom_call_target="tpu_custom_call" | custom-call | tf_op jit(solution)/shard_map/pallas_call | solution.py:601
  332.6 132.4 %conditional.3 = (f32[1,3,512,512]{3,2,1,0:T(8,128)S(1)}, f32[1,512,512]{2,1,0:T(8,128)}, f32[1,512,2048]{2,1,0:T(8,128)S(1)}, f32[1,2048,512]{2,1,0:T(8,128)S(1...) conditional(s32[]{:T(128)} %convert_element_type.79, (s32[]{:T(128)}, ...), branch_computations={%region_6.7_spmd, %region_7.8_spmd} | conditional | flops 47246213120 | bytes 190865696 | solution.py:787
  341.3 57.4 %branch_1_fun.2 = (bf16[2048,512]{1,0:T(8,128)(2,1)}, bf16[2048,512]{1,0:T(8,128)(2,1)}, bf16[2048,512]{1,0:T(8,128)(2,1)}, bf16[2048,512]{1,0:T(8,128)(2,1)}, f...) custom-call(bf16[2048,2048]{1,0:T(8,128)(2,1)} %get-tuple-element.90.normed_ref, ...), custom_call_target="tpu_custom_call" | custom-call | flops 17179869184 | bytes 25165824 | tf_op jit(solution)/shard_map/cond/branch_1_fun/pallas_call | solution.py:197
  415.5 34.7 %branch_1_fun.3 = (bf16[2048,2048]{1,0:T(8,128)(2,1)}, bf16[2048,2048]{1,0:T(8,128)(2,1)}, f32[1,2048]{1,0:T(1,128)}) custom-call(bf16[2048,2048]{1,0:T(8,128)(2,1)} %get-tuple-element.92.up_ref.x_ref, f32[2048,2048]{1,0:T(8,128)} %get-tuple-element.102.known_ref, bf16[2048,2048]{1,0:T(8,128)(2,1)} %get-tuple-element.103.w_ref, ...), custom_call_target="tpu_custom_call" | custom-call | flops 17179869184 | bytes 50331648 | tf_op jit(solution)/shard_map/cond/branch_1_fun/pallas_call | solution.py:538
  450.1 8.1 %convolution_bitcast_fusion.5 = f32[1,2048,512]{2,1,0:T(8,128)S(1)} fusion(bf16[2048,2048]{1,0:T(8,128)(2,1)} %get-tuple-element.106, bf16[2048,2048]{1,0:T(8,128)(2,1)} %get-tuple-element.92.up_ref.x_ref, s32[]{:T(128)S(6)} %select_n.115), kind=kOutput, calls=%fused_computation.22 | convolution fusion | flops 4294967296 | bytes 14680068 | tf_op jit(solution)/shard_map/cond/branch_1_fun/dot_general | solution.py:47
  458.2 6.6 %convolution_bitcast_fusion.6 = f32[1,512,2048]{2,1,0:T(8,128)S(1)} fusion(bf16[2048,2048]{1,0:T(8,128)(2,1)S(1)} %copy-done.40, bf16[2048,2048]{1,0:T(8,128)(2,1)} %get-tuple-element.90.normed_ref, s32[]{:T(128)S(6)} %select_n.115), kind=kOutput, calls=%fused_computation.23 | convolution fusion | flops 4294967296 | bytes 14680068 | tf_op jit(solution)/shard_map/cond/branch_1_fun/dot_general | solution.py:47
  (200 shorter events, 106.8 us)
Async XLA Ops:
  7.2 185.2 %all-gather.3.cloned.1.call-start = ((), (), s32[]{:S(2)}) async-start(), calls=%async_computation | async-start | bytes 10485760 | tf_op jit(solution)/shard_map/all_gather | solution.py:681
  10.7 13.1 %collective-permute-start = (f32[1,9216]{1,0:T(1,128)S(1)}, f32[1,9216]{1,0:T(1,128)S(1)}, u32[]{:S(2)}, u32[]{:S(2)}) collective-permute-start(f32[1,9216]{1,0:T(1,128)S(1)} %bitcast.246), channel_id=1, source_target_pairs={{0,16},{16,0},{1,17},{17,1},{2,18},{18,2},{3,19},{19,3},{4,20},{20... | collective-permute-start | bytes 110600 | tf_op jit(solution)/shard_map/ppermute | solution.py:640
  13.5 25.5 %collective-permute-start.2 = (bf16[256,2048]{1,0:T(8,128)(2,1)}, bf16[256,2048]{1,0:T(8,128)(2,1)}, u32[]{:S(2)}, u32[]{:S(2)}) collective-permute-start(bf16[256,2048]{1,0:T(8,128)(2,1)} %dynamic-slice_bitcast_fusion.3), channel_id=1, source_target_pairs={{0,16},{16,0},{1,17},{17,1},{2,18},{18,2},{3,19},{19,3},{4,20},{20... | collective-permute-start | bytes 3145736 | tf_op jit(solution)/shard_map/ppermute | solution.py:640
  17.3 25.1 %collective-permute-start.1 = (bf16[3,2048,256]{2,1,0:T(8,128)(2,1)}, bf16[3,2048,256]{2,1,0:T(8,128)(2,1)}, u32[]{:S(2)}, u32[]{:S(2)}) collective-permute-start(bf16[3,2048,256]{2,1,0:T(8,128)(2,1)} %dynamic-slice_bitcast_fusion.2), channel_id=1, source_target_pairs={{0,16},{16,0},{1,17},{17,1},{2,18},{18,2},{3,19},{19,3},{4,20},{20... | collective-permute-start | bytes 9437192 | tf_op jit(solution)/shard_map/ppermute | solution.py:640
  17.8 5.0 %copy-start.9 = (bf16[4,128,2048]{2,1,0:T(8,128)(2,1)S(1)}, bf16[4,128,2048]{2,1,0:T(8,128)(2,1)}, u32[]{:S(2)}) copy-start(bf16[4,128,2048]{2,1,0:T(8,128)(2,1)} %param.16) | copy-start | bytes 6291460
  22.7 44.0 %collective-permute-start.4 = (bf16[1024,2048]{1,0:T(8,128)(2,1)}, bf16[1024,2048]{1,0:T(8,128)(2,1)}, u32[]{:S(2)}, u32[]{:S(2)}) collective-permute-start(bf16[1024,2048]{1,0:T(8,128)(2,1)} %dynamic-slice_bitcast_fusion), channel_id=1, source_target_pairs={{0,16},{16,0},{1,17},{17,1},{2,18},{18,2},{3,19},{19,3},{4,20},{20... | collective-permute-start | bytes 12582920 | tf_op jit(solution)/shard_map/ppermute | solution.py:640
  28.4 304.1 %all-gather.5.cloned.1.call-start = ((), (), s32[]{:S(2)}) async-start(), calls=%async_computation.1 | async-start | bytes 8912896 | tf_op jit(solution)/shard_map/all_gather | solution.py:679
  33.1 26.5 %collective-permute-start.3 = (bf16[2048,1024]{1,0:T(8,128)(2,1)}, bf16[2048,1024]{1,0:T(8,128)(2,1)}, u32[]{:S(2)}, u32[]{:S(2)}) collective-permute-start(bf16[2048,1024]{1,0:T(8,128)(2,1)} %dynamic-slice_bitcast_fusion.1), channel_id=1, source_target_pairs={{0,16},{16,0},{1,17},{17,1},{2,18},{18,2},{3,19},{19,3},{4,20},{20... | collective-permute-start | bytes 12582920 | tf_op jit(solution)/shard_map/ppermute | solution.py:640
  42.4 6.2 %copy-start.22 = (bf16[4,128,2048]{2,1,0:T(8,128)(2,1)S(1)}, bf16[4,128,2048]{2,1,0:T(8,128)(2,1)}, u32[]{:S(2)}) copy-start(bf16[4,128,2048]{2,1,0:T(8,128)(2,1)} %get-tuple-element.198) | copy-start | bytes 6291460
  59.6 49.9 %slice-start.2 = ((s8[8388608]{0:T(1024)(128)(4,1)}), s8[4194304]{0:T(1024)(128)(4,1)S(1)}, s32[]{:S(2)}) async-start(s8[8388608]{0:T(1024)(128)(4,1)} %bitcast.228), calls=%async_computation.4 | async-start | bytes 8388608
  66.7 42.8 %slice-start.3 = ((s8[8388608]{0:T(1024)(128)(4,1)}), s8[4194304]{0:T(1024)(128)(4,1)S(1)}, s32[]{:S(2)}) async-start(s8[8388608]{0:T(1024)(128)(4,1)} %bitcast.228), calls=%async_computation.5 | async-start | bytes 8388608
  72.3 44.1 %slice-start.4 = ((s8[8388608]{0:T(1024)(128)(4,1)}), s8[4194304]{0:T(1024)(128)(4,1)S(1)}, s32[]{:S(2)}) async-start(s8[8388608]{0:T(1024)(128)(4,1)} %bitcast.231), calls=%async_computation.6 | async-start | bytes 8388608
  109.5 17.1 %copy-start.6 = (bf16[4,4,32,2048]{3,2,1,0:T(8,128)(2,1)}, bf16[4,4,32,2048]{3,2,1,0:T(8,128)(2,1)S(1)}, u32[]{:S(2)}) copy-start(bf16[4,4,32,2048]{3,2,1,0:T(8,128)(2,1)S(1)} %get-tuple-element.161) | copy-start | bytes 6291460
  109.5 6.9 %slice-start.5 = ((s8[8388608]{0:T(1024)(128)(4,1)}), s8[4194304]{0:T(1024)(128)(4,1)S(1)}, s32[]{:S(2)}) async-start(s8[8388608]{0:T(1024)(128)(4,1)} %bitcast.231), calls=%async_computation.7 | async-start | bytes 8388608
  116.4 7.1 %copy-start.12 = (bf16[3,2048,256]{2,1,0:T(8,128)(2,1)S(1)}, bf16[3,2048,256]{2,1,0:T(8,128)(2,1)}, u32[]{:S(2)}) copy-start(bf16[3,2048,256]{2,1,0:T(8,128)(2,1)} %get-tuple-element.199) | copy-start | bytes 9437188
  143.8 5.9 %copy-start.24 = (bf16[512,256]{1,0:T(8,128)(2,1)S(1)}, bf16[512,256]{1,0:T(8,128)(2,1)}, u32[]{:S(2)}) copy-start(bf16[512,256]{1,0:T(8,128)(2,1)} %get-tuple-element.167) | copy-start | bytes 786436
  204.2 5.4 %slice-start.6 = ((s8[8388608]{0:T(1024)(128)(4,1)}), s8[4194304]{0:T(1024)(128)(4,1)S(1)}, s32[]{:S(2)}) async-start(s8[8388608]{0:T(1024)(128)(4,1)} %bitcast.233), calls=%async_computation.8 | async-start | bytes 8388608
  204.7 5.0 %slice-start.7 = ((s8[8388608]{0:T(1024)(128)(4,1)}), s8[4194304]{0:T(1024)(128)(4,1)S(1)}, s32[]{:S(2)}) async-start(s8[8388608]{0:T(1024)(128)(4,1)} %bitcast.233), calls=%async_computation.9 | async-start | bytes 8388608
  209.6 4.9 %copy-start.15 = (bf16[1,512,2048]{2,1,0:T(8,128)(2,1)S(1)}, bf16[1,512,2048]{2,1,0:T(8,128)(2,1)}, u32[]{:S(2)}) copy-start(bf16[1,512,2048]{2,1,0:T(8,128)(2,1)} %param.23) | copy-start | bytes 6291460
  209.6 4.9 %copy-start.25 = (bf16[512,256]{1,0:T(8,128)(2,1)S(1)}, bf16[512,256]{1,0:T(8,128)(2,1)}, u32[]{:S(2)}) copy-start(bf16[512,256]{1,0:T(8,128)(2,1)} %get-tuple-element.177) | copy-start | bytes 786436
  214.6 7.2 %slice-start = ((s8[8388608]{0:T(1024)(128)(4,1)}), s8[4194304]{0:T(1024)(128)(4,1)S(1)}, s32[]{:S(2)}) async-start(s8[8388608]{0:T(1024)(128)(4,1)} %bitcast.220), calls=%async_computation.2 | async-start | bytes 8388608
  311.4 21.1 %copy-start.16 = (bf16[1,512,2048]{2,1,0:T(8,128)(2,1)S(1)}, bf16[1,512,2048]{2,1,0:T(8,128)(2,1)}, u32[]{:S(2)}) copy-start(bf16[1,512,2048]{2,1,0:T(8,128)(2,1)} %param.23) | copy-start | bytes 6291460
  311.4 21.1 %copy-start.31 = (f32[1,2,512]{2,1,0:T(2,128)S(1)}, f32[1,2,512]{2,1,0:T(2,128)}, u32[]{:S(2)}) copy-start(f32[1,2,512]{2,1,0:T(2,128)} %param.22) | copy-start | bytes 12292
  450.1 8.1 %copy-start.40 = (bf16[2048,2048]{1,0:T(8,128)(2,1)S(1)}, bf16[2048,2048]{1,0:T(8,128)(2,1)}, u32[]{:S(2)}) copy-start(bf16[2048,2048]{1,0:T(8,128)(2,1)} %get-tuple-element.105) | copy-start | bytes 25165828 | tf_op jit(solution)/shard_map/cond
  (32 other events, 92.9 us)
Sparse Core Ops, SparseCore 0:
  28.5 152.3 all-gather.2
  192.5 139.9 all-gather.4

commit v6 on v5

--- a/solution.py
+++ b/solution.py
@@ -526,7 +526,7 @@
 def hidden_call(first, x, known, weight, bias):
     tokens, width = x.shape
     units = known.shape[-1]
-    tile, chunk = 256, min(1024, units)
+    tile, chunk = 512 if tokens % 512 == 0 else 256, min(1024, units)
     flat = pl.BlockSpec((tile, chunk), lambda j, i: (i, j))
     line = pl.BlockSpec((1, chunk), lambda j, i: (0, j))
     w_spec = (

time: 486 us -> 484 us (level)
  the two profiles are of different devices: /device:TPU:0 before, /device:TPU:9 now
where the time goes in v6:
time: 484 us; the launch traced here: 478 us
  Pallas kernels  255 us (53%)
  matrix products  132 us (27%)
  local copies, waits for them, and re-layouts  35.7 us (7%)
  other arithmetic  30 us (6%)
  between operations  15 us (3%)
  loops' own time  8.45 us (2%)
    dot_general x31, matrix products, mm(): lax.dot_general(left, right, (dims, ((), ())), preferred_element_type=jnp...  132 us
    pallas_call x3, Pallas kernels, sum_call(): pl.pallas_call(functools.partial(kernel, n), out_shape=outs, in_specs=[vm...  114 us
    pallas_call x1, Pallas kernels, attention_again(): pl.pallas_call(attention_again_kernel, grid=(blocks // count,), in_specs=...  57.4 us
    pallas_call x1, Pallas kernels, hidden_call(): pl.pallas_call(functools.partial(hidden_kernel, first), grid=(units // ch...  34 us
    pallas_call x2, Pallas kernels, small_exchange(): pl.pallas_call(functools.partial(exchange_kernel, axes, add), out_shape=j...  25.2 us
    pallas_call x4, Pallas kernels, attention_call(): pl.pallas_call(kernel, grid=(blocks,), in_specs=[block] * len(arrays) + [...  24.7 us
    dynamic_slice x6, local copies, waits for them, and re-layouts, half(): return lax.dynamic_slice_in_dim(x, which * size, size, axis)  15.6 us
    unnamed x91, local copies, waits for them, and re-layouts  14.3 us
  transfers between devices with their start and end apart: 7, of which 0 were waited for; matrix products, arithmetic and copies ran while one was open for 31% of the time, Pallas kernels for 34%

profile of v6, /device:TPU:9, one launch (start us, length us, event | category | flops | bytes accessed | tf_op | source)
XLA Modules:
  0.0 477.9 jit_solution(4007200640982029147)
XLA Ops:
  18.0 4.9 %dynamic-slice_bitcast_fusion = bf16[1024,2048]{1,0:T(8,128)(2,1)} fusion(bf16[1,2048,2048]{2,1,0:T(8,128)(2,1)} %param.27, s32[]{:T(128)S(6)} %select_n.165), kind=kLoop, calls=%fused_computation.59 | loop fusion | bytes 8388612 | tf_op jit(solution)/shard_map/dynamic_slice | solution.py:644
  28.6 4.6 dynamic-slice_bitcast_fusion.1
  42.1 6.0 %bitcast_select_fusion.4 = (bf16[3,2048,256]{2,1,0:T(8,128)(2,1)}, bf16[3,2048,256]{2,1,0:T(8,128)(2,1)S(1)}) fusion(bf16[3,2048,256]{2,1,0:T(8,128)(2,1)} %collective-permute-done.1, pred[]{:T(512)S(6)} %eq.57, bf16[1,3,2048,512]{3,2,1,0:T(8,128)(2,1)} %param.21, s32[]{:T(128)S(6)} %select_n.157, pred[]{:T(512)S(6)} %eq.25), kind=kLoop, calls=%fused_computation.62 | loop fusion | flops 3145728 | bytes 12582918 | tf_op jit(solution)/shard_map/jit(_where)/select_n | solution.py:650
  53.0 5.9 %shard_map.203 = (bf16[512,256]{1,0:T(8,128)(2,1)}, bf16[512,256]{1,0:T(8,128)(2,1)}, bf16[512,256]{1,0:T(8,128)(2,1)}, bf16[512,256]{1,0:T(8,128)(2,1)}) custom-call(f32[512,256]{1,0:T(8,128)} %convolution_add_fusion.4.qf_ref, f32[512,256]{1,0:T(8,128)} %fusion.62.kf_ref, f32[512,256]{1,0:T(8,128)} %convolution_add_fusion.3.vf_ref, ...), custom_call_target="tpu_custom_call" | custom-call | flops 335544320 | bytes 2097152 | tf_op jit(solution)/shard_map/pallas_call | solution.py:224
  58.9 8.4 %multiply_convert_fusion.1 = (bf16[512,1024]{1,0:T(8,128)(2,1)S(1)}, f32[512,1024]{1,0:T(8,128)}) fusion(f32[1024]{0:T(1024)S(1)} %bitcast.259, bf16[512,2048]{1,0:T(8,128)(2,1)} %bitcast.236, bf16[2048,1024]{1,0:T(8,128)(2,1)} %collective-permute-done.3, pred[]{:T(512)S(6)} %eq.25, bf16[1,2048,2048]{2,1,0:T(8,128)(2,1)} %param.25, s32[]{:T(128)S(6)} %select_n.164), kind=kOutput, calls=%fused_computation.84 | convolution fusion | flops 2154823680 | bytes 13635589 | tf_op jit(solution)/shard_map/dot_general | solution.py:47
  67.3 6.0 %fusion.57 = f32[512,2048]{1,0:T(8,128)S(1)} fusion(bf16[512,1024]{1,0:T(8,128)(2,1)S(1)} %get-tuple-element.227, bf16[1024,2048]{1,0:T(8,128)(2,1)} %collective-permute-done.4, pred[]{:T(512)S(6)} %eq.25, bf16[1,2048,2048]{2,1,0:T(8,128)(2,1)} %param.27, s32[]{:T(128)S(6)} %select_n.164), kind=kOutput, calls=%fused_computation.99 | convolution fusion | flops 2149580800 | bytes 13631493 | tf_op jit(solution)/shard_map/dot_general | solution.py:47
  75.4 33.1 %shard_map.204 = (bf16[4,32,2048]{2,1,0:T(8,128)(2,1)S(1)}, bf16[4,4,32,2048]{3,2,1,0:T(8,128)(2,1)S(1)}) custom-call(bf16[4,4,32,2048]{3,2,1,0:T(8,128)(2,1)S(1)} %bitcast.202, bf16[4,32,2048]{2,1,0:T(8,128)(2,1)S(1)} %constant_dynamic-slice_fusion.3.resid_ref.hidden_ref, f32[1,2048]{1,0:T(1,128)S(1)} %get-tuple-element.211.bias_ref, ...), custom_call_target="tpu_custom_call" | custom-call | tf_op jit(solution)/shard_map/pallas_call | solution.py:478
  112.5 15.8 %fusion.51 = bf16[512,1024]{1,0:T(8,128)(2,1)} fusion(f32[512,1024]{1,0:T(8,128)S(1)} %get-tuple-element.230, bf16[512,2048]{1,0:T(8,128)(2,1)S(1)} %bitcast.205, bf16[1024,2048]{1,0:T(8,128)(2,1)} %collective-permute-done.4, pred[]{:T(512)S(6)} %eq.57, bf16[1,2048,2048]{2,1,0:T(8,128)(2,1)S(1)} %bitcast.232, s32[]{:T(128)S(6)} %select_n.164, ...), kind=kOutput, calls=%fused_computation.82 | convolution fusion | flops 2160590848 | bytes 13635589 | tf_op jit(solution)/shard_map/dot_general | solution.py:47
  132.7 5.7 %shard_map.205 = (bf16[512,256]{1,0:T(8,128)(2,1)}, bf16[512,256]{1,0:T(8,128)(2,1)}, bf16[512,256]{1,0:T(8,128)(2,1)}, bf16[512,256]{1,0:T(8,128)(2,1)}) custom-call(f32[512,256]{1,0:T(8,128)} %convolution_add_fusion.2.qf_ref, f32[512,256]{1,0:T(8,128)} %fusion.66.kf_ref, f32[512,256]{1,0:T(8,128)} %convolution_add_fusion.1.vf_ref, ...), custom_call_target="tpu_custom_call" | custom-call | flops 335544320 | bytes 2097152 | tf_op jit(solution)/shard_map/pallas_call | solution.py:224
  138.4 6.5 %shard_map.206 = (bf16[512,256]{1,0:T(8,128)(2,1)}, bf16[512,256]{1,0:T(8,128)(2,1)}, bf16[512,256]{1,0:T(8,128)(2,1)}) custom-call(bf16[512,256]{1,0:T(8,128)(2,1)} %get-tuple-element.162.q_ref, bf16[512,256]{1,0:T(8,128)(2,1)} %get-tuple-element.163.k_ref, bf16[512,256]{1,0:T(8,128)(2,1)} %get-tuple-element.164.v_ref, ...), custom_call_target="tpu_custom_call" | custom-call | flops 335544320 | bytes 2097152 | tf_op jit(solution)/shard_map/pallas_call | solution.py:224
  153.9 33.4 %shard_map.207 = (bf16[4,32,2048]{2,1,0:T(8,128)(2,1)S(1)}, f32[1,2048]{1,0:T(1,128)S(1)}, f32[1,2048]{1,0:T(1,128)S(1)}, bf16[4,4,32,2048]{3,2,1,0:T(8,128)(2,1)S(1)}) custom-call(bf16[4,4,32,2048]{3,2,1,0:T(8,128)(2,1)S(1)} %bitcast.203, bf16[4,4,32,2048]{3,2,1,0:T(8,128)(2,1)S(1)} %bitcast.206, ...), custom_call_target="tpu_custom_call" | custom-call | tf_op jit(solution)/shard_map/pallas_call | solution.py:478
  191.4 5.8 %shard_map.211 = s32[4,4,128]{2,1,0:T(4,128)} custom-call(s32[4,128]{1,0:T(4,128)} %x_ref.1), custom_call_target="tpu_custom_call" | custom-call | tf_op jit(solution)/shard_map/pallas_call | solution.py:601
  212.3 7.1 %fusion.44 = bf16[512,1024]{1,0:T(8,128)(2,1)} fusion(f32[512,1024]{1,0:T(8,128)S(1)} %copy-done.44, bf16[512,2048]{1,0:T(8,128)(2,1)S(1)} %bitcast.208, bf16[1024,2048]{1,0:T(8,128)(2,1)} %collective-permute-done.4, pred[]{:T(512)S(6)} %eq.25, bf16[1,2048,2048]{2,1,0:T(8,128)(2,1)S(1)} %bitcast.234, s32[]{:T(128)S(6)} %select_n.164, f32[1024]{0:T(1024)S(1)} %bitcast.260), kind=kOutput, calls=%fused_computation.75 | convolution fusion | flops 2160590848 | bytes 13635589 | tf_op jit(solution)/shard_map/dot_general | solution.py:47
  219.4 20.6 %conditional.2 = (f32[2048,2048]{1,0:T(8,128)}) conditional(s32[]{:T(128)} %convert_element_type.79, (bf16[2048,2048]{1,0:T(8,128)(2,1)S(1)}, bf16[2048,2048]{1,0:T(8,128)(2,1)S(1)}) %tuple.89, (bf16[2048,2048]{1,0:T(8,128)(2,1)S(1)}, bf16[2048,2048]{1,0:T(8,128)(2,1)}, f32[1,2048]{1,0:T(1,128)S(1)}) %tuple.90), branch_computations={%region_3.4_spmd, %region_4.5_spmd} | conditional | flops 17184063488 | bytes 33562632 | solution.py:735
  219.4 20.5 %fusion.89 = f32[2048,2048]{1,0:T(8,128)} fusion(bf16[2048,2048]{1,0:T(8,128)(2,1)S(1)} %get-tuple-element.64, bf16[2048,2048]{1,0:T(8,128)(2,1)S(1)} %get-tuple-element.65), kind=kOutput, calls=%fused_computation.183 | convolution fusion | flops 17179869184 | bytes 33554432 | tf_op jit(solution)/shard_map/cond/branch_0_fun/dot_general | solution.py:47
  243.6 6.5 %shard_map.208 = (bf16[512,256]{1,0:T(8,128)(2,1)}, bf16[512,256]{1,0:T(8,128)(2,1)}, bf16[512,256]{1,0:T(8,128)(2,1)}) custom-call(bf16[512,256]{1,0:T(8,128)(2,1)} %get-tuple-element.171.q_ref, bf16[512,256]{1,0:T(8,128)(2,1)} %get-tuple-element.172.k_ref, bf16[512,256]{1,0:T(8,128)(2,1)} %get-tuple-element.173.v_ref, ...), custom_call_target="tpu_custom_call" | custom-call | flops 335544320 | bytes 2097152 | tf_op jit(solution)/shard_map/pallas_call | solution.py:224
  254.0 5.9 %fusion.52 = f32[512,2048]{1,0:T(8,128)S(1)} fusion(bf16[512,1024]{1,0:T(8,128)(2,1)S(1)} %copy-done.45, bf16[2048,1024]{1,0:T(8,128)(2,1)} %collective-permute-done.3, pred[]{:T(512)S(6)} %eq.25, bf16[1,2048,2048]{2,1,0:T(8,128)(2,1)} %param.25, s32[]{:T(128)S(6)} %select_n.164), kind=kOutput, calls=%fused_computation.94 | convolution fusion | flops 2149580800 | bytes 13631493 | tf_op jit(solution)/shard_map/dot_general | solution.py:47
  261.5 47.3 %shard_map.209 = (bf16[4,32,2048]{2,1,0:T(8,128)(2,1)S(1)}, bf16[4,32,2048]{2,1,0:T(8,128)(2,1)S(1)}, f32[1,2048]{1,0:T(1,128)S(1)}, f32[1,2048]{1,0:T(1,128)S(1)}) custom-call(bf16[4,4,32,2048]{3,2,1,0:T(8,128)(2,1)S(1)} %bitcast.200, bf16[4,32,2048]{2,1,0:T(8,128)(2,1)S(1)} %get-tuple-element.160.hidden_ref.resid_ref, ...), custom_call_target="tpu_custom_call" | custom-call | tf_op jit(solution)/shard_map/pallas_call | solution.py:478
  311.0 19.4 %shard_map.210 = f32[2,2048]{1,0:T(2,128)} custom-call(f32[2,2048]{1,0:T(2,128)} %pad_maximum_fusion.x_ref), custom_call_target="tpu_custom_call" | custom-call | tf_op jit(solution)/shard_map/pallas_call | solution.py:601
  334.2 132.1 %conditional.3 = (f32[1,3,512,512]{3,2,1,0:T(8,128)S(1)}, f32[1,512,512]{2,1,0:T(8,128)}, f32[1,512,2048]{2,1,0:T(8,128)S(1)}, f32[1,2048,512]{2,1,0:T(8,128)S(1...) conditional(s32[]{:T(128)} %convert_element_type.79, (s32[]{:T(128)}, ...), branch_computations={%region_6.7_spmd, %region_7.8_spmd} | conditional | flops 47246213120 | bytes 190865696 | solution.py:787
  334.4 57.4 %branch_0_fun.2 = (bf16[2048,512]{1,0:T(8,128)(2,1)}, bf16[2048,512]{1,0:T(8,128)(2,1)}, bf16[2048,512]{1,0:T(8,128)(2,1)}, bf16[2048,512]{1,0:T(8,128)(2,1)}, f...) custom-call(bf16[2048,2048]{1,0:T(8,128)(2,1)} %get-tuple-element.69.normed_ref.x_ref, ...), custom_call_target="tpu_custom_call" | custom-call | flops 17179869184 | bytes 25165824 | tf_op jit(solution)/shard_map/cond/branch_0_fun/pallas_call | solution.py:197
  409.7 34.0 %branch_0_fun.3 = (bf16[2048,2048]{1,0:T(8,128)(2,1)}, bf16[2048,2048]{1,0:T(8,128)(2,1)}, f32[1,2048]{1,0:T(1,128)}) custom-call(bf16[2048,2048]{1,0:T(8,128)(2,1)} %get-tuple-element.69.normed_ref.x_ref, f32[2048,2048]{1,0:T(8,128)} %get-tuple-element.81.known_ref, bf16[2048,2048]{1,0:T(8,128)(2,1)} %get-tuple-element.82.w_ref, ...), custom_call_target="tpu_custom_call" | custom-call | flops 17179869184 | bytes 50331648 | tf_op jit(solution)/shard_map/cond/branch_0_fun/pallas_call | solution.py:538
  443.7 8.1 %convolution_bitcast_fusion = f32[1,2048,512]{2,1,0:T(8,128)S(1)} fusion(bf16[2048,2048]{1,0:T(8,128)(2,1)} %get-tuple-element.85, bf16[2048,2048]{1,0:T(8,128)(2,1)} %get-tuple-element.71.up_ref, s32[]{:T(128)S(6)} %select_n.114), kind=kOutput, calls=%fused_computation.1 | convolution fusion | flops 4294967296 | bytes 14680068 | tf_op jit(solution)/shard_map/cond/branch_0_fun/dot_general | solution.py:47
  451.8 6.6 %convolution_bitcast_fusion.1 = f32[1,512,2048]{2,1,0:T(8,128)S(1)} fusion(bf16[2048,2048]{1,0:T(8,128)(2,1)S(1)} %copy-done.39, bf16[2048,2048]{1,0:T(8,128)(2,1)} %get-tuple-element.69.normed_ref.x_ref, s32[]{:T(128)S(6)} %select_n.114), kind=kOutput, calls=%fused_computation.2 | convolution fusion | flops 4294967296 | bytes 14680068 | tf_op jit(solution)/shard_map/cond/branch_0_fun/dot_general | solution.py:47
  (200 shorter events, 105.5 us)
Async XLA Ops:
  7.2 184.2 %all-gather.3.cloned.1.call-start = ((), (), s32[]{:S(2)}) async-start(), calls=%async_computation | async-start | bytes 10485760 | tf_op jit(solution)/shard_map/all_gather | solution.py:681
  10.7 13.3 %collective-permute-start = (f32[1,9216]{1,0:T(1,128)S(1)}, f32[1,9216]{1,0:T(1,128)S(1)}, u32[]{:S(2)}, u32[]{:S(2)}) collective-permute-start(f32[1,9216]{1,0:T(1,128)S(1)} %bitcast.246), channel_id=1, source_target_pairs={{0,16},{16,0},{1,17},{17,1},{2,18},{18,2},{3,19},{19,3},{4,20},{20... | collective-permute-start | bytes 110600 | tf_op jit(solution)/shard_map/ppermute | solution.py:640
  13.7 25.5 %collective-permute-start.2 = (bf16[256,2048]{1,0:T(8,128)(2,1)}, bf16[256,2048]{1,0:T(8,128)(2,1)}, u32[]{:S(2)}, u32[]{:S(2)}) collective-permute-start(bf16[256,2048]{1,0:T(8,128)(2,1)} %dynamic-slice_bitcast_fusion.3), channel_id=1, source_target_pairs={{0,16},{16,0},{1,17},{17,1},{2,18},{18,2},{3,19},{19,3},{4,20},{20... | collective-permute-start | bytes 3145736 | tf_op jit(solution)/shard_map/ppermute | solution.py:640
  17.4 24.6 %collective-permute-start.1 = (bf16[3,2048,256]{2,1,0:T(8,128)(2,1)}, bf16[3,2048,256]{2,1,0:T(8,128)(2,1)}, u32[]{:S(2)}, u32[]{:S(2)}) collective-permute-start(bf16[3,2048,256]{2,1,0:T(8,128)(2,1)} %dynamic-slice_bitcast_fusion.2), channel_id=1, source_target_pairs={{0,16},{16,0},{1,17},{17,1},{2,18},{18,2},{3,19},{19,3},{4,20},{20... | collective-permute-start | bytes 9437192 | tf_op jit(solution)/shard_map/ppermute | solution.py:640
  22.9 44.4 %collective-permute-start.4 = (bf16[1024,2048]{1,0:T(8,128)(2,1)}, bf16[1024,2048]{1,0:T(8,128)(2,1)}, u32[]{:S(2)}, u32[]{:S(2)}) collective-permute-start(bf16[1024,2048]{1,0:T(8,128)(2,1)} %dynamic-slice_bitcast_fusion), channel_id=1, source_target_pairs={{0,16},{16,0},{1,17},{17,1},{2,18},{18,2},{3,19},{19,3},{4,20},{20... | collective-permute-start | bytes 12582920 | tf_op jit(solution)/shard_map/ppermute | solution.py:640
  28.6 305.6 %all-gather.5.cloned.1.call-start = ((), (), s32[]{:S(2)}) async-start(), calls=%async_computation.1 | async-start | bytes 8912896 | tf_op jit(solution)/shard_map/all_gather | solution.py:679
  33.3 25.6 %collective-permute-start.3 = (bf16[2048,1024]{1,0:T(8,128)(2,1)}, bf16[2048,1024]{1,0:T(8,128)(2,1)}, u32[]{:S(2)}, u32[]{:S(2)}) collective-permute-start(bf16[2048,1024]{1,0:T(8,128)(2,1)} %dynamic-slice_bitcast_fusion.1), channel_id=1, source_target_pairs={{0,16},{16,0},{1,17},{17,1},{2,18},{18,2},{3,19},{19,3},{4,20},{20... | collective-permute-start | bytes 12582920 | tf_op jit(solution)/shard_map/ppermute | solution.py:640
  42.1 6.1 %copy-start.22 = (bf16[4,128,2048]{2,1,0:T(8,128)(2,1)S(1)}, bf16[4,128,2048]{2,1,0:T(8,128)(2,1)}, u32[]{:S(2)}) copy-start(bf16[4,128,2048]{2,1,0:T(8,128)(2,1)} %get-tuple-element.198) | copy-start | bytes 6291460
  58.9 49.6 %slice-start.2 = ((s8[8388608]{0:T(1024)(128)(4,1)}), s8[4194304]{0:T(1024)(128)(4,1)S(1)}, s32[]{:S(2)}) async-start(s8[8388608]{0:T(1024)(128)(4,1)} %bitcast.228), calls=%async_computation.4 | async-start | bytes 8388608
  67.3 6.0 %copy-start.14 = (bf16[1,512,2048]{2,1,0:T(8,128)(2,1)S(1)}, bf16[1,512,2048]{2,1,0:T(8,128)(2,1)}, u32[]{:S(2)}) copy-start(bf16[1,512,2048]{2,1,0:T(8,128)(2,1)} %param.23) | copy-start | bytes 6291460
  67.3 6.0 %copy-start.26 = (bf16[512,256]{1,0:T(8,128)(2,1)S(1)}, bf16[512,256]{1,0:T(8,128)(2,1)}, u32[]{:S(2)}) copy-start(bf16[512,256]{1,0:T(8,128)(2,1)} %get-tuple-element.159) | copy-start | bytes 786436
  67.3 41.2 %slice-start.3 = ((s8[8388608]{0:T(1024)(128)(4,1)}), s8[4194304]{0:T(1024)(128)(4,1)S(1)}, s32[]{:S(2)}) async-start(s8[8388608]{0:T(1024)(128)(4,1)} %bitcast.228), calls=%async_computation.5 | async-start | bytes 8388608
  75.3 37.1 %slice-start.4 = ((s8[8388608]{0:T(1024)(128)(4,1)}), s8[4194304]{0:T(1024)(128)(4,1)S(1)}, s32[]{:S(2)}) async-start(s8[8388608]{0:T(1024)(128)(4,1)} %bitcast.231), calls=%async_computation.6 | async-start | bytes 8388608
  108.5 22.8 %copy-start.6 = (bf16[4,4,32,2048]{3,2,1,0:T(8,128)(2,1)}, bf16[4,4,32,2048]{3,2,1,0:T(8,128)(2,1)S(1)}, u32[]{:S(2)}) copy-start(bf16[4,4,32,2048]{3,2,1,0:T(8,128)(2,1)S(1)} %get-tuple-element.161) | copy-start | bytes 6291460
  112.4 15.8 %copy-start.12 = (bf16[3,2048,256]{2,1,0:T(8,128)(2,1)S(1)}, bf16[3,2048,256]{2,1,0:T(8,128)(2,1)}, u32[]{:S(2)}) copy-start(bf16[3,2048,256]{2,1,0:T(8,128)(2,1)} %get-tuple-element.199) | copy-start | bytes 9437188
  202.0 5.4 %slice-start.6 = ((s8[8388608]{0:T(1024)(128)(4,1)}), s8[4194304]{0:T(1024)(128)(4,1)S(1)}, s32[]{:S(2)}) async-start(s8[8388608]{0:T(1024)(128)(4,1)} %bitcast.233), calls=%async_computation.8 | async-start | bytes 8388608
  202.4 5.0 %slice-start.7 = ((s8[8388608]{0:T(1024)(128)(4,1)}), s8[4194304]{0:T(1024)(128)(4,1)S(1)}, s32[]{:S(2)}) async-start(s8[8388608]{0:T(1024)(128)(4,1)} %bitcast.233), calls=%async_computation.9 | async-start | bytes 8388608
  210.0 9.3 %slice-start = ((s8[8388608]{0:T(1024)(128)(4,1)}), s8[4194304]{0:T(1024)(128)(4,1)S(1)}, s32[]{:S(2)}) async-start(s8[8388608]{0:T(1024)(128)(4,1)} %bitcast.220), calls=%async_computation.2 | async-start | bytes 8388608
  212.3 7.1 %slice-start.1 = ((s8[8388608]{0:T(1024)(128)(4,1)}), s8[4194304]{0:T(1024)(128)(4,1)S(1)}, s32[]{:S(2)}) async-start(s8[8388608]{0:T(1024)(128)(4,1)} %bitcast.220), calls=%async_computation.3 | async-start | bytes 8388608
  212.3 7.1 %copy-start.30 = (f32[1,2048]{1,0:T(1,128)S(1)}, f32[1,2048]{1,0:T(1,128)}, u32[]{:S(2)}) copy-start(f32[1,2048]{1,0:T(1,128)} %param.26) | copy-start | bytes 24580
  254.0 5.9 %copy-start.23 = (bf16[512,256]{1,0:T(8,128)(2,1)S(1)}, bf16[512,256]{1,0:T(8,128)(2,1)}, u32[]{:S(2)}) copy-start(bf16[512,256]{1,0:T(8,128)(2,1)} %get-tuple-element.176) | copy-start | bytes 786436
  310.4 23.8 %copy-start.16 = (bf16[1,512,2048]{2,1,0:T(8,128)(2,1)S(1)}, bf16[1,512,2048]{2,1,0:T(8,128)(2,1)}, u32[]{:S(2)}) copy-start(bf16[1,512,2048]{2,1,0:T(8,128)(2,1)} %param.23) | copy-start | bytes 6291460
  310.4 23.8 %copy-start.31 = (f32[1,2,512]{2,1,0:T(2,128)S(1)}, f32[1,2,512]{2,1,0:T(2,128)}, u32[]{:S(2)}) copy-start(f32[1,2,512]{2,1,0:T(2,128)} %param.22) | copy-start | bytes 12292
  443.7 8.1 %copy-start.39 = (bf16[2048,2048]{1,0:T(8,128)(2,1)S(1)}, bf16[2048,2048]{1,0:T(8,128)(2,1)}, u32[]{:S(2)}) copy-start(bf16[2048,2048]{1,0:T(8,128)(2,1)} %get-tuple-element.84) | copy-start | bytes 25165828 | tf_op jit(solution)/shard_map/cond
  (32 other events, 84.4 us)
Sparse Core Ops, SparseCore 0:
  28.7 147.6 all-gather.2
  191.5 136.2 all-gather.4
